TPU v7x, 32 devices: a whole 2x2x4 slice. The times are simulated.
32 devices in a mesh: row: 8 (over z, y), col: 4 (over x, core).
Axes of the slice: x: 2, y: 2, z: 4, core: 2. Of those that a mesh axis runs over, the one named last changes fastest.
Arguments:
- embeddings: bfloat16 [12288, 768], P(('row', 'col'))
- doc_order: int32 [12288], P(('row', 'col')), may hold values from 0 to 12287, each once
Outputs:
- nearest_earlier: float32 [12288], P(('row', 'col'))
Inputs may be any that keep to these rules, and one draw needn't show every extreme that they name: `doc_order`: each value 0 to 12287 appears once.
All inputs are finite; a program needn't handle non-finite values.
Results may differ from a plain program's by a relative error of at most 0.00051.
Values may be sent and summed in bfloat16 or wider, within the bound.
No kernel may reach another device: no remote copies, remote signals or barrier semaphores. Data moves between devices by JAX's collectives and lax.ppermute only.
A program may use at most 64 MiB of HBM per device.

v0:
```python
import functools

import jax
import jax.numpy as jnp
from jax import lax
from jax.experimental import pallas as pl
from jax.experimental.pallas import tpu as pltpu
from jax.sharding import PartitionSpec as P

AXES = ("row", "col")
CORES = 2
PAD = 16
FAR = 1.0e9
VMEM_GRANT = 16 << 20


class Layout:
    def __init__(self, mesh):
        rows, cols = mesh.shape["row"], mesh.shape["col"]
        self.xs = cols // CORES
        self.ys = self.xs if rows % self.xs == 0 else 1
        self.lines = rows // self.ys

    def index(self, line, y, x, core):
        return ((line * self.ys + y) * self.xs + x) * CORES + core

    def pairs(self, target):
        found = []
        for line in range(self.lines):
            for y in range(self.ys):
                for x in range(self.xs):
                    for core in range(CORES):
                        to = target(line, y, x, core)
                        if to is not None:
                            found.append((self.index(line, y, x, core), self.index(*to)))
        return found

    def plane_move(self, dy, dx):
        return self.pairs(lambda l, y, x, c: (l, (y + dy) % self.ys, (x + dx) % self.xs, c))

    def swap(self):
        return self.pairs(lambda l, y, x, c: (l, y, x, CORES - 1 - c))

    def plane_offsets(self):
        return [(dy, dx) for dy in range(self.ys) for dx in range(self.xs) if dy or dx]

    def line_maps(self):
        maps = []
        for step in range(1, (self.lines + 1) // 2):
            maps.append({i: (i + step) % self.lines for i in range(self.lines)})
        if self.lines % 2 == 0:
            half = self.lines // 2
            maps.append({(i if i % 2 == 0 else i + half): (i + half if i % 2 == 0 else i) for i in range(half)})
        return maps

    def line_move(self, line_map):
        return self.pairs(lambda l, y, x, c: (line_map[l], y, x, c) if l in line_map else None)

    def line_return(self, line_map):
        back = {b: a for a, b in line_map.items()}
        free = [i for i in range(self.lines) if i not in line_map]
        back.update(zip([i for i in range(self.lines) if i not in back], free))
        return self.line_move(back)


def backward(pairs):
    return [(b, a) for a, b in pairs]


def pack_body(pieces, emb_ref, order_ref, out_ref, *piece_refs):
    n, width = emb_ref.shape
    floats = emb_ref[...].astype(jnp.float32)
    scale = lax.rsqrt(jnp.sum(floats * floats, axis=1, keepdims=True) + 1e-06)
    out_ref[:n, :] = (floats * scale).astype(jnp.bfloat16)
    code = order_ref[...].reshape(1, n) + 1
    high = (code >> 8).astype(jnp.float32)
    low = (code & 255).astype(jnp.float32)
    line = lax.broadcasted_iota(jnp.int32, (PAD, n), 0)
    tail = jnp.where(line == 0, high, jnp.where(line == 1, low, 0.0))
    out_ref[n:, :] = jnp.zeros((PAD, width), jnp.bfloat16)
    out_ref[n:, :n] = tail.astype(jnp.bfloat16)
    for (start, rows), ref in zip(pieces, piece_refs):
        cut(out_ref, start, rows, ref)


def pack(embeddings, doc_order, pieces=()):
    n, width = embeddings.shape
    shapes = [pltpu.VMEM((rows + PAD, width), jnp.bfloat16) for rows in (n, *(rows for _, rows in pieces))]
    call = pl.pallas_call(
        functools.partial(pack_body, pieces),
        out_shape=shapes,
        compiler_params=pltpu.CompilerParams(vmem_limit_bytes=VMEM_GRANT),
        name="pack",
    )
    return call(*in_vmem([embeddings, doc_order]))


def cut(ref, start, rows, out_ref):
    n = ref.shape[0] - PAD
    out_ref[:rows, :] = ref[start : start + rows, :]
    out_ref[rows:, :] = jnp.zeros((PAD, ref.shape[1]), jnp.bfloat16)
    out_ref[rows:, :rows] = ref[n:, start : start + rows]


def piece_body(start, rows, ref, out_ref):
    cut(ref, start, rows, out_ref)


def piece(block, start, rows):
    return pl.pallas_call(
        functools.partial(piece_body, start, rows),
        out_shape=pltpu.VMEM((rows + PAD, block.shape[1]), jnp.bfloat16),
        compiler_params=pltpu.CompilerParams(vmem_limit_bytes=VMEM_GRANT),
        name="piece",
    )(*in_vmem([block]))


def lane_orders(ref):
    n = ref.shape[0] - PAD
    tail = ref[n:, :n].astype(jnp.float32)
    order = tail[0:1] * 256.0 + tail[1:2]
    return jnp.where(order == 0.0, FAR, order)


def match_body(n_rows, n_plain, has_rows, chips, known, *refs):
    at = 0

    def take(count):
        nonlocal at
        at += count
        return refs[at - count : at]

    side_cols = sum(chips)
    rows, cols = take(n_rows), take(2 * side_cols)
    row_in, col_in = take(sum(has_rows)), take(2 * len(known))
    row_out, col_out = take(n_rows), take(2 if n_plain < n_rows else 0)
    (col_acc,) = take(1)
    lanes = 128
    col_orders = [lane_orders(ref) for ref in cols]
    row_in = list(row_in)
    for r in range(n_rows):
        n = rows[r].shape[0] - PAD
        own_orders = lane_orders(rows[r])
        own_order = jnp.broadcast_to(own_orders, (lanes, n)).T[:, 0:1]
        best = jnp.full((n, lanes), -1.0, jnp.float32)
        for c in range(2 * side_cols):
            m = cols[c].shape[0] - PAD
            score = lax.dot_general(
                rows[r][:n, :], cols[c][:m, :], (((1,), (1,)), ((), ())), preferred_element_type=jnp.float32
            )
            earlier = col_orders[c] < own_order
            masked = jnp.where(earlier, score, -1.0)
            for k in range(m // lanes):
                best = jnp.maximum(best, masked[:, k * lanes : (k + 1) * lanes])
            if r >= n_plain:
                other = jnp.max(jnp.where(earlier, -1.0, score).reshape(n // 8, 8, m), axis=0)
                col_acc[c, :, :m] = other if r == n_plain else jnp.maximum(col_acc[c, :, :m], other)
        value = jnp.where(own_orders == FAR, -1.0, jnp.max(best.T, axis=0, keepdims=True))
        if has_rows[r]:
            value = jnp.maximum(value, row_in.pop(0)[...])
        row_out[r][...] = value
    for side in range(len(col_out)):
        before = [col_in[side * len(known) + i][k : k + 1, :] for i in range(len(known)) for k in range(known[i])]
        c = side * side_cols
        for chip in range(len(chips)):
            start = 0
            for _ in range(chips[chip]):
                m = cols[c].shape[0] - PAD
                value = jnp.max(col_acc[c, :, :m], axis=0, keepdims=True)
                if before:
                    value = jnp.maximum(value, before[chip][:, start : start + m])
                col_out[side][chip : chip + 1, start : start + m] = value
                start += m
                c += 1


def in_vmem(values):
    return [pltpu.with_memory_space_constraint(v, pltpu.VMEM) for v in values]


def match(rows, chips, n_plain, row_in=None, col_in=()):
    ours = [block for mine, _ in chips for block in mine]
    twins = [block for _, other in chips for block in other]
    row_in = row_in or [None] * len(rows)
    width = rows[0].shape[1]
    n = sum(block.shape[0] - PAD for block in chips[0][0])
    sizes = [block.shape[0] - PAD for block in rows]
    block = pltpu.VMEM((len(chips), n), jnp.float32)
    before = [pair[0] for pair in col_in] + [pair[1] for pair in col_in]
    call = pl.pallas_call(
        functools.partial(
            match_body,
            len(rows),
            n_plain,
            [value is not None for value in row_in],
            [len(mine) for mine, _ in chips],
            [pair[0].shape[0] for pair in col_in],
        ),
        out_shape=[pltpu.VMEM((1, size), jnp.float32) for size in sizes] + [block, block] * (n_plain < len(rows)),
        scratch_shapes=[pltpu.VMEM((2 * len(ours), 8, n), jnp.float32)],
        cost_estimate=pl.CostEstimate(
            flops=4 * sum(sizes) * len(chips) * n * width,
            bytes_accessed=2 * (sum(sizes) + 2 * len(chips) * n) * width,
            transcendentals=0,
        ),
        compiler_params=pltpu.CompilerParams(vmem_limit_bytes=VMEM_GRANT),
    )
    outs = call(*in_vmem([*rows, *ours, *twins, *(value for value in row_in if value is not None), *before]))
    return outs[: len(rows)], tuple(outs[len(rows) :])


def merge_body(ours_ref, theirs_ref, *out_refs):
    value = jnp.maximum(ours_ref[...], theirs_ref[...])
    for k, ref in enumerate(out_refs):
        ref[...] = value[k : k + 1]


def merge(ours, theirs):
    count, n = ours.shape
    return pl.pallas_call(
        merge_body,
        out_shape=[pltpu.VMEM((1, n), jnp.float32)] * count,
        compiler_params=pltpu.CompilerParams(vmem_limit_bytes=VMEM_GRANT),
        name="merge",
    )(*in_vmem([ours, theirs]))


def solution(mesh):
    layout = Layout(mesh)
    maps = layout.line_maps()
    offsets = layout.plane_offsets()

    def send(value, pairs):
        return lax.ppermute(value, AXES, pairs)

    def nearest(embeddings, doc_order):
        n = embeddings.shape[0]
        last = min(n, 128)
        pieces = ((0, n - last), (n - last, last)) if n > last else ((0, n),)
        swap = layout.swap()
        early, late = maps[:-1], maps[-1]

        raw = [send(embeddings, layout.line_move(m)) for m in early]
        own, *parts = pack(embeddings, doc_order, pieces)
        plane = [send(own, layout.plane_move(*d)) for d in offsets[:-1]]
        half = [send(part, layout.line_move(late)) for part in parts]
        raw_order = [send(doc_order, layout.line_move(m)) for m in early]
        line = [pack(block, order)[0] for block, order in zip(raw, raw_order)]
        near_blocks = [own, *plane]
        near_chips = [([block], [send(block, swap)]) for block in near_blocks]

        dy, dx = offsets[-1]
        routes = [((0, dx), (dy, 0)), ((dy, 0), (0, dx))]
        corner = []
        for k, (start, rows) in enumerate(pieces):
            have, move = routes[k % 2]
            block = piece(plane[offsets.index(have)], start, rows)
            corner.append(send(block, layout.plane_move(*move)))
        far_chips = [(corner, [send(block, swap) for block in corner])]

        first = [own, *line]
        near_rows, near = match(first, near_chips, 1)
        half_rows, near = match(half[:-1], near_chips, 0, None, [near])
        rows, far = match(first + half[:-1], far_chips, 1, [*near_rows, *half_rows])
        last_rows, (ours, theirs) = match(half[-1:], near_chips + far_chips, 0, None, [near, far])

        mine, *answers = rows[: len(first)]
        answers.append(jnp.concatenate([*rows[len(first) :], *last_rows], axis=1))
        back = [mine]
        for value, m in zip(answers, maps):
            back.append(send(value, layout.line_return(m)))
        own_best, *others = merge(ours, send(theirs, swap))
        back.append(own_best)
        for value, d in zip(others, offsets):
            back.append(send(value, backward(layout.plane_move(*d))))
        best = functools.reduce(jnp.maximum, back)
        return jnp.maximum(best, -1.0).reshape(doc_order.shape)

    return jax.shard_map(
        nearest,
        mesh=mesh,
        in_specs=(P(AXES, None), P(AXES)),
        out_specs=P(AXES),
        check_vma=False,
    )
```

profile of v0, /device:TPU:0, one launch (start us, length us, event | category | flops | bytes accessed | tf_op | source)
XLA Modules:
  0.0 58.6 jit_solution(3811868790516331572)
XLA Ops:
  0.0 1.1 %copy-done = bf16[384,768]{1,0:T(8,128)(2,1)S(1)} copy-done((bf16[384,768]{1,0:T(8,128)(2,1)S(1)}, bf16[384,768]{1,0:T(8,128)(2,1)}, u32[]{:S(2)}) %copy-start) | copy-done | bytes 589848
  1.1 0.7 %copy-done.1 = s32[384]{0:T(512)S(1)} copy-done((s32[384]{0:T(512)S(1)}, s32[384]{0:T(512)}, u32[]{:S(2)}) %copy-start.1) | copy-done | bytes 1560
  1.7 0.2 pack.2
  2.0 3.0 %collective-permute-start.3 = (bf16[400,768]{1,0:T(8,128)(2,1)S(1)}, bf16[400,768]{1,0:T(8,128)(2,1)S(1)}, u32[]{:S(2)}, u32[]{:S(2)}) collective-permute-start(bf16[400,768]{1,0:T(8,128)(2,1)S(1)} %get-tuple-element.27.refs_0_.refs_2_.refs_1_), channel_id=1, source_target_pairs={{0,2},{1,3},{2,0},{3,1},{4,6},{5,7},{6,4},{7,5},{8,10},{9,11},{10,... | collective-permute-start | bytes 1843208 | tf_op jit(solution)/shard_map/ppermute | solution.py:234
  5.0 1.5 %collective-permute-start.5 = (bf16[400,768]{1,0:T(8,128)(2,1)S(1)}, bf16[400,768]{1,0:T(8,128)(2,1)S(1)}, u32[]{:S(2)}, u32[]{:S(2)}) collective-permute-start(bf16[400,768]{1,0:T(8,128)(2,1)S(1)} %get-tuple-element.27.refs_0_.refs_2_.refs_1_), channel_id=1, source_target_pairs={{0,4},{1,5},{2,6},{3,7},{4,0},{5,1},{6,2},{7,3},{8,12},{9,13},{10,... | collective-permute-start | bytes 1843208 | tf_op jit(solution)/shard_map/ppermute | solution.py:234
  6.5 1.6 %collective-permute-start = (bf16[384,768]{1,0:T(8,128)(2,1)S(1)}, bf16[384,768]{1,0:T(8,128)(2,1)S(1)}, u32[]{:S(2)}, u32[]{:S(2)}) collective-permute-start(bf16[384,768]{1,0:T(8,128)(2,1)S(1)} %copy-done), channel_id=1, source_target_pairs={{0,8},{1,9},{2,10},{3,11},{4,12},{5,13},{6,14},{7,15},{8,16},{9,17... | collective-permute-start | bytes 1769480 | tf_op jit(solution)/shard_map/ppermute | solution.py:234
  8.1 0.0 collective-permute-start.9
  8.1 10.8 %collective-permute-done.3.ref.refs_3_.refs_2_ = bf16[400,768]{1,0:T(8,128)(2,1)S(1)} collective-permute-done((bf16[400,768]{1,0:T(8,128)(2,1)S(1)}, bf16[400,768]{1,0:T(8,128)(2,1)S(1)}, u32[]{:S(2)}, u32[]{:S(2)}) %collective-permute-start.3) | collective-permute-done | bytes 614432 | tf_op jit(solution)/shard_map/ppermute | solution.py:234
  18.8 1.5 %collective-permute-done.5.ref.refs_4_.refs_3_ = bf16[400,768]{1,0:T(8,128)(2,1)S(1)} collective-permute-done((bf16[400,768]{1,0:T(8,128)(2,1)S(1)}, bf16[400,768]{1,0:T(8,128)(2,1)S(1)}, u32[]{:S(2)}, u32[]{:S(2)}) %collective-permute-start.5) | collective-permute-done | bytes 614432 | tf_op jit(solution)/shard_map/ppermute | solution.py:234
  20.3 0.0 collective-permute-start.11
  20.3 1.6 %collective-permute-start.1 = (s32[384]{0:T(512)S(1)}, s32[384]{0:T(512)S(1)}, u32[]{:S(2)}, u32[]{:S(2)}) collective-permute-start(s32[384]{0:T(512)S(1)} %copy-done.1), channel_id=1, source_target_pairs={{0,8},{1,9},{2,10},{3,11},{4,12},{5,13},{6,14},{7,15},{8,16},{9,17... | collective-permute-start | bytes 4616 | tf_op jit(solution)/shard_map/ppermute | solution.py:234
  21.9 3.8 %collective-permute-done.1.order_ref = s32[384]{0:T(512)S(1)} collective-permute-done((s32[384]{0:T(512)S(1)}, s32[384]{0:T(512)S(1)}, u32[]{:S(2)}, u32[]{:S(2)}) %collective-permute-start.1) | collective-permute-done | bytes 1568 | tf_op jit(solution)/shard_map/ppermute | solution.py:234
  25.7 1.5 %collective-permute-start.4 = (bf16[272,768]{1,0:T(8,128)(2,1)S(1)}, bf16[272,768]{1,0:T(8,128)(2,1)S(1)}, u32[]{:S(2)}, u32[]{:S(2)}) collective-permute-start(bf16[272,768]{1,0:T(8,128)(2,1)S(1)} %piece.2), channel_id=1, source_target_pairs={{0,4},{1,5},{2,6},{3,7},{4,0},{5,1},{6,2},{7,3},{8,12},{9,13},{10,... | collective-permute-start | bytes 1253384 | tf_op jit(solution)/shard_map/ppermute | solution.py:234
  27.2 0.9 %collective-permute-start.6 = (bf16[144,768]{1,0:T(8,128)(2,1)S(1)}, bf16[144,768]{1,0:T(8,128)(2,1)S(1)}, u32[]{:S(2)}, u32[]{:S(2)}) collective-permute-start(bf16[144,768]{1,0:T(8,128)(2,1)S(1)} %piece.3), channel_id=1, source_target_pairs={{0,2},{1,3},{2,0},{3,1},{4,6},{5,7},{6,4},{7,5},{8,10},{9,11},{10,... | collective-permute-start | bytes 663560 | tf_op jit(solution)/shard_map/ppermute | solution.py:234
  28.1 2.7 %collective-permute-start.2 = (bf16[272,768]{1,0:T(8,128)(2,1)S(1)}, bf16[272,768]{1,0:T(8,128)(2,1)S(1)}, u32[]{:S(2)}, u32[]{:S(2)}) collective-permute-start(bf16[272,768]{1,0:T(8,128)(2,1)S(1)} %get-tuple-element.28), channel_id=1, source_target_pairs={{0,16},{1,17},{2,18},{3,19},{4,20},{5,21},{6,22},{7,23},{24,8},{25... | collective-permute-start | bytes 1253384 | tf_op jit(solution)/shard_map/ppermute | solution.py:234
  30.8 5.8 %collective-permute-done.4.refs_3_.refs_4_ = bf16[272,768]{1,0:T(8,128)(2,1)S(1)} collective-permute-done((bf16[272,768]{1,0:T(8,128)(2,1)S(1)}, bf16[272,768]{1,0:T(8,128)(2,1)S(1)}, u32[]{:S(2)}, u32[]{:S(2)}) %collective-permute-start.4) | collective-permute-done | bytes 417824 | tf_op jit(solution)/shard_map/ppermute | solution.py:234
  36.7 0.2 pack.3.refs_1_
  36.9 2.6 %collective-permute-start.13 = (bf16[144,768]{1,0:T(8,128)(2,1)S(1)}, bf16[144,768]{1,0:T(8,128)(2,1)S(1)}, u32[]{:S(2)}, u32[]{:S(2)}) collective-permute-start(bf16[144,768]{1,0:T(8,128)(2,1)S(1)} %get-tuple-element.37), channel_id=1, source_target_pairs={{0,16},{1,17},{2,18},{3,19},{4,20},{5,21},{6,22},{7,23},{24,8},{25... | collective-permute-start | bytes 663560 | tf_op jit(solution)/shard_map/ppermute | solution.py:234
  39.5 0.3 collective-permute-start.8
  39.8 4.0 %shard_map.28 = (f32[1,384]{1,0:T(1,128)S(1)}, f32[1,384]{1,0:T(1,128)S(1)}, f32[3,384]{1,0:T(4,128)S(1)}, f32[3,384]{1,0:T(4,128)S(1)}) custom-call(bf16[400,768]{1,0:T(8,128)(2,1)S(1)} %get-tuple-element.27.refs_0_.refs_2_.refs_1_, bf16[400,768]{1,0:T(8,128)(2,1)S(1)} %pack.3.refs_1_, bf16[400,768]{1,0:T(8,128)(2,1)S(1)} %get-tuple-element.27.refs_0_.refs_2_.refs_1_, ...), custom_call_target="tpu_custom_call" | custom-call | flops 2717908992 | bytes 4718592 | tf_op jit(solution)/shard_map/pallas_call | solution.py:208
  43.9 1.5 %shard_map.29 = (f32[1,256]{1,0:T(1,128)S(1)}, f32[3,384]{1,0:T(4,128)S(1)}, f32[3,384]{1,0:T(4,128)S(1)}) custom-call(bf16[272,768]{1,0:T(8,128)(2,1)S(1)} %collective-permute-done.2.refs_0_.refs_2_, bf16[400,768]{1,0:T(8,128)(2,1)S(1)} %get-tuple-element.27.refs_0_.refs_2_.refs_1_, bf16[400,768]{1,0:T(8,128)(2,1)S(1)} %collective-permute-done.3.ref.refs_3_.refs_2_, ...), custom_call_target="tpu_custom_call" | custom-call | flops 905969664 | bytes 3932160 | tf_op jit(solution)/shard_map/pallas_call | solution.py:208
  45.4 1.9 %shard_map.30 = (f32[1,384]{1,0:T(1,128)S(1)}, f32[1,384]{1,0:T(1,128)S(1)}, f32[1,256]{1,0:T(1,128)S(1)}, f32[1,384]{1,0:T(1,128)S(1)}, f32[1,384]{1,0:T(1,128)S(1)}) custom-call(bf16[400,768]{1,0:T(8,128)(2,1)S(1)} %get-tuple-element.27.refs_0_.refs_2_.refs_1_, bf16[400,768]{1,0:T(8,128)(2,1)S(1)} %pack.3.refs_1_, ...), custom_call_target="tpu_custom_call" | custom-call | flops 1207959552 | bytes 2752512 | tf_op jit(solution)/shard_map/pallas_call | solution.py:208
  47.4 1.5 %shard_map.31 = (f32[1,128]{1,0:T(1,128)S(1)}, f32[4,384]{1,0:T(4,128)S(1)}, f32[4,384]{1,0:T(4,128)S(1)}) custom-call(bf16[144,768]{1,0:T(8,128)(2,1)S(1)} %collective-permute-done.13.refs_0_, bf16[400,768]{1,0:T(8,128)(2,1)S(1)} %get-tuple-element.27.refs_0_.refs_2_.refs_1_, bf16[400,768]{1,0:T(8,128)(2,1)S(1)} %collective-permute-done.3.ref.refs_3_.refs_2_, ...), custom_call_target="tpu_custom_call" | custom-call | flops 603979776 | bytes 4915200 | tf_op jit(solution)/shard_map/pallas_call | solution.py:208
  48.9 0.4 collective-permute-start.15
  49.3 2.1 %collective-permute-start.12 = (f32[1,384]{1,0:T(1,128)S(1)}, f32[1,384]{1,0:T(1,128)S(1)}, u32[]{:S(2)}, u32[]{:S(2)}) collective-permute-start(f32[1,384]{1,0:T(1,128)S(1)} %get-tuple-element.35), channel_id=1, source_target_pairs={{0,24},{1,25},{2,26},{3,27},{4,28},{5,29},{6,30},{7,31},{8,0},{9,1... | collective-permute-start | bytes 4616 | tf_op jit(solution)/shard_map/ppermute | solution.py:234
  51.4 0.6 %collective-permute-start.16 = (f32[1,384]{1,0:T(1,128)S(1)}, f32[1,384]{1,0:T(1,128)S(1)}, u32[]{:S(2)}, u32[]{:S(2)}) collective-permute-start(f32[1,384]{1,0:T(1,128)S(1)} %get-tuple-element.46), channel_id=1, source_target_pairs={{2,0},{3,1},{0,2},{1,3},{6,4},{7,5},{4,6},{5,7},{10,8},{11,9},{8,1... | collective-permute-start | bytes 4616 | tf_op jit(solution)/shard_map/ppermute | solution.py:234
  52.0 1.5 %collective-permute-start.17 = (f32[1,384]{1,0:T(1,128)S(1)}, f32[1,384]{1,0:T(1,128)S(1)}, u32[]{:S(2)}, u32[]{:S(2)}) collective-permute-start(f32[1,384]{1,0:T(1,128)S(1)} %get-tuple-element.47), channel_id=1, source_target_pairs={{4,0},{5,1},{6,2},{7,3},{0,4},{1,5},{2,6},{3,7},{12,8},{13,9},{14,... | collective-permute-start | bytes 4616 | tf_op jit(solution)/shard_map/ppermute | solution.py:234
  53.5 1.4 %collective-permute-start.18 = (f32[1,384]{1,0:T(1,128)S(1)}, f32[1,384]{1,0:T(1,128)S(1)}, u32[]{:S(2)}, u32[]{:S(2)}) collective-permute-start(f32[1,384]{1,0:T(1,128)S(1)} %get-tuple-element.48), channel_id=1, source_target_pairs={{6,0},{7,1},{4,2},{5,3},{2,4},{3,5},{0,6},{1,7},{14,8},{15,9},{12,... | collective-permute-start | bytes 4616 | tf_op jit(solution)/shard_map/ppermute | solution.py:234
  54.9 0.1 collective-permute-done.16
  55.0 0.5 collective-permute-done.17
  55.5 2.4 %collective-permute-done.18 = f32[1,384]{1,0:T(1,128)S(1)} collective-permute-done((f32[1,384]{1,0:T(1,128)S(1)}, f32[1,384]{1,0:T(1,128)S(1)}, u32[]{:S(2)}, u32[]{:S(2)}) %collective-permute-start.18) | collective-permute-done | bytes 1568 | tf_op jit(solution)/shard_map/ppermute | solution.py:234
  58.0 0.6 %maximum_reduce_fusion = f32[384]{0:T(512)} fusion(f32[1,384]{1,0:T(1,128)S(1)} %collective-permute-done.18, f32[1,384]{1,0:T(1,128)S(1)} %collective-permute-done.17, f32[1,384]{1,0:T(1,128)S(1)} %collective-permute-done.16, f32[1,384]{1,0:T(1,128)S(1)} %get-tuple-element.45, f32[1,384]{1,0:T(1,128)S(1)} %collective-permute-done.14, ...), kind=kLoop, calls=%fused_computation.1 | loop fusion | flops 2688 | bytes 12288 | tf_op jit(solution)/shard_map/max | solution.py:277
  (21 shorter events, 0.1 us)
Async XLA Ops:
  0.0 1.1 %copy-start = (bf16[384,768]{1,0:T(8,128)(2,1)S(1)}, bf16[384,768]{1,0:T(8,128)(2,1)}, u32[]{:S(2)}) copy-start(bf16[384,768]{1,0:T(8,128)(2,1)} %emb_ref.1) | copy-start | bytes 1769476
  1.1 0.7 %copy-start.1 = (s32[384]{0:T(512)S(1)}, s32[384]{0:T(512)}, u32[]{:S(2)}) copy-start(s32[384]{0:T(512)} %order_ref.1) | copy-start | bytes 4612
  2.0 16.9 %collective-permute-start.3 = (bf16[400,768]{1,0:T(8,128)(2,1)S(1)}, bf16[400,768]{1,0:T(8,128)(2,1)S(1)}, u32[]{:S(2)}, u32[]{:S(2)}) collective-permute-start(bf16[400,768]{1,0:T(8,128)(2,1)S(1)} %get-tuple-element.27.refs_0_.refs_2_.refs_1_), channel_id=1, source_target_pairs={{0,2},{1,3},{2,0},{3,1},{4,6},{5,7},{6,4},{7,5},{8,10},{9,11},{10,... | collective-permute-start | bytes 1843208 | tf_op jit(solution)/shard_map/ppermute | solution.py:234
  5.0 15.3 %collective-permute-start.5 = (bf16[400,768]{1,0:T(8,128)(2,1)S(1)}, bf16[400,768]{1,0:T(8,128)(2,1)S(1)}, u32[]{:S(2)}, u32[]{:S(2)}) collective-permute-start(bf16[400,768]{1,0:T(8,128)(2,1)S(1)} %get-tuple-element.27.refs_0_.refs_2_.refs_1_), channel_id=1, source_target_pairs={{0,4},{1,5},{2,6},{3,7},{4,0},{5,1},{6,2},{7,3},{8,12},{9,13},{10,... | collective-permute-start | bytes 1843208 | tf_op jit(solution)/shard_map/ppermute | solution.py:234
  6.5 20.7 %collective-permute-start = (bf16[384,768]{1,0:T(8,128)(2,1)S(1)}, bf16[384,768]{1,0:T(8,128)(2,1)S(1)}, u32[]{:S(2)}, u32[]{:S(2)}) collective-permute-start(bf16[384,768]{1,0:T(8,128)(2,1)S(1)} %copy-done), channel_id=1, source_target_pairs={{0,8},{1,9},{2,10},{3,11},{4,12},{5,13},{6,14},{7,15},{8,16},{9,17... | collective-permute-start | bytes 1769480 | tf_op jit(solution)/shard_map/ppermute | solution.py:234
  8.1 20.0 %collective-permute-start.9 = (bf16[400,768]{1,0:T(8,128)(2,1)S(1)}, bf16[400,768]{1,0:T(8,128)(2,1)S(1)}, u32[]{:S(2)}, u32[]{:S(2)}) collective-permute-start(bf16[400,768]{1,0:T(8,128)(2,1)S(1)} %get-tuple-element.27.refs_0_.refs_2_.refs_1_), channel_id=1, source_target_pairs={{0,1},{1,0},{2,3},{3,2},{4,5},{5,4},{6,7},{7,6},{8,9},{9,8},{10,11... | collective-permute-start | bytes 1843208 | tf_op jit(solution)/shard_map/ppermute | solution.py:234
  18.8 20.7 %collective-permute-start.10 = (bf16[400,768]{1,0:T(8,128)(2,1)S(1)}, bf16[400,768]{1,0:T(8,128)(2,1)S(1)}, u32[]{:S(2)}, u32[]{:S(2)}) collective-permute-start(bf16[400,768]{1,0:T(8,128)(2,1)S(1)} %collective-permute-done.3.ref.refs_3_.refs_2_), channel_id=1, source_target_pairs={{0,1},{1,0},{2,3},{3,2},{4,5},{5,4},{6,7},{7,6},{8,9},{9,8},{10,11... | collective-permute-start | bytes 1843208 | tf_op jit(solution)/shard_map/ppermute | solution.py:234
  20.3 19.5 %collective-permute-start.11 = (bf16[400,768]{1,0:T(8,128)(2,1)S(1)}, bf16[400,768]{1,0:T(8,128)(2,1)S(1)}, u32[]{:S(2)}, u32[]{:S(2)}) collective-permute-start(bf16[400,768]{1,0:T(8,128)(2,1)S(1)} %collective-permute-done.5.ref.refs_4_.refs_3_), channel_id=1, source_target_pairs={{0,1},{1,0},{2,3},{3,2},{4,5},{5,4},{6,7},{7,6},{8,9},{9,8},{10,11... | collective-permute-start | bytes 1843208 | tf_op jit(solution)/shard_map/ppermute | solution.py:234
  20.3 5.4 %collective-permute-start.1 = (s32[384]{0:T(512)S(1)}, s32[384]{0:T(512)S(1)}, u32[]{:S(2)}, u32[]{:S(2)}) collective-permute-start(s32[384]{0:T(512)S(1)} %copy-done.1), channel_id=1, source_target_pairs={{0,8},{1,9},{2,10},{3,11},{4,12},{5,13},{6,14},{7,15},{8,16},{9,17... | collective-permute-start | bytes 4616 | tf_op jit(solution)/shard_map/ppermute | solution.py:234
  25.7 11.0 %collective-permute-start.4 = (bf16[272,768]{1,0:T(8,128)(2,1)S(1)}, bf16[272,768]{1,0:T(8,128)(2,1)S(1)}, u32[]{:S(2)}, u32[]{:S(2)}) collective-permute-start(bf16[272,768]{1,0:T(8,128)(2,1)S(1)} %piece.2), channel_id=1, source_target_pairs={{0,4},{1,5},{2,6},{3,7},{4,0},{5,1},{6,2},{7,3},{8,12},{9,13},{10,... | collective-permute-start | bytes 1253384 | tf_op jit(solution)/shard_map/ppermute | solution.py:234
  27.2 9.6 %collective-permute-start.6 = (bf16[144,768]{1,0:T(8,128)(2,1)S(1)}, bf16[144,768]{1,0:T(8,128)(2,1)S(1)}, u32[]{:S(2)}, u32[]{:S(2)}) collective-permute-start(bf16[144,768]{1,0:T(8,128)(2,1)S(1)} %piece.3), channel_id=1, source_target_pairs={{0,2},{1,3},{2,0},{3,1},{4,6},{5,7},{6,4},{7,5},{8,10},{9,11},{10,... | collective-permute-start | bytes 663560 | tf_op jit(solution)/shard_map/ppermute | solution.py:234
  28.1 15.8 %collective-permute-start.2 = (bf16[272,768]{1,0:T(8,128)(2,1)S(1)}, bf16[272,768]{1,0:T(8,128)(2,1)S(1)}, u32[]{:S(2)}, u32[]{:S(2)}) collective-permute-start(bf16[272,768]{1,0:T(8,128)(2,1)S(1)} %get-tuple-element.28), channel_id=1, source_target_pairs={{0,16},{1,17},{2,18},{3,19},{4,20},{5,21},{6,22},{7,23},{24,8},{25... | collective-permute-start | bytes 1253384 | tf_op jit(solution)/shard_map/ppermute | solution.py:234
  36.7 8.8 %collective-permute-start.7 = (bf16[272,768]{1,0:T(8,128)(2,1)S(1)}, bf16[272,768]{1,0:T(8,128)(2,1)S(1)}, u32[]{:S(2)}, u32[]{:S(2)}) collective-permute-start(bf16[272,768]{1,0:T(8,128)(2,1)S(1)} %collective-permute-done.4.refs_3_.refs_4_), channel_id=1, source_target_pairs={{0,1},{1,0},{2,3},{3,2},{4,5},{5,4},{6,7},{7,6},{8,9},{9,8},{10,11... | collective-permute-start | bytes 1253384 | tf_op jit(solution)/shard_map/ppermute | solution.py:234
  36.9 10.5 %collective-permute-start.13 = (bf16[144,768]{1,0:T(8,128)(2,1)S(1)}, bf16[144,768]{1,0:T(8,128)(2,1)S(1)}, u32[]{:S(2)}, u32[]{:S(2)}) collective-permute-start(bf16[144,768]{1,0:T(8,128)(2,1)S(1)} %get-tuple-element.37), channel_id=1, source_target_pairs={{0,16},{1,17},{2,18},{3,19},{4,20},{5,21},{6,22},{7,23},{24,8},{25... | collective-permute-start | bytes 663560 | tf_op jit(solution)/shard_map/ppermute | solution.py:234
  39.5 5.9 %collective-permute-start.8 = (bf16[144,768]{1,0:T(8,128)(2,1)S(1)}, bf16[144,768]{1,0:T(8,128)(2,1)S(1)}, u32[]{:S(2)}, u32[]{:S(2)}) collective-permute-start(bf16[144,768]{1,0:T(8,128)(2,1)S(1)} %collective-permute-done.6.refs_4_.refs_5_), channel_id=1, source_target_pairs={{0,1},{1,0},{2,3},{3,2},{4,5},{5,4},{6,7},{7,6},{8,9},{9,8},{10,11... | collective-permute-start | bytes 663560 | tf_op jit(solution)/shard_map/ppermute | solution.py:234
  48.9 2.5 %collective-permute-start.15 = (f32[4,384]{1,0:T(4,128)S(1)}, f32[4,384]{1,0:T(4,128)S(1)}, u32[]{:S(2)}, u32[]{:S(2)}) collective-permute-start(f32[4,384]{1,0:T(4,128)S(1)} %get-tuple-element.44), channel_id=1, source_target_pairs={{0,1},{1,0},{2,3},{3,2},{4,5},{5,4},{6,7},{7,6},{8,9},{9,8},{10,11... | collective-permute-start | bytes 18440 | tf_op jit(solution)/shard_map/ppermute | solution.py:234
  49.2 5.7 %collective-permute-start.14 = (f32[1,384]{1,0:T(1,128)S(1)}, f32[1,384]{1,0:T(1,128)S(1)}, u32[]{:S(2)}, u32[]{:S(2)}) collective-permute-start(f32[1,384]{1,0:T(1,128)S(1)} %pad_maximum_fusion), channel_id=1, source_target_pairs={{0,8},{1,9},{2,10},{3,11},{4,12},{5,13},{6,14},{7,15},{8,24},{9,25... | collective-permute-start | bytes 4616 | tf_op jit(solution)/shard_map/ppermute | solution.py:234
  49.3 5.7 %collective-permute-start.12 = (f32[1,384]{1,0:T(1,128)S(1)}, f32[1,384]{1,0:T(1,128)S(1)}, u32[]{:S(2)}, u32[]{:S(2)}) collective-permute-start(f32[1,384]{1,0:T(1,128)S(1)} %get-tuple-element.35), channel_id=1, source_target_pairs={{0,24},{1,25},{2,26},{3,27},{4,28},{5,29},{6,30},{7,31},{8,0},{9,1... | collective-permute-start | bytes 4616 | tf_op jit(solution)/shard_map/ppermute | solution.py:234
  51.4 3.6 %collective-permute-start.16 = (f32[1,384]{1,0:T(1,128)S(1)}, f32[1,384]{1,0:T(1,128)S(1)}, u32[]{:S(2)}, u32[]{:S(2)}) collective-permute-start(f32[1,384]{1,0:T(1,128)S(1)} %get-tuple-element.46), channel_id=1, source_target_pairs={{2,0},{3,1},{0,2},{1,3},{6,4},{7,5},{4,6},{5,7},{10,8},{11,9},{8,1... | collective-permute-start | bytes 4616 | tf_op jit(solution)/shard_map/ppermute | solution.py:234
  52.0 3.6 %collective-permute-start.17 = (f32[1,384]{1,0:T(1,128)S(1)}, f32[1,384]{1,0:T(1,128)S(1)}, u32[]{:S(2)}, u32[]{:S(2)}) collective-permute-start(f32[1,384]{1,0:T(1,128)S(1)} %get-tuple-element.47), channel_id=1, source_target_pairs={{4,0},{5,1},{6,2},{7,3},{0,4},{1,5},{2,6},{3,7},{12,8},{13,9},{14,... | collective-permute-start | bytes 4616 | tf_op jit(solution)/shard_map/ppermute | solution.py:234
  53.5 4.5 %collective-permute-start.18 = (f32[1,384]{1,0:T(1,128)S(1)}, f32[1,384]{1,0:T(1,128)S(1)}, u32[]{:S(2)}, u32[]{:S(2)}) collective-permute-start(f32[1,384]{1,0:T(1,128)S(1)} %get-tuple-element.48), channel_id=1, source_target_pairs={{6,0},{7,1},{4,2},{5,3},{2,4},{3,5},{0,6},{1,7},{14,8},{15,9},{12,... | collective-permute-start | bytes 4616 | tf_op jit(solution)/shard_map/ppermute | solution.py:234
where the time goes:
time: 58.8 us; the launch traced here: 58.6 us
  waiting for transfers between devices  24.9 us (42%)
  starting transfers between devices  21.7 us (37%)
  Pallas kernels  9.45 us (16%)
  local copies, waits for them, and re-layouts  1.74 us (3%)
  other arithmetic  0.61 us (1%)
    ppermute x19, waiting for transfers between devices, send(): return lax.ppermute(value, AXES, pairs)  24.9 us
    ppermute x19, starting transfers between devices, send(): return lax.ppermute(value, AXES, pairs)  21.7 us
    pallas_call x4, Pallas kernels, match(): call(*in_vmem([*rows, *ours, *twins, *(value for value in row_in if value...  9 us
    unnamed x4, local copies, waits for them, and re-layouts  1.74 us
  transfers between devices with their start and end apart: 19, of which 7 were waited for; matrix products, arithmetic and copies ran while one was open for 0% of the time, Pallas kernels for 13%

commit v1 on v0

v1 whole, which is shorter than its diff:
```python
import functools

import jax
import jax.numpy as jnp
from jax import lax
from jax.experimental import pallas as pl
from jax.experimental.pallas import tpu as pltpu
from jax.sharding import PartitionSpec as P

AXES = ("row", "col")
CORES = 2
PAD = 16
FAR = 1.0e9
VMEM_GRANT = 16 << 20


class Layout:
    def __init__(self, mesh):
        rows, cols = mesh.shape["row"], mesh.shape["col"]
        self.xs = cols // CORES
        self.ys = self.xs if rows % self.xs == 0 else 1
        self.lines = rows // self.ys

    def index(self, line, y, x, core):
        return ((line * self.ys + y) * self.xs + x) * CORES + core

    def pairs(self, target):
        found = []
        for line in range(self.lines):
            for y in range(self.ys):
                for x in range(self.xs):
                    for core in range(CORES):
                        to = target(line, y, x, core)
                        if to is not None:
                            found.append((self.index(line, y, x, core), self.index(*to)))
        return found

    def plane_move(self, dy, dx):
        return self.pairs(lambda l, y, x, c: (l, (y + dy) % self.ys, (x + dx) % self.xs, c))

    def swap(self):
        return self.pairs(lambda l, y, x, c: (l, y, x, CORES - 1 - c))

    def plane_offsets(self):
        return [(dy, dx) for dy in range(self.ys) for dx in range(self.xs) if dy or dx]

    def line_maps(self):
        maps = []
        for step in range(1, (self.lines + 1) // 2):
            maps.append({i: (i + step) % self.lines for i in range(self.lines)})
        if self.lines % 2 == 0:
            half = self.lines // 2
            maps.append({(i if i % 2 == 0 else i + half): (i + half if i % 2 == 0 else i) for i in range(half)})
        return maps

    def line_move(self, line_map):
        return self.pairs(lambda l, y, x, c: (line_map[l], y, x, c) if l in line_map else None)

    def line_return(self, line_map):
        back = {b: a for a, b in line_map.items()}
        free = [i for i in range(self.lines) if i not in line_map]
        back.update(zip([i for i in range(self.lines) if i not in back], free))
        return self.line_move(back)


def backward(pairs):
    return [(b, a) for a, b in pairs]


def pack_body(pieces, chunk, emb_hbm, order_hbm, out_ref, *refs):
    piece_refs, (emb_ref, order_ref, sems) = refs[: len(pieces)], refs[len(pieces) :]
    n, width = emb_ref.shape
    order_copy = pltpu.make_async_copy(order_hbm, order_ref, sems.at[0])
    order_copy.start()
    copies = []
    for k in range(n // chunk):
        rows = pl.ds(k * chunk, chunk)
        copies.append(pltpu.make_async_copy(emb_hbm.at[rows, :], emb_ref.at[rows, :], sems.at[k + 1]))
        copies[-1].start()
    out_ref[n:, :] = jnp.zeros((PAD, width), jnp.bfloat16)
    order_copy.wait()
    code = order_ref[...].reshape(1, n) + 1
    high = (code >> 8).astype(jnp.float32)
    low = (code & 255).astype(jnp.float32)
    line = lax.broadcasted_iota(jnp.int32, (PAD, n), 0)
    tail = jnp.where(line == 0, high, jnp.where(line == 1, low, 0.0))
    out_ref[n:, :n] = tail.astype(jnp.bfloat16)
    for k in range(n // chunk):
        copies[k].wait()
        rows = slice(k * chunk, (k + 1) * chunk)
        floats = emb_ref[rows, :].astype(jnp.float32)
        scale = lax.rsqrt(jnp.sum(floats * floats, axis=1, keepdims=True) + 1e-06)
        out_ref[rows, :] = (floats * scale).astype(jnp.bfloat16)
    for (start, rows), ref in zip(pieces, piece_refs):
        cut(out_ref, start, rows, ref)


def pack(embeddings, doc_order, pieces):
    n, width = embeddings.shape
    chunk = 128 if n % 128 == 0 else n
    call = pl.pallas_call(
        functools.partial(pack_body, pieces, chunk),
        in_specs=[pl.BlockSpec(memory_space=pltpu.HBM)] * 2,
        out_shape=[pltpu.VMEM((rows + PAD, width), jnp.bfloat16) for rows in (n, *(rows for _, rows in pieces))],
        scratch_shapes=[
            pltpu.VMEM((n, width), jnp.bfloat16),
            pltpu.VMEM((n,), jnp.int32),
            pltpu.SemaphoreType.DMA((n // chunk + 1,)),
        ],
        compiler_params=pltpu.CompilerParams(vmem_limit_bytes=VMEM_GRANT),
        name="pack",
    )
    return call(*(pltpu.with_memory_space_constraint(v, pltpu.HBM) for v in (embeddings, doc_order)))


def cut(ref, start, rows, out_ref):
    n = ref.shape[0] - PAD
    out_ref[:rows, :] = ref[start : start + rows, :]
    out_ref[rows:, :] = jnp.zeros((PAD, ref.shape[1]), jnp.bfloat16)
    out_ref[rows:, :rows] = ref[n:, start : start + rows]


def piece_body(start, rows, ref, out_ref):
    cut(ref, start, rows, out_ref)


def piece(block, start, rows):
    return pl.pallas_call(
        functools.partial(piece_body, start, rows),
        out_shape=pltpu.VMEM((rows + PAD, block.shape[1]), jnp.bfloat16),
        compiler_params=pltpu.CompilerParams(vmem_limit_bytes=VMEM_GRANT),
        name="piece",
    )(*in_vmem([block]))


def lane_orders(ref):
    n = ref.shape[0] - PAD
    tail = ref[n:, :n].astype(jnp.float32)
    order = tail[0:1] * 256.0 + tail[1:2]
    return jnp.where(order == 0.0, FAR, order)


def match_body(plan, chips, known, *refs):
    at = 0

    def take(count):
        nonlocal at
        at += count
        return refs[at - count : at]

    side_cols = sum(chips)
    rows, ours, twins = take(len(plan)), take(side_cols), take(side_cols)
    row_in, col_in = list(take(sum(p[2] for p in plan))), take(2 * known.count(0))
    row_out, col_out = take(1 + max(p[3] for p in plan)), take(2)
    (col_acc,) = take(1)
    lanes = 128
    firsts = [sum(chips[:k]) for k in range(len(chips) + 1)]
    fresh = set()
    for r, (meets, counted, has_known, out, first_lane) in enumerate(plan):
        n = rows[r].shape[0] - PAD
        own_orders = lane_orders(rows[r])
        own_order = jnp.broadcast_to(own_orders, (lanes, n)).T[:, 0:1]
        best = jnp.full((n, lanes), -1.0, jnp.float32)
        for chip in meets:
            blocks = [side[c] for side in (ours, twins) for c in range(firsts[chip], firsts[chip + 1])]
            units = jnp.concatenate([ref[: ref.shape[0] - PAD, :] for ref in blocks], axis=0)
            orders = jnp.concatenate([lane_orders(ref) for ref in blocks], axis=1)
            score = lax.dot_general(
                rows[r][:n, :], units, (((1,), (1,)), ((), ())), preferred_element_type=jnp.float32
            )
            for k in range(0, units.shape[0], lanes):
                part = score[:, k : k + lanes]
                earlier = orders[:, k : k + lanes] < own_order
                best = jnp.maximum(best, jnp.where(earlier, part, -1.0))
                if counted:
                    other = jnp.max(jnp.where(earlier, -1.0, part).reshape(n // 8, 8, lanes), axis=0)
                    if chip in fresh:
                        other = jnp.maximum(col_acc[chip, :, k : k + lanes], other)
                    col_acc[chip, :, k : k + lanes] = other
            if counted:
                fresh.add(chip)
        value = jnp.where(own_orders == FAR, -1.0, jnp.max(best.T, axis=0, keepdims=True))
        if has_known:
            value = jnp.maximum(value, row_in.pop(0)[...])
        row_out[out][0:1, first_lane : first_lane + n] = value
    for side in range(2):
        before = [col_in[side * known.count(0) + i][k : k + 1, :] for i, k in zip(group_index(known), known)]
        n = col_out[side].shape[1]
        for chip in range(len(chips)):
            value = jnp.max(col_acc[chip, :, side * n : (side + 1) * n], axis=0, keepdims=True)
            if chip < len(before):
                value = jnp.maximum(value, before[chip])
            col_out[side][chip : chip + 1, :] = value


def group_index(known):
    groups = []
    for k in known:
        groups.append((groups[-1] if groups else -1) + (k == 0))
    return groups


def in_vmem(values):
    return [pltpu.with_memory_space_constraint(v, pltpu.VMEM) for v in values]


def match(rows, chips, col_in=()):
    ours = [block for mine, _ in chips for block in mine]
    twins = [block for _, other in chips for block in other]
    width = rows[0][0].shape[1]
    n = sum(block.shape[0] - PAD for block in chips[0][0])
    sizes = [row[0].shape[0] - PAD for row in rows]
    plan = [(tuple(meets), counted, value is not None, out, lane) for _, meets, counted, value, out, lane in rows]
    totals = [max(p[4] + size for p, size in zip(plan, sizes) if p[3] == k) for k in range(1 + max(p[3] for p in plan))]
    known = [k for pair in col_in for k in range(pair[0].shape[0])]
    before = [pair[0] for pair in col_in] + [pair[1] for pair in col_in]
    block = pltpu.VMEM((len(chips), n), jnp.float32)
    call = pl.pallas_call(
        functools.partial(match_body, plan, [len(mine) for mine, _ in chips], known),
        out_shape=[pltpu.VMEM((1, total), jnp.float32) for total in totals] + [block, block],
        scratch_shapes=[pltpu.VMEM((len(chips), 8, 2 * n), jnp.float32)],
        cost_estimate=pl.CostEstimate(
            flops=4 * sum(size * len(p[0]) for p, size in zip(plan, sizes)) * n * width,
            bytes_accessed=2 * (sum(sizes) + 2 * len(chips) * n) * width,
            transcendentals=0,
        ),
        compiler_params=pltpu.CompilerParams(vmem_limit_bytes=VMEM_GRANT),
    )
    values = [row[3] for row in rows if row[3] is not None]
    outs = call(*in_vmem([*(row[0] for row in rows), *ours, *twins, *values, *before]))
    return outs[: len(totals)], tuple(outs[len(totals) :])


def merge_body(ours_ref, theirs_ref, *out_refs):
    value = jnp.maximum(ours_ref[...], theirs_ref[...])
    for k, ref in enumerate(out_refs):
        ref[...] = value[k : k + 1]


def merge(ours, theirs):
    count, n = ours.shape
    return pl.pallas_call(
        merge_body,
        out_shape=[pltpu.VMEM((1, n), jnp.float32)] * count,
        compiler_params=pltpu.CompilerParams(vmem_limit_bytes=VMEM_GRANT),
        name="merge",
    )(*in_vmem([ours, theirs]))


def solution(mesh):
    layout = Layout(mesh)
    maps = layout.line_maps()
    offsets = layout.plane_offsets()

    def send(value, pairs):
        return lax.ppermute(value, AXES, pairs)

    def nearest(embeddings, doc_order):
        n = embeddings.shape[0]
        last = min(n, 128)
        pieces = ((0, n - last), (n - last, last)) if n > last else ((0, n),)
        swap = layout.swap()

        own, *parts = pack(embeddings, doc_order, pieces)
        line = [send(own, layout.line_move(m)) for m in maps[:-1]]
        plane = [send(own, layout.plane_move(*d)) for d in offsets[:-1]]
        half = [send(part, layout.line_move(maps[-1])) for part in parts]

        dy, dx = offsets[-1]
        routes = [((0, dx), (dy, 0)), ((dy, 0), (0, dx))]
        corner = []
        for k, (start, rows) in enumerate(pieces):
            have, move = routes[k % 2]
            block = piece(plane[offsets.index(have)], start, rows)
            corner.append(send(block, layout.plane_move(*move)))
        near_chips = [([block], [send(block, swap)]) for block in [own, *plane]]
        far_chip = (corner, [send(block, swap) for block in corner])

        every = range(len(near_chips))
        far = len(near_chips)
        first = [own, *line]
        rows = [(block, every, k > 0, None, k, 0) for k, block in enumerate(first)]
        best, cols = match(rows, near_chips)
        side, cols = match([(block, every, True, None, k, 0) for k, block in enumerate(half[:-1])], near_chips, [cols])
        rows = [(block, [far], k > 0, best[k], k, 0) for k, block in enumerate(first)]
        rows += [(block, [far], True, side[k], len(first), pieces[k][0]) for k, block in enumerate(half[:-1])]
        rows.append((half[-1], [far, *every], True, None, len(first), pieces[-1][0]))
        best, (ours, theirs) = match(rows, [*near_chips, far_chip], [cols])

        theirs = send(theirs, swap)
        back = [best[0]]
        for value, m in zip(best[1:], maps):
            back.append(send(value, layout.line_return(m)))
        own_best, *others = merge(ours, theirs)
        back.append(own_best)
        for value, d in zip(others, offsets):
            back.append(send(value, backward(layout.plane_move(*d))))
        best = functools.reduce(jnp.maximum, back)
        return jnp.maximum(best, -1.0).reshape(doc_order.shape)

    return jax.shard_map(
        nearest,
        mesh=mesh,
        in_specs=(P(AXES, None), P(AXES)),
        out_specs=P(AXES),
        check_vma=False,
    )
```

time: 58.8 us -> 54.7 us (0.930)
  waiting for transfers between devices: 24.9 us -> 22.8 us
  local copies, waits for them, and re-layouts: 1.74 us -> 0 us
  Pallas kernels: 9.45 us -> 8.86 us
    ppermute x19 -> x18, waiting for transfers between devices: 24.9 us -> 22.8 us  [send(): return lax.ppermute(value, AXES, pairs)]
    unnamed x4 -> x0, local copies, waits for them, and re-layouts: 1.74 us -> none
    pallas_call x6 -> x4, Pallas kernels: 9.4 us -> 8.8 us  [the longest x3 7.42 us: match(): call(*in_vmem([*(row[0] for row in rows), *ours, *twins, *values, *before]))]
    ppermute x19 -> x18, starting transfers between devices: 21.7 us -> 22.1 us  [send(): return lax.ppermute(value, AXES, pairs)]
  transfers between devices with their start and end apart: 19 -> 18, of which waited for: 7 -> 8; matrix products, arithmetic and copies ran while one was open for 0% -> 0% of each run, Pallas kernels for 13% -> 8%
where the time goes in v1:
time: 54.7 us; the launch traced here: 54.5 us
  waiting for transfers between devices  22.8 us (42%)
  starting transfers between devices  22.1 us (40%)
  Pallas kernels  8.86 us (16%)
  other arithmetic  0.6 us (1%)
    ppermute x18, waiting for transfers between devices, send(): return lax.ppermute(value, AXES, pairs)  22.8 us
    ppermute x18, starting transfers between devices, send(): return lax.ppermute(value, AXES, pairs)  22.1 us
    pallas_call x3, Pallas kernels, match(): call(*in_vmem([*(row[0] for row in rows), *ours, *twins, *values, *before]))  7.42 us
    pallas_call x1, Pallas kernels, pack(): call(*(pltpu.with_memory_space_constraint(v, pltpu.HBM) for v in (embeddi...  1.38 us
  transfers between devices with their start and end apart: 18, of which 8 were waited for; matrix products, arithmetic and copies ran while one was open for 0% of the time, Pallas kernels for 8%

profile of v1, /device:TPU:0, one launch (start us, length us, event | category | flops | bytes accessed | tf_op | source)
XLA Modules:
  0.0 54.5 jit_solution(6795502703284380715)
XLA Ops:
  0.0 1.4 %pack.1 = (bf16[400,768]{1,0:T(8,128)(2,1)S(1)}, bf16[272,768]{1,0:T(8,128)(2,1)S(1)}, bf16[144,768]{1,0:T(8,128)(2,1)S(1)}) custom-call(bf16[384,768]{1,0:T(8,128)(2,1)} %emb_hbm.1, s32[384]{0:T(512)} %order_hbm.1), custom_call_target="tpu_custom_call" | custom-call | tf_op jit(solution)/shard_map/pack/pallas_call | solution.py:113
  1.4 3.1 %collective-permute-start.4 = (bf16[400,768]{1,0:T(8,128)(2,1)S(1)}, bf16[400,768]{1,0:T(8,128)(2,1)S(1)}, u32[]{:S(2)}, u32[]{:S(2)}) collective-permute-start(bf16[400,768]{1,0:T(8,128)(2,1)S(1)} %get-tuple-element.24.refs_0_.refs_2_.refs_1_.refs_4_), channel_id=1, source_target_pairs={{0,4},{1,5},{2,6},{3,7},{4,0},{5,1},{6,2},{7,3},{8,12},{9,13},{10,... | collective-permute-start | bytes 1843208 | tf_op jit(solution)/shard_map/ppermute | solution.py:256
  4.5 1.5 %collective-permute-start.3 = (bf16[400,768]{1,0:T(8,128)(2,1)S(1)}, bf16[400,768]{1,0:T(8,128)(2,1)S(1)}, u32[]{:S(2)}, u32[]{:S(2)}) collective-permute-start(bf16[400,768]{1,0:T(8,128)(2,1)S(1)} %get-tuple-element.24.refs_0_.refs_2_.refs_1_.refs_4_), channel_id=1, source_target_pairs={{0,2},{1,3},{2,0},{3,1},{4,6},{5,7},{6,4},{7,5},{8,10},{9,11},{10,... | collective-permute-start | bytes 1843208 | tf_op jit(solution)/shard_map/ppermute | solution.py:256
  5.9 1.6 %collective-permute-start = (bf16[400,768]{1,0:T(8,128)(2,1)S(1)}, bf16[400,768]{1,0:T(8,128)(2,1)S(1)}, u32[]{:S(2)}, u32[]{:S(2)}) collective-permute-start(bf16[400,768]{1,0:T(8,128)(2,1)S(1)} %get-tuple-element.24.refs_0_.refs_2_.refs_1_.refs_4_), channel_id=1, source_target_pairs={{0,8},{1,9},{2,10},{3,11},{4,12},{5,13},{6,14},{7,15},{8,16},{9,17... | collective-permute-start | bytes 1843208 | tf_op jit(solution)/shard_map/ppermute | solution.py:256
  7.5 10.8 %collective-permute-done.4.ref.refs_4_.refs_3_.refs_6_ = bf16[400,768]{1,0:T(8,128)(2,1)S(1)} collective-permute-done((bf16[400,768]{1,0:T(8,128)(2,1)S(1)}, bf16[400,768]{1,0:T(8,128)(2,1)S(1)}, u32[]{:S(2)}, u32[]{:S(2)}) %collective-permute-start.4) | collective-permute-done | bytes 614432 | tf_op jit(solution)/shard_map/ppermute | solution.py:256
  18.3 1.5 %collective-permute-done.3.ref.refs_3_.refs_2_.refs_5_ = bf16[400,768]{1,0:T(8,128)(2,1)S(1)} collective-permute-done((bf16[400,768]{1,0:T(8,128)(2,1)S(1)}, bf16[400,768]{1,0:T(8,128)(2,1)S(1)}, u32[]{:S(2)}, u32[]{:S(2)}) %collective-permute-start.3) | collective-permute-done | bytes 614432 | tf_op jit(solution)/shard_map/ppermute | solution.py:256
  19.8 0.0 collective-permute-start.8
  19.8 0.9 %collective-permute-start.5 = (bf16[272,768]{1,0:T(8,128)(2,1)S(1)}, bf16[272,768]{1,0:T(8,128)(2,1)S(1)}, u32[]{:S(2)}, u32[]{:S(2)}) collective-permute-start(bf16[272,768]{1,0:T(8,128)(2,1)S(1)} %piece.2), channel_id=1, source_target_pairs={{0,4},{1,5},{2,6},{3,7},{4,0},{5,1},{6,2},{7,3},{8,12},{9,13},{10,... | collective-permute-start | bytes 1253384 | tf_op jit(solution)/shard_map/ppermute | solution.py:256
  20.7 0.0 collective-permute-done.7.refs_5_.refs_4_.refs_9_
  20.7 1.6 %collective-permute-start.6 = (bf16[144,768]{1,0:T(8,128)(2,1)S(1)}, bf16[144,768]{1,0:T(8,128)(2,1)S(1)}, u32[]{:S(2)}, u32[]{:S(2)}) collective-permute-start(bf16[144,768]{1,0:T(8,128)(2,1)S(1)} %piece.3), channel_id=1, source_target_pairs={{0,2},{1,3},{2,0},{3,1},{4,6},{5,7},{6,4},{7,5},{8,10},{9,11},{10,... | collective-permute-start | bytes 663560 | tf_op jit(solution)/shard_map/ppermute | solution.py:256
  22.2 1.8 %collective-permute-done.refs_1_ = bf16[400,768]{1,0:T(8,128)(2,1)S(1)} collective-permute-done((bf16[400,768]{1,0:T(8,128)(2,1)S(1)}, bf16[400,768]{1,0:T(8,128)(2,1)S(1)}, u32[]{:S(2)}, u32[]{:S(2)}) %collective-permute-start) | collective-permute-done | bytes 614432 | tf_op jit(solution)/shard_map/ppermute | solution.py:256
  24.1 2.7 %collective-permute-start.1 = (bf16[272,768]{1,0:T(8,128)(2,1)S(1)}, bf16[272,768]{1,0:T(8,128)(2,1)S(1)}, u32[]{:S(2)}, u32[]{:S(2)}) collective-permute-start(bf16[272,768]{1,0:T(8,128)(2,1)S(1)} %get-tuple-element.25), channel_id=1, source_target_pairs={{0,16},{1,17},{2,18},{3,19},{4,20},{5,21},{6,22},{7,23},{24,8},{25... | collective-permute-start | bytes 1253384 | tf_op jit(solution)/shard_map/ppermute | solution.py:256
  26.8 5.2 %collective-permute-done.5.refs_7_ = bf16[272,768]{1,0:T(8,128)(2,1)S(1)} collective-permute-done((bf16[272,768]{1,0:T(8,128)(2,1)S(1)}, bf16[272,768]{1,0:T(8,128)(2,1)S(1)}, u32[]{:S(2)}, u32[]{:S(2)}) %collective-permute-start.5) | collective-permute-done | bytes 417824 | tf_op jit(solution)/shard_map/ppermute | solution.py:256
  31.9 0.0 collective-permute-start.10
  31.9 0.0 collective-permute-done.6.refs_8_
  31.9 4.5 %collective-permute-start.2 = (bf16[144,768]{1,0:T(8,128)(2,1)S(1)}, bf16[144,768]{1,0:T(8,128)(2,1)S(1)}, u32[]{:S(2)}, u32[]{:S(2)}) collective-permute-start(bf16[144,768]{1,0:T(8,128)(2,1)S(1)} %get-tuple-element.26), channel_id=1, source_target_pairs={{0,16},{1,17},{2,18},{3,19},{4,20},{5,21},{6,22},{7,23},{24,8},{25... | collective-permute-start | bytes 663560 | tf_op jit(solution)/shard_map/ppermute | solution.py:256
  36.4 0.3 collective-permute-start.11
  36.7 0.0 collective-permute-done.8.refs_6_.refs_5_.refs_10_
  36.7 3.1 %shard_map.28 = (f32[1,384]{1,0:T(1,128)S(1)}, f32[1,384]{1,0:T(1,128)S(1)}, f32[3,384]{1,0:T(4,128)S(1)}, f32[3,384]{1,0:T(4,128)S(1)}) custom-call(bf16[400,768]{1,0:T(8,128)(2,1)S(1)} %get-tuple-element.24.refs_0_.refs_2_.refs_1_.refs_4_, bf16[400,768]{1,0:T(8,128)(2,1)S(1)} %collective-permute-done.refs_1_, ...), custom_call_target="tpu_custom_call" | custom-call | flops 2717908992 | bytes 4718592 | tf_op jit(solution)/shard_map/pallas_call | solution.py:230
  39.9 1.3 %shard_map.29 = (f32[1,256]{1,0:T(1,128)S(1)}, f32[3,384]{1,0:T(4,128)S(1)}, f32[3,384]{1,0:T(4,128)S(1)}) custom-call(bf16[272,768]{1,0:T(8,128)(2,1)S(1)} %collective-permute-done.1.refs_0_.refs_2_, bf16[400,768]{1,0:T(8,128)(2,1)S(1)} %get-tuple-element.24.refs_0_.refs_2_.refs_1_.refs_4_, ...), custom_call_target="tpu_custom_call" | custom-call | flops 905969664 | bytes 3932160 | tf_op jit(solution)/shard_map/pallas_call | solution.py:230
  41.1 0.6 %collective-permute-done.2.refs_3_ = bf16[144,768]{1,0:T(8,128)(2,1)S(1)} collective-permute-done((bf16[144,768]{1,0:T(8,128)(2,1)S(1)}, bf16[144,768]{1,0:T(8,128)(2,1)S(1)}, u32[]{:S(2)}, u32[]{:S(2)}) %collective-permute-start.2) | collective-permute-done | bytes 221216 | tf_op jit(solution)/shard_map/ppermute | solution.py:256
  41.8 3.0 %shard_map.30 = (f32[1,384]{1,0:T(1,128)S(1)}, f32[1,384]{1,0:T(1,128)S(1)}, f32[1,384]{1,0:T(1,128)S(1)}, f32[4,384]{1,0:T(4,128)S(1)}, f32[4,384]{1,0:T(4,128)S(1)}) custom-call(bf16[400,768]{1,0:T(8,128)(2,1)S(1)} %get-tuple-element.24.refs_0_.refs_2_.refs_1_.refs_4_, bf16[400,768]{1,0:T(8,128)(2,1)S(1)} %collective-permute-done.refs_1_, ...), custom_call_target="tpu_custom_call" | custom-call | flops 1811939328 | bytes 6488064 | tf_op jit(solution)/shard_map/pallas_call | solution.py:230
  44.8 0.1 collective-permute-start.14
  44.9 1.4 %collective-permute-start.12 = (f32[1,384]{1,0:T(1,128)S(1)}, f32[1,384]{1,0:T(1,128)S(1)}, u32[]{:S(2)}, u32[]{:S(2)}) collective-permute-start(f32[1,384]{1,0:T(1,128)S(1)} %get-tuple-element.35), channel_id=1, source_target_pairs={{0,24},{1,25},{2,26},{3,27},{4,28},{5,29},{6,30},{7,31},{8,0},{9,1... | collective-permute-start | bytes 4616 | tf_op jit(solution)/shard_map/ppermute | solution.py:256
  46.3 1.1 %collective-permute-start.13 = (f32[1,384]{1,0:T(1,128)S(1)}, f32[1,384]{1,0:T(1,128)S(1)}, u32[]{:S(2)}, u32[]{:S(2)}) collective-permute-start(f32[1,384]{1,0:T(1,128)S(1)} %get-tuple-element.36), channel_id=1, source_target_pairs={{0,8},{1,9},{2,10},{3,11},{4,12},{5,13},{6,14},{7,15},{8,24},{9,25... | collective-permute-start | bytes 4616 | tf_op jit(solution)/shard_map/ppermute | solution.py:256
  47.4 1.6 %collective-permute-start.15 = (f32[1,384]{1,0:T(1,128)S(1)}, f32[1,384]{1,0:T(1,128)S(1)}, u32[]{:S(2)}, u32[]{:S(2)}) collective-permute-start(f32[1,384]{1,0:T(1,128)S(1)} %get-tuple-element.40), channel_id=1, source_target_pairs={{2,0},{3,1},{0,2},{1,3},{6,4},{7,5},{4,6},{5,7},{10,8},{11,9},{8,1... | collective-permute-start | bytes 4616 | tf_op jit(solution)/shard_map/ppermute | solution.py:256
  48.9 0.5 collective-permute-start.16
  49.5 1.5 %collective-permute-start.17 = (f32[1,384]{1,0:T(1,128)S(1)}, f32[1,384]{1,0:T(1,128)S(1)}, u32[]{:S(2)}, u32[]{:S(2)}) collective-permute-start(f32[1,384]{1,0:T(1,128)S(1)} %get-tuple-element.42), channel_id=1, source_target_pairs={{6,0},{7,1},{4,2},{5,3},{2,4},{3,5},{0,6},{1,7},{14,8},{15,9},{12,... | collective-permute-start | bytes 4616 | tf_op jit(solution)/shard_map/ppermute | solution.py:256
  50.9 0.1 collective-permute-done.15
  51.0 1.5 %collective-permute-done.16 = f32[1,384]{1,0:T(1,128)S(1)} collective-permute-done((f32[1,384]{1,0:T(1,128)S(1)}, f32[1,384]{1,0:T(1,128)S(1)}, u32[]{:S(2)}, u32[]{:S(2)}) %collective-permute-start.16) | collective-permute-done | bytes 1568 | tf_op jit(solution)/shard_map/ppermute | solution.py:256
  52.5 1.4 %collective-permute-done.17 = f32[1,384]{1,0:T(1,128)S(1)} collective-permute-done((f32[1,384]{1,0:T(1,128)S(1)}, f32[1,384]{1,0:T(1,128)S(1)}, u32[]{:S(2)}, u32[]{:S(2)}) %collective-permute-start.17) | collective-permute-done | bytes 1568 | tf_op jit(solution)/shard_map/ppermute | solution.py:256
  53.9 0.6 %maximum_reduce_fusion = f32[384]{0:T(512)} fusion(f32[1,384]{1,0:T(1,128)S(1)} %collective-permute-done.17, f32[1,384]{1,0:T(1,128)S(1)} %collective-permute-done.16, f32[1,384]{1,0:T(1,128)S(1)} %collective-permute-done.15, f32[1,384]{1,0:T(1,128)S(1)} %get-tuple-element.39, f32[1,384]{1,0:T(1,128)S(1)} %collective-permute-done.13, ...), kind=kLoop, calls=%fused_computation | loop fusion | flops 2688 | bytes 12288 | tf_op jit(solution)/shard_map/max | solution.py:299
  (12 shorter events, 0.1 us)
Async XLA Ops:
  1.4 16.9 %collective-permute-start.4 = (bf16[400,768]{1,0:T(8,128)(2,1)S(1)}, bf16[400,768]{1,0:T(8,128)(2,1)S(1)}, u32[]{:S(2)}, u32[]{:S(2)}) collective-permute-start(bf16[400,768]{1,0:T(8,128)(2,1)S(1)} %get-tuple-element.24.refs_0_.refs_2_.refs_1_.refs_4_), channel_id=1, source_target_pairs={{0,4},{1,5},{2,6},{3,7},{4,0},{5,1},{6,2},{7,3},{8,12},{9,13},{10,... | collective-permute-start | bytes 1843208 | tf_op jit(solution)/shard_map/ppermute | solution.py:256
  4.5 15.3 %collective-permute-start.3 = (bf16[400,768]{1,0:T(8,128)(2,1)S(1)}, bf16[400,768]{1,0:T(8,128)(2,1)S(1)}, u32[]{:S(2)}, u32[]{:S(2)}) collective-permute-start(bf16[400,768]{1,0:T(8,128)(2,1)S(1)} %get-tuple-element.24.refs_0_.refs_2_.refs_1_.refs_4_), channel_id=1, source_target_pairs={{0,2},{1,3},{2,0},{3,1},{4,6},{5,7},{6,4},{7,5},{8,10},{9,11},{10,... | collective-permute-start | bytes 1843208 | tf_op jit(solution)/shard_map/ppermute | solution.py:256
  5.9 14.7 %collective-permute-start.7 = (bf16[400,768]{1,0:T(8,128)(2,1)S(1)}, bf16[400,768]{1,0:T(8,128)(2,1)S(1)}, u32[]{:S(2)}, u32[]{:S(2)}) collective-permute-start(bf16[400,768]{1,0:T(8,128)(2,1)S(1)} %get-tuple-element.24.refs_0_.refs_2_.refs_1_.refs_4_), channel_id=1, source_target_pairs={{0,1},{1,0},{2,3},{3,2},{4,5},{5,4},{6,7},{7,6},{8,9},{9,8},{10,11... | collective-permute-start | bytes 1843208 | tf_op jit(solution)/shard_map/ppermute | solution.py:256
  5.9 18.1 %collective-permute-start = (bf16[400,768]{1,0:T(8,128)(2,1)S(1)}, bf16[400,768]{1,0:T(8,128)(2,1)S(1)}, u32[]{:S(2)}, u32[]{:S(2)}) collective-permute-start(bf16[400,768]{1,0:T(8,128)(2,1)S(1)} %get-tuple-element.24.refs_0_.refs_2_.refs_1_.refs_4_), channel_id=1, source_target_pairs={{0,8},{1,9},{2,10},{3,11},{4,12},{5,13},{6,14},{7,15},{8,16},{9,17... | collective-permute-start | bytes 1843208 | tf_op jit(solution)/shard_map/ppermute | solution.py:256
  18.3 18.1 %collective-permute-start.9 = (bf16[400,768]{1,0:T(8,128)(2,1)S(1)}, bf16[400,768]{1,0:T(8,128)(2,1)S(1)}, u32[]{:S(2)}, u32[]{:S(2)}) collective-permute-start(bf16[400,768]{1,0:T(8,128)(2,1)S(1)} %collective-permute-done.4.ref.refs_4_.refs_3_.refs_6_), channel_id=1, source_target_pairs={{0,1},{1,0},{2,3},{3,2},{4,5},{5,4},{6,7},{7,6},{8,9},{9,8},{10,11... | collective-permute-start | bytes 1843208 | tf_op jit(solution)/shard_map/ppermute | solution.py:256
  19.8 17.0 %collective-permute-start.8 = (bf16[400,768]{1,0:T(8,128)(2,1)S(1)}, bf16[400,768]{1,0:T(8,128)(2,1)S(1)}, u32[]{:S(2)}, u32[]{:S(2)}) collective-permute-start(bf16[400,768]{1,0:T(8,128)(2,1)S(1)} %collective-permute-done.3.ref.refs_3_.refs_2_.refs_5_), channel_id=1, source_target_pairs={{0,1},{1,0},{2,3},{3,2},{4,5},{5,4},{6,7},{7,6},{8,9},{9,8},{10,11... | collective-permute-start | bytes 1843208 | tf_op jit(solution)/shard_map/ppermute | solution.py:256
  19.8 12.1 %collective-permute-start.5 = (bf16[272,768]{1,0:T(8,128)(2,1)S(1)}, bf16[272,768]{1,0:T(8,128)(2,1)S(1)}, u32[]{:S(2)}, u32[]{:S(2)}) collective-permute-start(bf16[272,768]{1,0:T(8,128)(2,1)S(1)} %piece.2), channel_id=1, source_target_pairs={{0,4},{1,5},{2,6},{3,7},{4,0},{5,1},{6,2},{7,3},{8,12},{9,13},{10,... | collective-permute-start | bytes 1253384 | tf_op jit(solution)/shard_map/ppermute | solution.py:256
  20.7 11.2 %collective-permute-start.6 = (bf16[144,768]{1,0:T(8,128)(2,1)S(1)}, bf16[144,768]{1,0:T(8,128)(2,1)S(1)}, u32[]{:S(2)}, u32[]{:S(2)}) collective-permute-start(bf16[144,768]{1,0:T(8,128)(2,1)S(1)} %piece.3), channel_id=1, source_target_pairs={{0,2},{1,3},{2,0},{3,1},{4,6},{5,7},{6,4},{7,5},{8,10},{9,11},{10,... | collective-permute-start | bytes 663560 | tf_op jit(solution)/shard_map/ppermute | solution.py:256
  24.1 15.8 %collective-permute-start.1 = (bf16[272,768]{1,0:T(8,128)(2,1)S(1)}, bf16[272,768]{1,0:T(8,128)(2,1)S(1)}, u32[]{:S(2)}, u32[]{:S(2)}) collective-permute-start(bf16[272,768]{1,0:T(8,128)(2,1)S(1)} %get-tuple-element.25), channel_id=1, source_target_pairs={{0,16},{1,17},{2,18},{3,19},{4,20},{5,21},{6,22},{7,23},{24,8},{25... | collective-permute-start | bytes 1253384 | tf_op jit(solution)/shard_map/ppermute | solution.py:256
  31.9 9.8 %collective-permute-start.10 = (bf16[272,768]{1,0:T(8,128)(2,1)S(1)}, bf16[272,768]{1,0:T(8,128)(2,1)S(1)}, u32[]{:S(2)}, u32[]{:S(2)}) collective-permute-start(bf16[272,768]{1,0:T(8,128)(2,1)S(1)} %collective-permute-done.5.refs_7_), channel_id=1, source_target_pairs={{0,1},{1,0},{2,3},{3,2},{4,5},{5,4},{6,7},{7,6},{8,9},{9,8},{10,11... | collective-permute-start | bytes 1253384 | tf_op jit(solution)/shard_map/ppermute | solution.py:256
  31.9 9.8 %collective-permute-start.2 = (bf16[144,768]{1,0:T(8,128)(2,1)S(1)}, bf16[144,768]{1,0:T(8,128)(2,1)S(1)}, u32[]{:S(2)}, u32[]{:S(2)}) collective-permute-start(bf16[144,768]{1,0:T(8,128)(2,1)S(1)} %get-tuple-element.26), channel_id=1, source_target_pairs={{0,16},{1,17},{2,18},{3,19},{4,20},{5,21},{6,22},{7,23},{24,8},{25... | collective-permute-start | bytes 663560 | tf_op jit(solution)/shard_map/ppermute | solution.py:256
  36.4 5.3 %collective-permute-start.11 = (bf16[144,768]{1,0:T(8,128)(2,1)S(1)}, bf16[144,768]{1,0:T(8,128)(2,1)S(1)}, u32[]{:S(2)}, u32[]{:S(2)}) collective-permute-start(bf16[144,768]{1,0:T(8,128)(2,1)S(1)} %collective-permute-done.6.refs_8_), channel_id=1, source_target_pairs={{0,1},{1,0},{2,3},{3,2},{4,5},{5,4},{6,7},{7,6},{8,9},{9,8},{10,11... | collective-permute-start | bytes 663560 | tf_op jit(solution)/shard_map/ppermute | solution.py:256
  44.8 2.6 %collective-permute-start.14 = (f32[4,384]{1,0:T(4,128)S(1)}, f32[4,384]{1,0:T(4,128)S(1)}, u32[]{:S(2)}, u32[]{:S(2)}) collective-permute-start(f32[4,384]{1,0:T(4,128)S(1)} %get-tuple-element.38), channel_id=1, source_target_pairs={{0,1},{1,0},{2,3},{3,2},{4,5},{5,4},{6,7},{7,6},{8,9},{9,8},{10,11... | collective-permute-start | bytes 18440 | tf_op jit(solution)/shard_map/ppermute | solution.py:256
  44.9 6.1 %collective-permute-start.12 = (f32[1,384]{1,0:T(1,128)S(1)}, f32[1,384]{1,0:T(1,128)S(1)}, u32[]{:S(2)}, u32[]{:S(2)}) collective-permute-start(f32[1,384]{1,0:T(1,128)S(1)} %get-tuple-element.35), channel_id=1, source_target_pairs={{0,24},{1,25},{2,26},{3,27},{4,28},{5,29},{6,30},{7,31},{8,0},{9,1... | collective-permute-start | bytes 4616 | tf_op jit(solution)/shard_map/ppermute | solution.py:256
  46.3 4.7 %collective-permute-start.13 = (f32[1,384]{1,0:T(1,128)S(1)}, f32[1,384]{1,0:T(1,128)S(1)}, u32[]{:S(2)}, u32[]{:S(2)}) collective-permute-start(f32[1,384]{1,0:T(1,128)S(1)} %get-tuple-element.36), channel_id=1, source_target_pairs={{0,8},{1,9},{2,10},{3,11},{4,12},{5,13},{6,14},{7,15},{8,24},{9,25... | collective-permute-start | bytes 4616 | tf_op jit(solution)/shard_map/ppermute | solution.py:256
  47.4 3.6 %collective-permute-start.15 = (f32[1,384]{1,0:T(1,128)S(1)}, f32[1,384]{1,0:T(1,128)S(1)}, u32[]{:S(2)}, u32[]{:S(2)}) collective-permute-start(f32[1,384]{1,0:T(1,128)S(1)} %get-tuple-element.40), channel_id=1, source_target_pairs={{2,0},{3,1},{0,2},{1,3},{6,4},{7,5},{4,6},{5,7},{10,8},{11,9},{8,1... | collective-permute-start | bytes 4616 | tf_op jit(solution)/shard_map/ppermute | solution.py:256
  48.9 3.6 %collective-permute-start.16 = (f32[1,384]{1,0:T(1,128)S(1)}, f32[1,384]{1,0:T(1,128)S(1)}, u32[]{:S(2)}, u32[]{:S(2)}) collective-permute-start(f32[1,384]{1,0:T(1,128)S(1)} %get-tuple-element.41), channel_id=1, source_target_pairs={{4,0},{5,1},{6,2},{7,3},{0,4},{1,5},{2,6},{3,7},{12,8},{13,9},{14,... | collective-permute-start | bytes 4616 | tf_op jit(solution)/shard_map/ppermute | solution.py:256
  49.5 4.5 %collective-permute-start.17 = (f32[1,384]{1,0:T(1,128)S(1)}, f32[1,384]{1,0:T(1,128)S(1)}, u32[]{:S(2)}, u32[]{:S(2)}) collective-permute-start(f32[1,384]{1,0:T(1,128)S(1)} %get-tuple-element.42), channel_id=1, source_target_pairs={{6,0},{7,1},{4,2},{5,3},{2,4},{3,5},{0,6},{1,7},{14,8},{15,9},{12,... | collective-permute-start | bytes 4616 | tf_op jit(solution)/shard_map/ppermute | solution.py:256

commit v2 on v1

--- a/solution.py
+++ b/solution.py
@@ -55,6 +55,9 @@
 
     def line_move(self, line_map):
         return self.pairs(lambda l, y, x, c: (line_map[l], y, x, c) if l in line_map else None)
+
+    def line_hops(self):
+        return [{(b - 1) % self.lines: b for b in m.values()} for m in self.line_maps()]
 
     def line_return(self, line_map):
         back = {b: a for a, b in line_map.items()}
@@ -181,7 +184,7 @@
                 fresh.add(chip)
         value = jnp.where(own_orders == FAR, -1.0, jnp.max(best.T, axis=0, keepdims=True))
         if has_known:
-            value = jnp.maximum(value, row_in.pop(0)[...])
+            value = jnp.maximum(value, row_in.pop(0)[0:1, first_lane : first_lane + n])
         row_out[out][0:1, first_lane : first_lane + n] = value
     for side in range(2):
         before = [col_in[side * known.count(0) + i][k : k + 1, :] for i, k in zip(group_index(known), known)]
@@ -262,9 +265,11 @@
         swap = layout.swap()
 
         own, *parts = pack(embeddings, doc_order, pieces)
-        line = [send(own, layout.line_move(m)) for m in maps[:-1]]
+        line = []
+        for hop in layout.line_hops():
+            parts = [send(part, layout.line_move(hop)) for part in parts]
+            line.append(parts)
         plane = [send(own, layout.plane_move(*d)) for d in offsets[:-1]]
-        half = [send(part, layout.line_move(maps[-1])) for part in parts]
 
         dy, dx = offsets[-1]
         routes = [((0, dx), (dy, 0)), ((dy, 0), (0, dx))]
@@ -278,13 +283,15 @@
 
         every = range(len(near_chips))
         far = len(near_chips)
-        first = [own, *line]
-        rows = [(block, every, k > 0, None, k, 0) for k, block in enumerate(first)]
-        best, cols = match(rows, near_chips)
-        side, cols = match([(block, every, True, None, k, 0) for k, block in enumerate(half[:-1])], near_chips, [cols])
-        rows = [(block, [far], k > 0, best[k], k, 0) for k, block in enumerate(first)]
-        rows += [(block, [far], True, side[k], len(first), pieces[k][0]) for k, block in enumerate(half[:-1])]
-        rows.append((half[-1], [far, *every], True, None, len(first), pieces[-1][0]))
+        lanes = [start for start, _ in pieces]
+        first = [(own, False, 0, 0)]
+        first += [(block, True, k + 1, lane) for k, step in enumerate(line[:-1]) for block, lane in zip(step, lanes)]
+        half = [(block, True, len(line), lane) for block, lane in zip(line[-1], lanes)]
+        best, cols = match([(r[0], every, r[1], None, *r[2:]) for r in first], near_chips)
+        side, cols = match([(r[0], every, True, None, 0, r[3]) for r in half[:-1]], near_chips, [cols])
+        known = [*best, *side]
+        rows = [(r[0], [far], r[1], known[r[2]], *r[2:]) for r in first + half[:-1]]
+        rows.append((half[-1][0], [far, *every], True, None, *half[-1][2:]))
         best, (ours, theirs) = match(rows, [*near_chips, far_chip], [cols])
 
         theirs = send(theirs, swap)

time: 54.7 us -> 54.1 us (0.989)
  starting transfers between devices: 22.1 us -> 20.6 us
  Pallas kernels: 8.86 us -> 9.77 us
    ppermute x18 -> x19, starting transfers between devices: 22.1 us -> 20.6 us  [send(): return lax.ppermute(value, AXES, pairs)]
    pallas_call x3, Pallas kernels: 7.42 us -> 8.34 us  [match(): call(*in_vmem([*(row[0] for row in rows), *ours, *twins, *values, *before]))]
    ppermute x18 -> x19, waiting for transfers between devices: 22.8 us -> 22.7 us  [send(): return lax.ppermute(value, AXES, pairs)]
  transfers between devices with their start and end apart: 18 -> 19, of which waited for: 8 -> 7; matrix products, arithmetic and copies ran while one was open for 0% -> 0% of each run, Pallas kernels for 8% -> 9%
where the time goes in v2:
time: 54.1 us; the launch traced here: 53.9 us
  waiting for transfers between devices  22.7 us (42%)
  starting transfers between devices  20.6 us (38%)
  Pallas kernels  9.77 us (18%)
  other arithmetic  0.6 us (1%)
    ppermute x19, waiting for transfers between devices, send(): return lax.ppermute(value, AXES, pairs)  22.7 us
    ppermute x19, starting transfers between devices, send(): return lax.ppermute(value, AXES, pairs)  20.6 us
    pallas_call x3, Pallas kernels, match(): call(*in_vmem([*(row[0] for row in rows), *ours, *twins, *values, *before]))  8.34 us
    pallas_call x1, Pallas kernels, pack(): call(*(pltpu.with_memory_space_constraint(v, pltpu.HBM) for v in (embeddi...  1.38 us
  transfers between devices with their start and end apart: 19, of which 7 were waited for; matrix products, arithmetic and copies ran while one was open for 0% of the time, Pallas kernels for 9%

profile of v2, /device:TPU:0, one launch (start us, length us, event | category | flops | bytes accessed | tf_op | source)
XLA Modules:
  0.0 53.9 jit_solution(11547073609261082674)
XLA Ops:
  0.0 1.4 %pack.1 = (bf16[400,768]{1,0:T(8,128)(2,1)S(1)}, bf16[272,768]{1,0:T(8,128)(2,1)S(1)}, bf16[144,768]{1,0:T(8,128)(2,1)S(1)}) custom-call(bf16[384,768]{1,0:T(8,128)(2,1)} %emb_hbm.1, s32[384]{0:T(512)} %order_hbm.1), custom_call_target="tpu_custom_call" | custom-call | tf_op jit(solution)/shard_map/pack/pallas_call | solution.py:116
  1.4 3.1 %collective-permute-start.5 = (bf16[400,768]{1,0:T(8,128)(2,1)S(1)}, bf16[400,768]{1,0:T(8,128)(2,1)S(1)}, u32[]{:S(2)}, u32[]{:S(2)}) collective-permute-start(bf16[400,768]{1,0:T(8,128)(2,1)S(1)} %get-tuple-element.24.refs_0_.refs_3_.refs_1_.refs_5_), channel_id=1, source_target_pairs={{0,4},{1,5},{2,6},{3,7},{4,0},{5,1},{6,2},{7,3},{8,12},{9,13},{10,... | collective-permute-start | bytes 1843208 | tf_op jit(solution)/shard_map/ppermute | solution.py:259
  4.5 1.5 %collective-permute-start.4 = (bf16[400,768]{1,0:T(8,128)(2,1)S(1)}, bf16[400,768]{1,0:T(8,128)(2,1)S(1)}, u32[]{:S(2)}, u32[]{:S(2)}) collective-permute-start(bf16[400,768]{1,0:T(8,128)(2,1)S(1)} %get-tuple-element.24.refs_0_.refs_3_.refs_1_.refs_5_), channel_id=1, source_target_pairs={{0,2},{1,3},{2,0},{3,1},{4,6},{5,7},{6,4},{7,5},{8,10},{9,11},{10,... | collective-permute-start | bytes 1843208 | tf_op jit(solution)/shard_map/ppermute | solution.py:259
  5.9 1.6 %collective-permute-start.1 = (bf16[144,768]{1,0:T(8,128)(2,1)S(1)}, bf16[144,768]{1,0:T(8,128)(2,1)S(1)}, u32[]{:S(2)}, u32[]{:S(2)}) collective-permute-start(bf16[144,768]{1,0:T(8,128)(2,1)S(1)} %get-tuple-element.26), channel_id=1, source_target_pairs={{0,8},{1,9},{2,10},{3,11},{4,12},{5,13},{6,14},{7,15},{8,16},{9,17... | collective-permute-start | bytes 663560 | tf_op jit(solution)/shard_map/ppermute | solution.py:259
  7.5 1.6 %collective-permute-start = (bf16[272,768]{1,0:T(8,128)(2,1)S(1)}, bf16[272,768]{1,0:T(8,128)(2,1)S(1)}, u32[]{:S(2)}, u32[]{:S(2)}) collective-permute-start(bf16[272,768]{1,0:T(8,128)(2,1)S(1)} %get-tuple-element.25), channel_id=1, source_target_pairs={{0,8},{1,9},{2,10},{3,11},{4,12},{5,13},{6,14},{7,15},{8,16},{9,17... | collective-permute-start | bytes 1253384 | tf_op jit(solution)/shard_map/ppermute | solution.py:259
  9.1 9.2 %collective-permute-done.5.ref.refs_5_.refs_3_.refs_7_ = bf16[400,768]{1,0:T(8,128)(2,1)S(1)} collective-permute-done((bf16[400,768]{1,0:T(8,128)(2,1)S(1)}, bf16[400,768]{1,0:T(8,128)(2,1)S(1)}, u32[]{:S(2)}, u32[]{:S(2)}) %collective-permute-start.5) | collective-permute-done | bytes 614432 | tf_op jit(solution)/shard_map/ppermute | solution.py:259
  18.3 1.5 %collective-permute-done.4.ref.refs_4_.refs_2_.refs_6_ = bf16[400,768]{1,0:T(8,128)(2,1)S(1)} collective-permute-done((bf16[400,768]{1,0:T(8,128)(2,1)S(1)}, bf16[400,768]{1,0:T(8,128)(2,1)S(1)}, u32[]{:S(2)}, u32[]{:S(2)}) %collective-permute-start.4) | collective-permute-done | bytes 614432 | tf_op jit(solution)/shard_map/ppermute | solution.py:259
  19.8 0.0 collective-permute-start.9
  19.8 0.0 collective-permute-done.1.refs_2_
  19.8 0.9 %collective-permute-start.6 = (bf16[272,768]{1,0:T(8,128)(2,1)S(1)}, bf16[272,768]{1,0:T(8,128)(2,1)S(1)}, u32[]{:S(2)}, u32[]{:S(2)}) collective-permute-start(bf16[272,768]{1,0:T(8,128)(2,1)S(1)} %piece.2), channel_id=1, source_target_pairs={{0,4},{1,5},{2,6},{3,7},{4,0},{5,1},{6,2},{7,3},{8,12},{9,13},{10,... | collective-permute-start | bytes 1253384 | tf_op jit(solution)/shard_map/ppermute | solution.py:259
  20.7 3.9 %collective-permute-done.refs_1_ = bf16[272,768]{1,0:T(8,128)(2,1)S(1)} collective-permute-done((bf16[272,768]{1,0:T(8,128)(2,1)S(1)}, bf16[272,768]{1,0:T(8,128)(2,1)S(1)}, u32[]{:S(2)}, u32[]{:S(2)}) %collective-permute-start) | collective-permute-done | bytes 417824 | tf_op jit(solution)/shard_map/ppermute | solution.py:259
  24.6 0.5 collective-permute-start.7
  25.1 0.0 collective-permute-done.8.refs_6_.refs_4_.refs_10_
  25.1 1.6 %collective-permute-start.2 = (bf16[272,768]{1,0:T(8,128)(2,1)S(1)}, bf16[272,768]{1,0:T(8,128)(2,1)S(1)}, u32[]{:S(2)}, u32[]{:S(2)}) collective-permute-start(bf16[272,768]{1,0:T(8,128)(2,1)S(1)} %collective-permute-done.refs_1_), channel_id=1, source_target_pairs={{0,8},{1,9},{2,10},{3,11},{4,12},{5,13},{6,14},{7,15},{8,16},{9,17... | collective-permute-start | bytes 1253384 | tf_op jit(solution)/shard_map/ppermute | solution.py:259
  26.8 5.1 %collective-permute-done.6.refs_8_ = bf16[272,768]{1,0:T(8,128)(2,1)S(1)} collective-permute-done((bf16[272,768]{1,0:T(8,128)(2,1)S(1)}, bf16[272,768]{1,0:T(8,128)(2,1)S(1)}, u32[]{:S(2)}, u32[]{:S(2)}) %collective-permute-start.6) | collective-permute-done | bytes 417824 | tf_op jit(solution)/shard_map/ppermute | solution.py:259
  31.9 3.5 %collective-permute-start.3 = (bf16[144,768]{1,0:T(8,128)(2,1)S(1)}, bf16[144,768]{1,0:T(8,128)(2,1)S(1)}, u32[]{:S(2)}, u32[]{:S(2)}) collective-permute-start(bf16[144,768]{1,0:T(8,128)(2,1)S(1)} %collective-permute-done.1.refs_2_), channel_id=1, source_target_pairs={{0,8},{1,9},{2,10},{3,11},{4,12},{5,13},{6,14},{7,15},{8,16},{9,17... | collective-permute-start | bytes 663560 | tf_op jit(solution)/shard_map/ppermute | solution.py:259
  35.4 0.3 collective-permute-start.12
  35.7 0.0 collective-permute-done.9.refs_7_.refs_5_.refs_11_
  35.7 3.8 %shard_map.28 = (f32[1,384]{1,0:T(1,128)S(1)}, f32[1,384]{1,0:T(1,128)S(1)}, f32[3,384]{1,0:T(4,128)S(1)}, f32[3,384]{1,0:T(4,128)S(1)}) custom-call(bf16[400,768]{1,0:T(8,128)(2,1)S(1)} %get-tuple-element.24.refs_0_.refs_3_.refs_1_.refs_5_, bf16[272,768]{1,0:T(8,128)(2,1)S(1)} %collective-permute-done.refs_1_, ...), custom_call_target="tpu_custom_call" | custom-call | flops 2717908992 | bytes 4718592 | tf_op jit(solution)/shard_map/pallas_call | solution.py:233
  39.6 1.3 %shard_map.29 = (f32[1,256]{1,0:T(1,128)S(1)}, f32[3,384]{1,0:T(4,128)S(1)}, f32[3,384]{1,0:T(4,128)S(1)}) custom-call(bf16[272,768]{1,0:T(8,128)(2,1)S(1)} %collective-permute-done.2.refs_0_.refs_3_, bf16[400,768]{1,0:T(8,128)(2,1)S(1)} %get-tuple-element.24.refs_0_.refs_3_.refs_1_.refs_5_, ...), custom_call_target="tpu_custom_call" | custom-call | flops 905969664 | bytes 3932160 | tf_op jit(solution)/shard_map/pallas_call | solution.py:233
  40.8 0.0 collective-permute-done.12.refs_14_
  40.8 3.3 %shard_map.30 = (f32[1,384]{1,0:T(1,128)S(1)}, f32[1,384]{1,0:T(1,128)S(1)}, f32[1,384]{1,0:T(1,128)S(1)}, f32[4,384]{1,0:T(4,128)S(1)}, f32[4,384]{1,0:T(4,128)S(1)}) custom-call(bf16[400,768]{1,0:T(8,128)(2,1)S(1)} %get-tuple-element.24.refs_0_.refs_3_.refs_1_.refs_5_, bf16[272,768]{1,0:T(8,128)(2,1)S(1)} %collective-permute-done.refs_1_, ...), custom_call_target="tpu_custom_call" | custom-call | flops 1811939328 | bytes 6488064 | tf_op jit(solution)/shard_map/pallas_call | solution.py:233
  44.1 0.4 collective-permute-start.15
  44.5 0.8 %collective-permute-start.13 = (f32[1,384]{1,0:T(1,128)S(1)}, f32[1,384]{1,0:T(1,128)S(1)}, u32[]{:S(2)}, u32[]{:S(2)}) collective-permute-start(f32[1,384]{1,0:T(1,128)S(1)} %get-tuple-element.35), channel_id=1, source_target_pairs={{0,24},{1,25},{2,26},{3,27},{4,28},{5,29},{6,30},{7,31},{8,0},{9,1... | collective-permute-start | bytes 4616 | tf_op jit(solution)/shard_map/ppermute | solution.py:259
  45.3 1.4 %collective-permute-start.14 = (f32[1,384]{1,0:T(1,128)S(1)}, f32[1,384]{1,0:T(1,128)S(1)}, u32[]{:S(2)}, u32[]{:S(2)}) collective-permute-start(f32[1,384]{1,0:T(1,128)S(1)} %get-tuple-element.36), channel_id=1, source_target_pairs={{0,8},{1,9},{2,10},{3,11},{4,12},{5,13},{6,14},{7,15},{8,24},{9,25... | collective-permute-start | bytes 4616 | tf_op jit(solution)/shard_map/ppermute | solution.py:259
  46.7 1.6 %collective-permute-start.16 = (f32[1,384]{1,0:T(1,128)S(1)}, f32[1,384]{1,0:T(1,128)S(1)}, u32[]{:S(2)}, u32[]{:S(2)}) collective-permute-start(f32[1,384]{1,0:T(1,128)S(1)} %get-tuple-element.40), channel_id=1, source_target_pairs={{2,0},{3,1},{0,2},{1,3},{6,4},{7,5},{4,6},{5,7},{10,8},{11,9},{8,1... | collective-permute-start | bytes 4616 | tf_op jit(solution)/shard_map/ppermute | solution.py:259
  48.3 0.5 collective-permute-start.17
  48.8 1.5 %collective-permute-start.18 = (f32[1,384]{1,0:T(1,128)S(1)}, f32[1,384]{1,0:T(1,128)S(1)}, u32[]{:S(2)}, u32[]{:S(2)}) collective-permute-start(f32[1,384]{1,0:T(1,128)S(1)} %get-tuple-element.42), channel_id=1, source_target_pairs={{6,0},{7,1},{4,2},{5,3},{2,4},{3,5},{0,6},{1,7},{14,8},{15,9},{12,... | collective-permute-start | bytes 4616 | tf_op jit(solution)/shard_map/ppermute | solution.py:259
  50.3 0.1 collective-permute-done.16
  50.4 1.5 %collective-permute-done.17 = f32[1,384]{1,0:T(1,128)S(1)} collective-permute-done((f32[1,384]{1,0:T(1,128)S(1)}, f32[1,384]{1,0:T(1,128)S(1)}, u32[]{:S(2)}, u32[]{:S(2)}) %collective-permute-start.17) | collective-permute-done | bytes 1568 | tf_op jit(solution)/shard_map/ppermute | solution.py:259
  51.9 1.4 %collective-permute-done.18 = f32[1,384]{1,0:T(1,128)S(1)} collective-permute-done((f32[1,384]{1,0:T(1,128)S(1)}, f32[1,384]{1,0:T(1,128)S(1)}, u32[]{:S(2)}, u32[]{:S(2)}) %collective-permute-start.18) | collective-permute-done | bytes 1568 | tf_op jit(solution)/shard_map/ppermute | solution.py:259
  53.3 0.6 %maximum_reduce_fusion = f32[384]{0:T(512)} fusion(f32[1,384]{1,0:T(1,128)S(1)} %collective-permute-done.18, f32[1,384]{1,0:T(1,128)S(1)} %collective-permute-done.17, f32[1,384]{1,0:T(1,128)S(1)} %collective-permute-done.16, f32[1,384]{1,0:T(1,128)S(1)} %get-tuple-element.39, f32[1,384]{1,0:T(1,128)S(1)} %collective-permute-done.14, ...), kind=kLoop, calls=%fused_computation | loop fusion | flops 2688 | bytes 12288 | tf_op jit(solution)/shard_map/max | solution.py:306
  (14 shorter events, 0.1 us)
Async XLA Ops:
  1.4 16.9 %collective-permute-start.5 = (bf16[400,768]{1,0:T(8,128)(2,1)S(1)}, bf16[400,768]{1,0:T(8,128)(2,1)S(1)}, u32[]{:S(2)}, u32[]{:S(2)}) collective-permute-start(bf16[400,768]{1,0:T(8,128)(2,1)S(1)} %get-tuple-element.24.refs_0_.refs_3_.refs_1_.refs_5_), channel_id=1, source_target_pairs={{0,4},{1,5},{2,6},{3,7},{4,0},{5,1},{6,2},{7,3},{8,12},{9,13},{10,... | collective-permute-start | bytes 1843208 | tf_op jit(solution)/shard_map/ppermute | solution.py:259
  4.5 15.3 %collective-permute-start.4 = (bf16[400,768]{1,0:T(8,128)(2,1)S(1)}, bf16[400,768]{1,0:T(8,128)(2,1)S(1)}, u32[]{:S(2)}, u32[]{:S(2)}) collective-permute-start(bf16[400,768]{1,0:T(8,128)(2,1)S(1)} %get-tuple-element.24.refs_0_.refs_3_.refs_1_.refs_5_), channel_id=1, source_target_pairs={{0,2},{1,3},{2,0},{3,1},{4,6},{5,7},{6,4},{7,5},{8,10},{9,11},{10,... | collective-permute-start | bytes 1843208 | tf_op jit(solution)/shard_map/ppermute | solution.py:259
  5.9 19.2 %collective-permute-start.8 = (bf16[400,768]{1,0:T(8,128)(2,1)S(1)}, bf16[400,768]{1,0:T(8,128)(2,1)S(1)}, u32[]{:S(2)}, u32[]{:S(2)}) collective-permute-start(bf16[400,768]{1,0:T(8,128)(2,1)S(1)} %get-tuple-element.24.refs_0_.refs_3_.refs_1_.refs_5_), channel_id=1, source_target_pairs={{0,1},{1,0},{2,3},{3,2},{4,5},{5,4},{6,7},{7,6},{8,9},{9,8},{10,11... | collective-permute-start | bytes 1843208 | tf_op jit(solution)/shard_map/ppermute | solution.py:259
  5.9 13.9 %collective-permute-start.1 = (bf16[144,768]{1,0:T(8,128)(2,1)S(1)}, bf16[144,768]{1,0:T(8,128)(2,1)S(1)}, u32[]{:S(2)}, u32[]{:S(2)}) collective-permute-start(bf16[144,768]{1,0:T(8,128)(2,1)S(1)} %get-tuple-element.26), channel_id=1, source_target_pairs={{0,8},{1,9},{2,10},{3,11},{4,12},{5,13},{6,14},{7,15},{8,16},{9,17... | collective-permute-start | bytes 663560 | tf_op jit(solution)/shard_map/ppermute | solution.py:259
  7.5 17.1 %collective-permute-start = (bf16[272,768]{1,0:T(8,128)(2,1)S(1)}, bf16[272,768]{1,0:T(8,128)(2,1)S(1)}, u32[]{:S(2)}, u32[]{:S(2)}) collective-permute-start(bf16[272,768]{1,0:T(8,128)(2,1)S(1)} %get-tuple-element.25), channel_id=1, source_target_pairs={{0,8},{1,9},{2,10},{3,11},{4,12},{5,13},{6,14},{7,15},{8,16},{9,17... | collective-permute-start | bytes 1253384 | tf_op jit(solution)/shard_map/ppermute | solution.py:259
  18.3 17.1 %collective-permute-start.10 = (bf16[400,768]{1,0:T(8,128)(2,1)S(1)}, bf16[400,768]{1,0:T(8,128)(2,1)S(1)}, u32[]{:S(2)}, u32[]{:S(2)}) collective-permute-start(bf16[400,768]{1,0:T(8,128)(2,1)S(1)} %collective-permute-done.5.ref.refs_5_.refs_3_.refs_7_), channel_id=1, source_target_pairs={{0,1},{1,0},{2,3},{3,2},{4,5},{5,4},{6,7},{7,6},{8,9},{9,8},{10,11... | collective-permute-start | bytes 1843208 | tf_op jit(solution)/shard_map/ppermute | solution.py:259
  19.8 16.0 %collective-permute-start.9 = (bf16[400,768]{1,0:T(8,128)(2,1)S(1)}, bf16[400,768]{1,0:T(8,128)(2,1)S(1)}, u32[]{:S(2)}, u32[]{:S(2)}) collective-permute-start(bf16[400,768]{1,0:T(8,128)(2,1)S(1)} %collective-permute-done.4.ref.refs_4_.refs_2_.refs_6_), channel_id=1, source_target_pairs={{0,1},{1,0},{2,3},{3,2},{4,5},{5,4},{6,7},{7,6},{8,9},{9,8},{10,11... | collective-permute-start | bytes 1843208 | tf_op jit(solution)/shard_map/ppermute | solution.py:259
  19.8 12.1 %collective-permute-start.6 = (bf16[272,768]{1,0:T(8,128)(2,1)S(1)}, bf16[272,768]{1,0:T(8,128)(2,1)S(1)}, u32[]{:S(2)}, u32[]{:S(2)}) collective-permute-start(bf16[272,768]{1,0:T(8,128)(2,1)S(1)} %piece.2), channel_id=1, source_target_pairs={{0,4},{1,5},{2,6},{3,7},{4,0},{5,1},{6,2},{7,3},{8,12},{9,13},{10,... | collective-permute-start | bytes 1253384 | tf_op jit(solution)/shard_map/ppermute | solution.py:259
  24.6 7.3 %collective-permute-start.7 = (bf16[144,768]{1,0:T(8,128)(2,1)S(1)}, bf16[144,768]{1,0:T(8,128)(2,1)S(1)}, u32[]{:S(2)}, u32[]{:S(2)}) collective-permute-start(bf16[144,768]{1,0:T(8,128)(2,1)S(1)} %piece.3), channel_id=1, source_target_pairs={{0,2},{1,3},{2,0},{3,1},{4,6},{5,7},{6,4},{7,5},{8,10},{9,11},{10,... | collective-permute-start | bytes 663560 | tf_op jit(solution)/shard_map/ppermute | solution.py:259
  25.1 14.4 %collective-permute-start.2 = (bf16[272,768]{1,0:T(8,128)(2,1)S(1)}, bf16[272,768]{1,0:T(8,128)(2,1)S(1)}, u32[]{:S(2)}, u32[]{:S(2)}) collective-permute-start(bf16[272,768]{1,0:T(8,128)(2,1)S(1)} %collective-permute-done.refs_1_), channel_id=1, source_target_pairs={{0,8},{1,9},{2,10},{3,11},{4,12},{5,13},{6,14},{7,15},{8,16},{9,17... | collective-permute-start | bytes 1253384 | tf_op jit(solution)/shard_map/ppermute | solution.py:259
  31.9 8.9 %collective-permute-start.11 = (bf16[272,768]{1,0:T(8,128)(2,1)S(1)}, bf16[272,768]{1,0:T(8,128)(2,1)S(1)}, u32[]{:S(2)}, u32[]{:S(2)}) collective-permute-start(bf16[272,768]{1,0:T(8,128)(2,1)S(1)} %collective-permute-done.6.refs_8_), channel_id=1, source_target_pairs={{0,1},{1,0},{2,3},{3,2},{4,5},{5,4},{6,7},{7,6},{8,9},{9,8},{10,11... | collective-permute-start | bytes 1253384 | tf_op jit(solution)/shard_map/ppermute | solution.py:259
  31.9 8.9 %collective-permute-start.3 = (bf16[144,768]{1,0:T(8,128)(2,1)S(1)}, bf16[144,768]{1,0:T(8,128)(2,1)S(1)}, u32[]{:S(2)}, u32[]{:S(2)}) collective-permute-start(bf16[144,768]{1,0:T(8,128)(2,1)S(1)} %collective-permute-done.1.refs_2_), channel_id=1, source_target_pairs={{0,8},{1,9},{2,10},{3,11},{4,12},{5,13},{6,14},{7,15},{8,16},{9,17... | collective-permute-start | bytes 663560 | tf_op jit(solution)/shard_map/ppermute | solution.py:259
  35.4 5.4 %collective-permute-start.12 = (bf16[144,768]{1,0:T(8,128)(2,1)S(1)}, bf16[144,768]{1,0:T(8,128)(2,1)S(1)}, u32[]{:S(2)}, u32[]{:S(2)}) collective-permute-start(bf16[144,768]{1,0:T(8,128)(2,1)S(1)} %collective-permute-done.7.refs_9_), channel_id=1, source_target_pairs={{0,1},{1,0},{2,3},{3,2},{4,5},{5,4},{6,7},{7,6},{8,9},{9,8},{10,11... | collective-permute-start | bytes 663560 | tf_op jit(solution)/shard_map/ppermute | solution.py:259
  44.1 2.6 %collective-permute-start.15 = (f32[4,384]{1,0:T(4,128)S(1)}, f32[4,384]{1,0:T(4,128)S(1)}, u32[]{:S(2)}, u32[]{:S(2)}) collective-permute-start(f32[4,384]{1,0:T(4,128)S(1)} %get-tuple-element.38), channel_id=1, source_target_pairs={{0,1},{1,0},{2,3},{3,2},{4,5},{5,4},{6,7},{7,6},{8,9},{9,8},{10,11... | collective-permute-start | bytes 18440 | tf_op jit(solution)/shard_map/ppermute | solution.py:259
  44.5 5.8 %collective-permute-start.13 = (f32[1,384]{1,0:T(1,128)S(1)}, f32[1,384]{1,0:T(1,128)S(1)}, u32[]{:S(2)}, u32[]{:S(2)}) collective-permute-start(f32[1,384]{1,0:T(1,128)S(1)} %get-tuple-element.35), channel_id=1, source_target_pairs={{0,24},{1,25},{2,26},{3,27},{4,28},{5,29},{6,30},{7,31},{8,0},{9,1... | collective-permute-start | bytes 4616 | tf_op jit(solution)/shard_map/ppermute | solution.py:259
  45.3 5.0 %collective-permute-start.14 = (f32[1,384]{1,0:T(1,128)S(1)}, f32[1,384]{1,0:T(1,128)S(1)}, u32[]{:S(2)}, u32[]{:S(2)}) collective-permute-start(f32[1,384]{1,0:T(1,128)S(1)} %get-tuple-element.36), channel_id=1, source_target_pairs={{0,8},{1,9},{2,10},{3,11},{4,12},{5,13},{6,14},{7,15},{8,24},{9,25... | collective-permute-start | bytes 4616 | tf_op jit(solution)/shard_map/ppermute | solution.py:259
  46.7 3.6 %collective-permute-start.16 = (f32[1,384]{1,0:T(1,128)S(1)}, f32[1,384]{1,0:T(1,128)S(1)}, u32[]{:S(2)}, u32[]{:S(2)}) collective-permute-start(f32[1,384]{1,0:T(1,128)S(1)} %get-tuple-element.40), channel_id=1, source_target_pairs={{2,0},{3,1},{0,2},{1,3},{6,4},{7,5},{4,6},{5,7},{10,8},{11,9},{8,1... | collective-permute-start | bytes 4616 | tf_op jit(solution)/shard_map/ppermute | solution.py:259
  48.3 3.6 %collective-permute-start.17 = (f32[1,384]{1,0:T(1,128)S(1)}, f32[1,384]{1,0:T(1,128)S(1)}, u32[]{:S(2)}, u32[]{:S(2)}) collective-permute-start(f32[1,384]{1,0:T(1,128)S(1)} %get-tuple-element.41), channel_id=1, source_target_pairs={{4,0},{5,1},{6,2},{7,3},{0,4},{1,5},{2,6},{3,7},{12,8},{13,9},{14,... | collective-permute-start | bytes 4616 | tf_op jit(solution)/shard_map/ppermute | solution.py:259
  48.8 4.5 %collective-permute-start.18 = (f32[1,384]{1,0:T(1,128)S(1)}, f32[1,384]{1,0:T(1,128)S(1)}, u32[]{:S(2)}, u32[]{:S(2)}) collective-permute-start(f32[1,384]{1,0:T(1,128)S(1)} %get-tuple-element.42), channel_id=1, source_target_pairs={{6,0},{7,1},{4,2},{5,3},{2,4},{3,5},{0,6},{1,7},{14,8},{15,9},{12,... | collective-permute-start | bytes 4616 | tf_op jit(solution)/shard_map/ppermute | solution.py:259

commit v3 on v2

--- a/solution.py
+++ b/solution.py
@@ -143,33 +143,37 @@
     return jnp.where(order == 0.0, FAR, order)
 
 
-def match_body(plan, chips, known, *refs):
-    at = 0
-
-    def take(count):
-        nonlocal at
-        at += count
-        return refs[at - count : at]
-
-    side_cols = sum(chips)
-    rows, ours, twins = take(len(plan)), take(side_cols), take(side_cols)
-    row_in, col_in = list(take(sum(p[2] for p in plan))), take(2 * known.count(0))
-    row_out, col_out = take(1 + max(p[3] for p in plan)), take(2)
-    (col_acc,) = take(1)
+def match_body(tasks, groups, initial, final, n_blocks, *refs):
+    blocks, refs = refs[:n_blocks], refs[n_blocks:]
+    before, refs = (None, refs) if initial else (refs[:3], refs[3:])
+    row_out, col_out, col_acc = refs[:-3], refs[-3:-1], refs[-1]
     lanes = 128
-    firsts = [sum(chips[:k]) for k in range(len(chips) + 1)]
+
+    def result(row):
+        return (row_out[row], 0) if final else (row_out[0], row)
+
+    for side in range(2):
+        if initial:
+            col_out[side][...] = jnp.full(col_out[side].shape, -1.0, jnp.float32)
+        else:
+            col_out[side][...] = before[1 + side][...]
+    for k in range(len(row_out)):
+        if initial:
+            row_out[k][...] = jnp.full(row_out[k].shape, -1.0, jnp.float32)
+        else:
+            row_out[k][...] = before[0][k : k + 1, :] if final else before[0][...]
     fresh = set()
-    for r, (meets, counted, has_known, out, first_lane) in enumerate(plan):
-        n = rows[r].shape[0] - PAD
-        own_orders = lane_orders(rows[r])
+    for block, row, lane, counted, meets in tasks:
+        n = blocks[block].shape[0] - PAD
+        own_orders = lane_orders(blocks[block])
         own_order = jnp.broadcast_to(own_orders, (lanes, n)).T[:, 0:1]
         best = jnp.full((n, lanes), -1.0, jnp.float32)
-        for chip in meets:
-            blocks = [side[c] for side in (ours, twins) for c in range(firsts[chip], firsts[chip + 1])]
-            units = jnp.concatenate([ref[: ref.shape[0] - PAD, :] for ref in blocks], axis=0)
-            orders = jnp.concatenate([lane_orders(ref) for ref in blocks], axis=1)
+        for g in meets:
+            cols = [blocks[col[0]] for col in groups[g]]
+            units = jnp.concatenate([ref[: ref.shape[0] - PAD, :] for ref in cols], axis=0)
+            orders = jnp.concatenate([lane_orders(ref) for ref in cols], axis=1)
             score = lax.dot_general(
-                rows[r][:n, :], units, (((1,), (1,)), ((), ())), preferred_element_type=jnp.float32
+                blocks[block][:n, :], units, (((1,), (1,)), ((), ())), preferred_element_type=jnp.float32
             )
             for k in range(0, units.shape[0], lanes):
                 part = score[:, k : k + lanes]
@@ -177,61 +181,58 @@
                 best = jnp.maximum(best, jnp.where(earlier, part, -1.0))
                 if counted:
                     other = jnp.max(jnp.where(earlier, -1.0, part).reshape(n // 8, 8, lanes), axis=0)
-                    if chip in fresh:
-                        other = jnp.maximum(col_acc[chip, :, k : k + lanes], other)
-                    col_acc[chip, :, k : k + lanes] = other
+                    if g in fresh:
+                        other = jnp.maximum(col_acc[g, :, k : k + lanes], other)
+                    col_acc[g, :, k : k + lanes] = other
             if counted:
-                fresh.add(chip)
+                fresh.add(g)
         value = jnp.where(own_orders == FAR, -1.0, jnp.max(best.T, axis=0, keepdims=True))
-        if has_known:
-            value = jnp.maximum(value, row_in.pop(0)[0:1, first_lane : first_lane + n])
-        row_out[out][0:1, first_lane : first_lane + n] = value
-    for side in range(2):
-        before = [col_in[side * known.count(0) + i][k : k + 1, :] for i, k in zip(group_index(known), known)]
-        n = col_out[side].shape[1]
-        for chip in range(len(chips)):
-            value = jnp.max(col_acc[chip, :, side * n : (side + 1) * n], axis=0, keepdims=True)
-            if chip < len(before):
-                value = jnp.maximum(value, before[chip])
-            col_out[side][chip : chip + 1, :] = value
-
-
-def group_index(known):
-    groups = []
-    for k in known:
-        groups.append((groups[-1] if groups else -1) + (k == 0))
-    return groups
+        ref, at = result(row)
+        ref[at : at + 1, lane : lane + n] = jnp.maximum(ref[at : at + 1, lane : lane + n], value)
+    for g in sorted(fresh):
+        start = 0
+        for col, side, chip, lane in groups[g]:
+            n = blocks[col].shape[0] - PAD
+            value = jnp.max(col_acc[g, :, start : start + n], axis=0, keepdims=True)
+            ref = col_out[side]
+            ref[chip : chip + 1, lane : lane + n] = jnp.maximum(ref[chip : chip + 1, lane : lane + n], value)
+            start += n
 
 
 def in_vmem(values):
     return [pltpu.with_memory_space_constraint(v, pltpu.VMEM) for v in values]
 
 
-def match(rows, chips, col_in=()):
-    ours = [block for mine, _ in chips for block in mine]
-    twins = [block for _, other in chips for block in other]
-    width = rows[0][0].shape[1]
-    n = sum(block.shape[0] - PAD for block in chips[0][0])
-    sizes = [row[0].shape[0] - PAD for row in rows]
-    plan = [(tuple(meets), counted, value is not None, out, lane) for _, meets, counted, value, out, lane in rows]
-    totals = [max(p[4] + size for p, size in zip(plan, sizes) if p[3] == k) for k in range(1 + max(p[3] for p in plan))]
-    known = [k for pair in col_in for k in range(pair[0].shape[0])]
-    before = [pair[0] for pair in col_in] + [pair[1] for pair in col_in]
-    block = pltpu.VMEM((len(chips), n), jnp.float32)
-    call = pl.pallas_call(
-        functools.partial(match_body, plan, [len(mine) for mine, _ in chips], known),
-        out_shape=[pltpu.VMEM((1, total), jnp.float32) for total in totals] + [block, block],
-        scratch_shapes=[pltpu.VMEM((len(chips), 8, 2 * n), jnp.float32)],
-        cost_estimate=pl.CostEstimate(
-            flops=4 * sum(size * len(p[0]) for p, size in zip(plan, sizes)) * n * width,
-            bytes_accessed=2 * (sum(sizes) + 2 * len(chips) * n) * width,
-            transcendentals=0,
-        ),
+def match(state, tasks, shape, final=False):
+    blocks, groups, plan = [], [], []
+
+    def place(value, values):
+        for k, known in enumerate(values):
+            if known is value:
+                return k
+        values.append(value)
+        return len(values) - 1
+
+    for block, row, lane, counted, meets in tasks:
+        found = []
+        for group in meets:
+            group = [(place(col, blocks), *where) for col, *where in group]
+            if group not in groups:
+                groups.append(group)
+            found.append(groups.index(group))
+        plan.append((place(block, blocks), row, lane, counted, found))
+    rows, chips, n = shape
+    width = blocks[0].shape[1]
+    widest = max(sum(blocks[col[0]].shape[0] - PAD for col in group) for group in groups)
+    pairs = sum(blocks[p[0]].shape[0] * blocks[col[0]].shape[0] for p in plan for g in p[4] for col in groups[g])
+    best = [pltpu.VMEM((1, n), jnp.float32)] * rows if final else [pltpu.VMEM((rows, n), jnp.float32)]
+    return pl.pallas_call(
+        functools.partial(match_body, plan, groups, state is None, final, len(blocks)),
+        out_shape=best + [pltpu.VMEM((chips, n), jnp.float32)] * 2,
+        scratch_shapes=[pltpu.VMEM((len(groups), 8, widest), jnp.float32)],
+        cost_estimate=pl.CostEstimate(flops=2 * pairs * width, bytes_accessed=2 * len(blocks) * n * width, transcendentals=0),
         compiler_params=pltpu.CompilerParams(vmem_limit_bytes=VMEM_GRANT),
-    )
-    values = [row[3] for row in rows if row[3] is not None]
-    outs = call(*in_vmem([*(row[0] for row in rows), *ours, *twins, *values, *before]))
-    return outs[: len(totals)], tuple(outs[len(totals) :])
+    )(*in_vmem([*blocks, *(state or ())]))
 
 
 def merge_body(ours_ref, theirs_ref, *out_refs):
@@ -260,8 +261,9 @@
 
     def nearest(embeddings, doc_order):
         n = embeddings.shape[0]
-        last = min(n, 128)
-        pieces = ((0, n - last), (n - last, last)) if n > last else ((0, n),)
+        tile = 128
+        pieces = ((0, tile), (tile, n - tile))
+        corner_pieces = ((0, n - tile), (n - tile, tile))
         swap = layout.swap()
 
         own, *parts = pack(embeddings, doc_order, pieces)
@@ -274,25 +276,40 @@
         dy, dx = offsets[-1]
         routes = [((0, dx), (dy, 0)), ((dy, 0), (0, dx))]
         corner = []
-        for k, (start, rows) in enumerate(pieces):
+        for k, (start, rows) in enumerate(corner_pieces):
             have, move = routes[k % 2]
             block = piece(plane[offsets.index(have)], start, rows)
             corner.append(send(block, layout.plane_move(*move)))
-        near_chips = [([block], [send(block, swap)]) for block in [own, *plane]]
-        far_chip = (corner, [send(block, swap) for block in corner])
-
-        every = range(len(near_chips))
-        far = len(near_chips)
+        twins = [send(block, swap) for block in [own, *plane]]
+        corner_twins = [send(block, swap) for block in corner]
+
+        def by_two(blocks, side):
+            cols = [(block, side, k + 1, 0) for k, block in enumerate(blocks)]
+            return [cols[k : k + 2] for k in range(0, len(cols), 2)]
+
+        far = len(offsets)
+        own_cols = [[(own, 0, 0, 0), (twins[0], 1, 0, 0)]]
+        plane_cols, twin_cols = by_two(plane, 0), by_two(twins[1:], 1)
+        corner_cols = [[(block, 0, far, start) for block, (start, _) in zip(corner, corner_pieces)]]
+        ctwin_cols = [[(block, 1, far, start) for block, (start, _) in zip(corner_twins, corner_pieces)]]
+
         lanes = [start for start, _ in pieces]
-        first = [(own, False, 0, 0)]
-        first += [(block, True, k + 1, lane) for k, step in enumerate(line[:-1]) for block, lane in zip(step, lanes)]
-        half = [(block, True, len(line), lane) for block, lane in zip(line[-1], lanes)]
-        best, cols = match([(r[0], every, r[1], None, *r[2:]) for r in first], near_chips)
-        side, cols = match([(r[0], every, True, None, 0, r[3]) for r in half[:-1]], near_chips, [cols])
-        known = [*best, *side]
-        rows = [(r[0], [far], r[1], known[r[2]], *r[2:]) for r in first + half[:-1]]
-        rows.append((half[-1][0], [far, *every], True, None, *half[-1][2:]))
-        best, (ours, theirs) = match(rows, [*near_chips, far_chip], [cols])
+        mine = [(own, 0, 0, False)]
+        early = [(block, k + 1, at, True) for k, step in enumerate(line[:-1]) for block, at in zip(step, lanes)]
+        half_a, half_b = [(block, len(line), at, True) for block, at in zip(line[-1], lanes)]
+        shape = (len(line) + 1, far + 1, n)
+        state = match(None, [(*r, own_cols) for r in mine], shape)
+        if early:
+            state = match(state, [(*early[0], own_cols)], shape)
+        rows = [(*r, own_cols * (k > 0) + plane_cols) for k, r in enumerate(early)]
+        state = match(state, rows + [(*r, plane_cols) for r in mine], shape)
+        state = match(state, [(*r, twin_cols) for r in mine + early], shape)
+        near_cols = own_cols + plane_cols + twin_cols
+        state = match(state, [(*half_a, near_cols)], shape)
+        state = match(state, [(*r, corner_cols) for r in [*mine, *early, half_a]], shape)
+        state = match(state, [(*half_b, near_cols + corner_cols)], shape)
+        everyone = [*mine, *early, half_a, half_b]
+        *best, ours, theirs = match(state, [(*r, ctwin_cols) for r in everyone], shape, True)
 
         theirs = send(theirs, swap)
         back = [best[0]]

time: 54.1 us -> 56.5 us (1.044)
  waiting for transfers between devices: 22.7 us -> 25.5 us
  starting transfers between devices: 20.6 us -> 18.8 us
  Pallas kernels: 9.77 us -> 11.3 us
    ppermute x19, waiting for transfers between devices: 22.7 us -> 25.5 us  [send(): return lax.ppermute(value, AXES, pairs)]
    ppermute x19, starting transfers between devices: 20.6 us -> 18.8 us  [send(): return lax.ppermute(value, AXES, pairs)]
    pallas_call x3 -> x8, Pallas kernels: 8.34 us -> 9.86 us  [match(): pl.pallas_call(functools.partial(match_body, plan, groups, state is None,...]
  transfers between devices with their start and end apart: 19 -> 19, of which waited for: 7 -> 9; matrix products, arithmetic and copies ran while one was open for 0% -> 0% of each run, Pallas kernels for 9% -> 15%
where the time goes in v3:
time: 56.5 us; the launch traced here: 56.4 us
  waiting for transfers between devices  25.5 us (45%)
  starting transfers between devices  18.8 us (33%)
  Pallas kernels  11.3 us (20%)
  other arithmetic  0.6 us (1%)
    ppermute x19, waiting for transfers between devices, send(): return lax.ppermute(value, AXES, pairs)  25.5 us
    ppermute x19, starting transfers between devices, send(): return lax.ppermute(value, AXES, pairs)  18.8 us
    pallas_call x8, Pallas kernels, match(): pl.pallas_call(functools.partial(match_body, plan, groups, state is None,...  9.86 us
    pallas_call x1, Pallas kernels, pack(): call(*(pltpu.with_memory_space_constraint(v, pltpu.HBM) for v in (embeddi...  1.38 us
  transfers between devices with their start and end apart: 19, of which 9 were waited for; matrix products, arithmetic and copies ran while one was open for 0% of the time, Pallas kernels for 15%

profile of v3, /device:TPU:0, one launch (start us, length us, event | category | flops | bytes accessed | tf_op | source)
XLA Modules:
  0.0 56.4 jit_solution(15977663189230256268)
XLA Ops:
  0.0 1.4 %pack.1 = (bf16[400,768]{1,0:T(8,128)(2,1)S(1)}, bf16[144,768]{1,0:T(8,128)(2,1)S(1)}, bf16[272,768]{1,0:T(8,128)(2,1)S(1)}) custom-call(bf16[384,768]{1,0:T(8,128)(2,1)} %emb_hbm.1, s32[384]{0:T(512)} %order_hbm.1), custom_call_target="tpu_custom_call" | custom-call | tf_op jit(solution)/shard_map/pack/pallas_call | solution.py:116
  1.4 3.0 %collective-permute-start = (bf16[400,768]{1,0:T(8,128)(2,1)S(1)}, bf16[400,768]{1,0:T(8,128)(2,1)S(1)}, u32[]{:S(2)}, u32[]{:S(2)}) collective-permute-start(bf16[400,768]{1,0:T(8,128)(2,1)S(1)} %get-tuple-element.38.refs_0_.refs_3_.refs_2_), channel_id=1, source_target_pairs={{0,2},{1,3},{2,0},{3,1},{4,6},{5,7},{6,4},{7,5},{8,10},{9,11},{10,... | collective-permute-start | bytes 1843208 | tf_op jit(solution)/shard_map/ppermute | solution.py:260
  4.4 1.5 %collective-permute-start.3 = (bf16[400,768]{1,0:T(8,128)(2,1)S(1)}, bf16[400,768]{1,0:T(8,128)(2,1)S(1)}, u32[]{:S(2)}, u32[]{:S(2)}) collective-permute-start(bf16[400,768]{1,0:T(8,128)(2,1)S(1)} %get-tuple-element.38.refs_0_.refs_3_.refs_2_), channel_id=1, source_target_pairs={{0,4},{1,5},{2,6},{3,7},{4,0},{5,1},{6,2},{7,3},{8,12},{9,13},{10,... | collective-permute-start | bytes 1843208 | tf_op jit(solution)/shard_map/ppermute | solution.py:260
  5.9 1.6 %collective-permute-start.7 = (bf16[272,768]{1,0:T(8,128)(2,1)S(1)}, bf16[272,768]{1,0:T(8,128)(2,1)S(1)}, u32[]{:S(2)}, u32[]{:S(2)}) collective-permute-start(bf16[272,768]{1,0:T(8,128)(2,1)S(1)} %get-tuple-element.40), channel_id=1, source_target_pairs={{0,8},{1,9},{2,10},{3,11},{4,12},{5,13},{6,14},{7,15},{8,16},{9,17... | collective-permute-start | bytes 1253384 | tf_op jit(solution)/shard_map/ppermute | solution.py:260
  7.5 1.6 %collective-permute-start.6 = (bf16[144,768]{1,0:T(8,128)(2,1)S(1)}, bf16[144,768]{1,0:T(8,128)(2,1)S(1)}, u32[]{:S(2)}, u32[]{:S(2)}) collective-permute-start(bf16[144,768]{1,0:T(8,128)(2,1)S(1)} %get-tuple-element.39), channel_id=1, source_target_pairs={{0,8},{1,9},{2,10},{3,11},{4,12},{5,13},{6,14},{7,15},{8,16},{9,17... | collective-permute-start | bytes 663560 | tf_op jit(solution)/shard_map/ppermute | solution.py:260
  9.1 9.2 %collective-permute-done.ref.refs_0_.refs_2_ = bf16[400,768]{1,0:T(8,128)(2,1)S(1)} collective-permute-done((bf16[400,768]{1,0:T(8,128)(2,1)S(1)}, bf16[400,768]{1,0:T(8,128)(2,1)S(1)}, u32[]{:S(2)}, u32[]{:S(2)}) %collective-permute-start) | collective-permute-done | bytes 614432 | tf_op jit(solution)/shard_map/ppermute | solution.py:260
  18.3 1.5 %collective-permute-done.3.ref.refs_1_.refs_3_ = bf16[400,768]{1,0:T(8,128)(2,1)S(1)} collective-permute-done((bf16[400,768]{1,0:T(8,128)(2,1)S(1)}, bf16[400,768]{1,0:T(8,128)(2,1)S(1)}, u32[]{:S(2)}, u32[]{:S(2)}) %collective-permute-start.3) | collective-permute-done | bytes 614432 | tf_op jit(solution)/shard_map/ppermute | solution.py:260
  19.8 4.8 %collective-permute-done.6.refs_2_.refs_3_ = bf16[144,768]{1,0:T(8,128)(2,1)S(1)} collective-permute-done((bf16[144,768]{1,0:T(8,128)(2,1)S(1)}, bf16[144,768]{1,0:T(8,128)(2,1)S(1)}, u32[]{:S(2)}, u32[]{:S(2)}) %collective-permute-start.6) | collective-permute-done | bytes 221216 | tf_op jit(solution)/shard_map/ppermute | solution.py:260
  24.6 0.5 collective-permute-start.1
  25.1 0.6 %collective-permute-start.4 = (bf16[144,768]{1,0:T(8,128)(2,1)S(1)}, bf16[144,768]{1,0:T(8,128)(2,1)S(1)}, u32[]{:S(2)}, u32[]{:S(2)}) collective-permute-start(bf16[144,768]{1,0:T(8,128)(2,1)S(1)} %piece.3), channel_id=1, source_target_pairs={{0,2},{1,3},{2,0},{3,1},{4,6},{5,7},{6,4},{7,5},{8,10},{9,11},{10,... | collective-permute-start | bytes 663560 | tf_op jit(solution)/shard_map/ppermute | solution.py:260
  25.7 1.6 %collective-permute-start.9 = (bf16[272,768]{1,0:T(8,128)(2,1)S(1)}, bf16[272,768]{1,0:T(8,128)(2,1)S(1)}, u32[]{:S(2)}, u32[]{:S(2)}) collective-permute-start(bf16[272,768]{1,0:T(8,128)(2,1)S(1)} %collective-permute-done.7.refs_5_.refs_4_), channel_id=1, source_target_pairs={{0,8},{1,9},{2,10},{3,11},{4,12},{5,13},{6,14},{7,15},{8,16},{9,17... | collective-permute-start | bytes 1253384 | tf_op jit(solution)/shard_map/ppermute | solution.py:260
  27.4 0.8 %shard_map.28 = (f32[3,384]{1,0:T(4,128)S(1)}, f32[4,384]{1,0:T(4,128)S(1)}, f32[4,384]{1,0:T(4,128)S(1)}) custom-call(bf16[400,768]{1,0:T(8,128)(2,1)S(1)} %get-tuple-element.38.refs_0_.refs_3_.refs_2_, bf16[400,768]{1,0:T(8,128)(2,1)S(1)} %collective-permute-done.10.refs_1_.refs_4_), custom_call_target="tpu_custom_call" | custom-call | flops 491520000 | bytes 1179648 | tf_op jit(solution)/shard_map/pallas_call | solution.py:229
  28.2 3.8 %collective-permute-done.4.refs_1_.refs_7_ = bf16[144,768]{1,0:T(8,128)(2,1)S(1)} collective-permute-done((bf16[144,768]{1,0:T(8,128)(2,1)S(1)}, bf16[144,768]{1,0:T(8,128)(2,1)S(1)}, u32[]{:S(2)}, u32[]{:S(2)}) %collective-permute-start.4) | collective-permute-done | bytes 221216 | tf_op jit(solution)/shard_map/ppermute | solution.py:260
  32.0 1.6 %collective-permute-start.8 = (bf16[144,768]{1,0:T(8,128)(2,1)S(1)}, bf16[144,768]{1,0:T(8,128)(2,1)S(1)}, u32[]{:S(2)}, u32[]{:S(2)}) collective-permute-start(bf16[144,768]{1,0:T(8,128)(2,1)S(1)} %collective-permute-done.6.refs_2_.refs_3_), channel_id=1, source_target_pairs={{0,8},{1,9},{2,10},{3,11},{4,12},{5,13},{6,14},{7,15},{8,16},{9,17... | collective-permute-start | bytes 663560 | tf_op jit(solution)/shard_map/ppermute | solution.py:260
  33.5 0.6 %shard_map.29 = (f32[3,384]{1,0:T(4,128)S(1)}, f32[4,384]{1,0:T(4,128)S(1)}, f32[4,384]{1,0:T(4,128)S(1)}) custom-call(bf16[400,768]{1,0:T(8,128)(2,1)S(1)} %get-tuple-element.38.refs_0_.refs_3_.refs_2_, bf16[400,768]{1,0:T(8,128)(2,1)S(1)} %collective-permute-done.10.refs_1_.refs_4_, bf16[144,768]{1,0:T(8,128)(2,1)S(1)} %collective-permute-done.6.refs_2_.refs_3_, ...), custom_call_target="tpu_custom_call" | custom-call | flops 176947200 | bytes 1769472 | tf_op jit(solution)/shard_map/pallas_call | solution.py:229
  34.2 1.7 %collective-permute-done.1.refs_0_.refs_6_ = bf16[272,768]{1,0:T(8,128)(2,1)S(1)} collective-permute-done((bf16[272,768]{1,0:T(8,128)(2,1)S(1)}, bf16[272,768]{1,0:T(8,128)(2,1)S(1)}, u32[]{:S(2)}, u32[]{:S(2)}) %collective-permute-start.1) | collective-permute-done | bytes 417824 | tf_op jit(solution)/shard_map/ppermute | solution.py:260
  35.9 1.8 %shard_map.30 = (f32[3,384]{1,0:T(4,128)S(1)}, f32[4,384]{1,0:T(4,128)S(1)}, f32[4,384]{1,0:T(4,128)S(1)}) custom-call(bf16[400,768]{1,0:T(8,128)(2,1)S(1)} %collective-permute-done.ref.refs_0_.refs_2_, bf16[400,768]{1,0:T(8,128)(2,1)S(1)} %collective-permute-done.3.ref.refs_1_.refs_3_, bf16[144,768]{1,0:T(8,128)(2,1)S(1)} %collective-permute-done.6.refs_2_.refs_3_, ...), custom_call_target="tpu_custom_call" | custom-call | flops 1336934400 | bytes 3538944 | tf_op jit(solution)/shard_map/pallas_call | solution.py:229
  37.7 0.6 %collective-permute-start.5 = (bf16[144,768]{1,0:T(8,128)(2,1)S(1)}, bf16[144,768]{1,0:T(8,128)(2,1)S(1)}, u32[]{:S(2)}, u32[]{:S(2)}) collective-permute-start(bf16[144,768]{1,0:T(8,128)(2,1)S(1)} %collective-permute-done.4.refs_1_.refs_7_), channel_id=1, source_target_pairs={{0,1},{1,0},{2,3},{3,2},{4,5},{5,4},{6,7},{7,6},{8,9},{9,8},{10,11... | collective-permute-start | bytes 663560 | tf_op jit(solution)/shard_map/ppermute | solution.py:260
  38.2 1.4 %shard_map.31 = (f32[3,384]{1,0:T(4,128)S(1)}, f32[4,384]{1,0:T(4,128)S(1)}, f32[4,384]{1,0:T(4,128)S(1)}) custom-call(bf16[400,768]{1,0:T(8,128)(2,1)S(1)} %collective-permute-done.11.refs_0_.refs_4_, bf16[400,768]{1,0:T(8,128)(2,1)S(1)} %collective-permute-done.12.refs_1_.refs_5_, bf16[400,768]{1,0:T(8,128)(2,1)S(1)} %get-tuple-element.38.refs_0_.refs_3_.refs_2_, ...), custom_call_target="tpu_custom_call" | custom-call | flops 1002700800 | bytes 2949120 | tf_op jit(solution)/shard_map/pallas_call | solution.py:229
  39.6 0.8 %collective-permute-done.8.refs_6_.refs_5_ = bf16[144,768]{1,0:T(8,128)(2,1)S(1)} collective-permute-done((bf16[144,768]{1,0:T(8,128)(2,1)S(1)}, bf16[144,768]{1,0:T(8,128)(2,1)S(1)}, u32[]{:S(2)}, u32[]{:S(2)}) %collective-permute-start.8) | collective-permute-done | bytes 221216 | tf_op jit(solution)/shard_map/ppermute | solution.py:260
  40.5 1.4 %shard_map.32 = (f32[3,384]{1,0:T(4,128)S(1)}, f32[4,384]{1,0:T(4,128)S(1)}, f32[4,384]{1,0:T(4,128)S(1)}) custom-call(bf16[400,768]{1,0:T(8,128)(2,1)S(1)} %get-tuple-element.38.refs_0_.refs_3_.refs_2_, bf16[400,768]{1,0:T(8,128)(2,1)S(1)} %collective-permute-done.10.refs_1_.refs_4_, bf16[400,768]{1,0:T(8,128)(2,1)S(1)} %collective-permute-done.ref.refs_0_.refs_2_, ...), custom_call_target="tpu_custom_call" | custom-call | flops 530841600 | bytes 4128768 | tf_op jit(solution)/shard_map/pallas_call | solution.py:229
  41.9 1.1 %shard_map.33 = (f32[3,384]{1,0:T(4,128)S(1)}, f32[4,384]{1,0:T(4,128)S(1)}, f32[4,384]{1,0:T(4,128)S(1)}) custom-call(bf16[272,768]{1,0:T(8,128)(2,1)S(1)} %collective-permute-done.1.refs_0_.refs_6_, bf16[144,768]{1,0:T(8,128)(2,1)S(1)} %collective-permute-done.4.refs_1_.refs_7_, bf16[400,768]{1,0:T(8,128)(2,1)S(1)} %get-tuple-element.38.refs_0_.refs_3_.refs_2_, ...), custom_call_target="tpu_custom_call" | custom-call | flops 613416960 | bytes 3538944 | tf_op jit(solution)/shard_map/pallas_call | solution.py:229
  43.0 1.4 %shard_map.34 = (f32[3,384]{1,0:T(4,128)S(1)}, f32[4,384]{1,0:T(4,128)S(1)}, f32[4,384]{1,0:T(4,128)S(1)}) custom-call(bf16[400,768]{1,0:T(8,128)(2,1)S(1)} %get-tuple-element.38.refs_0_.refs_3_.refs_2_, bf16[400,768]{1,0:T(8,128)(2,1)S(1)} %collective-permute-done.10.refs_1_.refs_4_, bf16[400,768]{1,0:T(8,128)(2,1)S(1)} %collective-permute-done.ref.refs_0_.refs_2_, ...), custom_call_target="tpu_custom_call" | custom-call | flops 1176502272 | bytes 5308416 | tf_op jit(solution)/shard_map/pallas_call | solution.py:229
  44.4 1.3 %shard_map.35 = (f32[1,384]{1,0:T(1,128)S(1)}, f32[1,384]{1,0:T(1,128)S(1)}, f32[1,384]{1,0:T(1,128)S(1)}, f32[4,384]{1,0:T(4,128)S(1)}, f32[4,384]{1,0:T(4,128)S(1)}) custom-call(bf16[272,768]{1,0:T(8,128)(2,1)S(1)} %collective-permute-done.2.refs_0_, bf16[144,768]{1,0:T(8,128)(2,1)S(1)} %collective-permute-done.5.refs_1_, ...), custom_call_target="tpu_custom_call" | custom-call | flops 787218432 | bytes 4128768 | tf_op jit(solution)/shard_map/pallas_call | solution.py:229
  45.8 0.9 %collective-permute-start.13 = (f32[1,384]{1,0:T(1,128)S(1)}, f32[1,384]{1,0:T(1,128)S(1)}, u32[]{:S(2)}, u32[]{:S(2)}) collective-permute-start(f32[1,384]{1,0:T(1,128)S(1)} %get-tuple-element.63), channel_id=1, source_target_pairs={{0,24},{1,25},{2,26},{3,27},{4,28},{5,29},{6,30},{7,31},{8,0},{9,1... | collective-permute-start | bytes 4616 | tf_op jit(solution)/shard_map/ppermute | solution.py:260
  46.7 1.7 %collective-permute-start.14 = (f32[1,384]{1,0:T(1,128)S(1)}, f32[1,384]{1,0:T(1,128)S(1)}, u32[]{:S(2)}, u32[]{:S(2)}) collective-permute-start(f32[1,384]{1,0:T(1,128)S(1)} %get-tuple-element.64), channel_id=1, source_target_pairs={{0,8},{1,9},{2,10},{3,11},{4,12},{5,13},{6,14},{7,15},{8,24},{9,25... | collective-permute-start | bytes 4616 | tf_op jit(solution)/shard_map/ppermute | solution.py:260
  48.4 1.3 %collective-permute-start.16 = (f32[1,384]{1,0:T(1,128)S(1)}, f32[1,384]{1,0:T(1,128)S(1)}, u32[]{:S(2)}, u32[]{:S(2)}) collective-permute-start(f32[1,384]{1,0:T(1,128)S(1)} %get-tuple-element.68), channel_id=1, source_target_pairs={{2,0},{3,1},{0,2},{1,3},{6,4},{7,5},{4,6},{5,7},{10,8},{11,9},{8,1... | collective-permute-start | bytes 4616 | tf_op jit(solution)/shard_map/ppermute | solution.py:260
  49.8 1.5 %collective-permute-start.17 = (f32[1,384]{1,0:T(1,128)S(1)}, f32[1,384]{1,0:T(1,128)S(1)}, u32[]{:S(2)}, u32[]{:S(2)}) collective-permute-start(f32[1,384]{1,0:T(1,128)S(1)} %get-tuple-element.69), channel_id=1, source_target_pairs={{4,0},{5,1},{6,2},{7,3},{0,4},{1,5},{2,6},{3,7},{12,8},{13,9},{14,... | collective-permute-start | bytes 4616 | tf_op jit(solution)/shard_map/ppermute | solution.py:260
  51.3 0.7 %collective-permute-start.18 = (f32[1,384]{1,0:T(1,128)S(1)}, f32[1,384]{1,0:T(1,128)S(1)}, u32[]{:S(2)}, u32[]{:S(2)}) collective-permute-start(f32[1,384]{1,0:T(1,128)S(1)} %get-tuple-element.70), channel_id=1, source_target_pairs={{6,0},{7,1},{4,2},{5,3},{2,4},{3,5},{0,6},{1,7},{14,8},{15,9},{12,... | collective-permute-start | bytes 4616 | tf_op jit(solution)/shard_map/ppermute | solution.py:260
  52.1 1.3 %collective-permute-done.17 = f32[1,384]{1,0:T(1,128)S(1)} collective-permute-done((f32[1,384]{1,0:T(1,128)S(1)}, f32[1,384]{1,0:T(1,128)S(1)}, u32[]{:S(2)}, u32[]{:S(2)}) %collective-permute-start.17) | collective-permute-done | bytes 1568 | tf_op jit(solution)/shard_map/ppermute | solution.py:260
  53.3 2.4 %collective-permute-done.18 = f32[1,384]{1,0:T(1,128)S(1)} collective-permute-done((f32[1,384]{1,0:T(1,128)S(1)}, f32[1,384]{1,0:T(1,128)S(1)}, u32[]{:S(2)}, u32[]{:S(2)}) %collective-permute-start.18) | collective-permute-done | bytes 1568 | tf_op jit(solution)/shard_map/ppermute | solution.py:260
  55.8 0.6 %maximum_reduce_fusion = f32[384]{0:T(512)} fusion(f32[1,384]{1,0:T(1,128)S(1)} %collective-permute-done.18, f32[1,384]{1,0:T(1,128)S(1)} %collective-permute-done.17, f32[1,384]{1,0:T(1,128)S(1)} %collective-permute-done.16, f32[1,384]{1,0:T(1,128)S(1)} %get-tuple-element.67, f32[1,384]{1,0:T(1,128)S(1)} %collective-permute-done.14, ...), kind=kLoop, calls=%fused_computation | loop fusion | flops 2688 | bytes 12288 | tf_op jit(solution)/shard_map/max | solution.py:323
  (19 shorter events, 0.2 us)
Async XLA Ops:
  1.4 16.9 %collective-permute-start = (bf16[400,768]{1,0:T(8,128)(2,1)S(1)}, bf16[400,768]{1,0:T(8,128)(2,1)S(1)}, u32[]{:S(2)}, u32[]{:S(2)}) collective-permute-start(bf16[400,768]{1,0:T(8,128)(2,1)S(1)} %get-tuple-element.38.refs_0_.refs_3_.refs_2_), channel_id=1, source_target_pairs={{0,2},{1,3},{2,0},{3,1},{4,6},{5,7},{6,4},{7,5},{8,10},{9,11},{10,... | collective-permute-start | bytes 1843208 | tf_op jit(solution)/shard_map/ppermute | solution.py:260
  4.4 15.3 %collective-permute-start.3 = (bf16[400,768]{1,0:T(8,128)(2,1)S(1)}, bf16[400,768]{1,0:T(8,128)(2,1)S(1)}, u32[]{:S(2)}, u32[]{:S(2)}) collective-permute-start(bf16[400,768]{1,0:T(8,128)(2,1)S(1)} %get-tuple-element.38.refs_0_.refs_3_.refs_2_), channel_id=1, source_target_pairs={{0,4},{1,5},{2,6},{3,7},{4,0},{5,1},{6,2},{7,3},{8,12},{9,13},{10,... | collective-permute-start | bytes 1843208 | tf_op jit(solution)/shard_map/ppermute | solution.py:260
  5.9 19.8 %collective-permute-start.10 = (bf16[400,768]{1,0:T(8,128)(2,1)S(1)}, bf16[400,768]{1,0:T(8,128)(2,1)S(1)}, u32[]{:S(2)}, u32[]{:S(2)}) collective-permute-start(bf16[400,768]{1,0:T(8,128)(2,1)S(1)} %get-tuple-element.38.refs_0_.refs_3_.refs_2_), channel_id=1, source_target_pairs={{0,1},{1,0},{2,3},{3,2},{4,5},{5,4},{6,7},{7,6},{8,9},{9,8},{10,11... | collective-permute-start | bytes 1843208 | tf_op jit(solution)/shard_map/ppermute | solution.py:260
  5.9 19.2 %collective-permute-start.7 = (bf16[272,768]{1,0:T(8,128)(2,1)S(1)}, bf16[272,768]{1,0:T(8,128)(2,1)S(1)}, u32[]{:S(2)}, u32[]{:S(2)}) collective-permute-start(bf16[272,768]{1,0:T(8,128)(2,1)S(1)} %get-tuple-element.40), channel_id=1, source_target_pairs={{0,8},{1,9},{2,10},{3,11},{4,12},{5,13},{6,14},{7,15},{8,16},{9,17... | collective-permute-start | bytes 1253384 | tf_op jit(solution)/shard_map/ppermute | solution.py:260
  7.5 17.1 %collective-permute-start.6 = (bf16[144,768]{1,0:T(8,128)(2,1)S(1)}, bf16[144,768]{1,0:T(8,128)(2,1)S(1)}, u32[]{:S(2)}, u32[]{:S(2)}) collective-permute-start(bf16[144,768]{1,0:T(8,128)(2,1)S(1)} %get-tuple-element.39), channel_id=1, source_target_pairs={{0,8},{1,9},{2,10},{3,11},{4,12},{5,13},{6,14},{7,15},{8,16},{9,17... | collective-permute-start | bytes 663560 | tf_op jit(solution)/shard_map/ppermute | solution.py:260
  18.3 19.4 %collective-permute-start.11 = (bf16[400,768]{1,0:T(8,128)(2,1)S(1)}, bf16[400,768]{1,0:T(8,128)(2,1)S(1)}, u32[]{:S(2)}, u32[]{:S(2)}) collective-permute-start(bf16[400,768]{1,0:T(8,128)(2,1)S(1)} %collective-permute-done.ref.refs_0_.refs_2_), channel_id=1, source_target_pairs={{0,1},{1,0},{2,3},{3,2},{4,5},{5,4},{6,7},{7,6},{8,9},{9,8},{10,11... | collective-permute-start | bytes 1843208 | tf_op jit(solution)/shard_map/ppermute | solution.py:260
  19.7 18.5 %collective-permute-start.12 = (bf16[400,768]{1,0:T(8,128)(2,1)S(1)}, bf16[400,768]{1,0:T(8,128)(2,1)S(1)}, u32[]{:S(2)}, u32[]{:S(2)}) collective-permute-start(bf16[400,768]{1,0:T(8,128)(2,1)S(1)} %collective-permute-done.3.ref.refs_1_.refs_3_), channel_id=1, source_target_pairs={{0,1},{1,0},{2,3},{3,2},{4,5},{5,4},{6,7},{7,6},{8,9},{9,8},{10,11... | collective-permute-start | bytes 1843208 | tf_op jit(solution)/shard_map/ppermute | solution.py:260
  24.6 11.3 %collective-permute-start.1 = (bf16[272,768]{1,0:T(8,128)(2,1)S(1)}, bf16[272,768]{1,0:T(8,128)(2,1)S(1)}, u32[]{:S(2)}, u32[]{:S(2)}) collective-permute-start(bf16[272,768]{1,0:T(8,128)(2,1)S(1)} %piece.2), channel_id=1, source_target_pairs={{0,4},{1,5},{2,6},{3,7},{4,0},{5,1},{6,2},{7,3},{8,12},{9,13},{10,... | collective-permute-start | bytes 1253384 | tf_op jit(solution)/shard_map/ppermute | solution.py:260
  25.1 6.8 %collective-permute-start.4 = (bf16[144,768]{1,0:T(8,128)(2,1)S(1)}, bf16[144,768]{1,0:T(8,128)(2,1)S(1)}, u32[]{:S(2)}, u32[]{:S(2)}) collective-permute-start(bf16[144,768]{1,0:T(8,128)(2,1)S(1)} %piece.3), channel_id=1, source_target_pairs={{0,2},{1,3},{2,0},{3,1},{4,6},{5,7},{6,4},{7,5},{8,10},{9,11},{10,... | collective-permute-start | bytes 663560 | tf_op jit(solution)/shard_map/ppermute | solution.py:260
  25.7 17.2 %collective-permute-start.9 = (bf16[272,768]{1,0:T(8,128)(2,1)S(1)}, bf16[272,768]{1,0:T(8,128)(2,1)S(1)}, u32[]{:S(2)}, u32[]{:S(2)}) collective-permute-start(bf16[272,768]{1,0:T(8,128)(2,1)S(1)} %collective-permute-done.7.refs_5_.refs_4_), channel_id=1, source_target_pairs={{0,8},{1,9},{2,10},{3,11},{4,12},{5,13},{6,14},{7,15},{8,16},{9,17... | collective-permute-start | bytes 1253384 | tf_op jit(solution)/shard_map/ppermute | solution.py:260
  32.0 8.5 %collective-permute-start.8 = (bf16[144,768]{1,0:T(8,128)(2,1)S(1)}, bf16[144,768]{1,0:T(8,128)(2,1)S(1)}, u32[]{:S(2)}, u32[]{:S(2)}) collective-permute-start(bf16[144,768]{1,0:T(8,128)(2,1)S(1)} %collective-permute-done.6.refs_2_.refs_3_), channel_id=1, source_target_pairs={{0,8},{1,9},{2,10},{3,11},{4,12},{5,13},{6,14},{7,15},{8,16},{9,17... | collective-permute-start | bytes 663560 | tf_op jit(solution)/shard_map/ppermute | solution.py:260
  35.9 8.6 %collective-permute-start.2 = (bf16[272,768]{1,0:T(8,128)(2,1)S(1)}, bf16[272,768]{1,0:T(8,128)(2,1)S(1)}, u32[]{:S(2)}, u32[]{:S(2)}) collective-permute-start(bf16[272,768]{1,0:T(8,128)(2,1)S(1)} %collective-permute-done.1.refs_0_.refs_6_), channel_id=1, source_target_pairs={{0,1},{1,0},{2,3},{3,2},{4,5},{5,4},{6,7},{7,6},{8,9},{9,8},{10,11... | collective-permute-start | bytes 1253384 | tf_op jit(solution)/shard_map/ppermute | solution.py:260
  37.7 6.7 %collective-permute-start.5 = (bf16[144,768]{1,0:T(8,128)(2,1)S(1)}, bf16[144,768]{1,0:T(8,128)(2,1)S(1)}, u32[]{:S(2)}, u32[]{:S(2)}) collective-permute-start(bf16[144,768]{1,0:T(8,128)(2,1)S(1)} %collective-permute-done.4.refs_1_.refs_7_), channel_id=1, source_target_pairs={{0,1},{1,0},{2,3},{3,2},{4,5},{5,4},{6,7},{7,6},{8,9},{9,8},{10,11... | collective-permute-start | bytes 663560 | tf_op jit(solution)/shard_map/ppermute | solution.py:260
  45.7 2.7 %collective-permute-start.15 = (f32[4,384]{1,0:T(4,128)S(1)}, f32[4,384]{1,0:T(4,128)S(1)}, u32[]{:S(2)}, u32[]{:S(2)}) collective-permute-start(f32[4,384]{1,0:T(4,128)S(1)} %get-tuple-element.66), channel_id=1, source_target_pairs={{0,1},{1,0},{2,3},{3,2},{4,5},{5,4},{6,7},{7,6},{8,9},{9,8},{10,11... | collective-permute-start | bytes 18440 | tf_op jit(solution)/shard_map/ppermute | solution.py:260
  45.8 6.2 %collective-permute-start.13 = (f32[1,384]{1,0:T(1,128)S(1)}, f32[1,384]{1,0:T(1,128)S(1)}, u32[]{:S(2)}, u32[]{:S(2)}) collective-permute-start(f32[1,384]{1,0:T(1,128)S(1)} %get-tuple-element.63), channel_id=1, source_target_pairs={{0,24},{1,25},{2,26},{3,27},{4,28},{5,29},{6,30},{7,31},{8,0},{9,1... | collective-permute-start | bytes 4616 | tf_op jit(solution)/shard_map/ppermute | solution.py:260
  46.7 5.2 %collective-permute-start.14 = (f32[1,384]{1,0:T(1,128)S(1)}, f32[1,384]{1,0:T(1,128)S(1)}, u32[]{:S(2)}, u32[]{:S(2)}) collective-permute-start(f32[1,384]{1,0:T(1,128)S(1)} %get-tuple-element.64), channel_id=1, source_target_pairs={{0,8},{1,9},{2,10},{3,11},{4,12},{5,13},{6,14},{7,15},{8,24},{9,25... | collective-permute-start | bytes 4616 | tf_op jit(solution)/shard_map/ppermute | solution.py:260
  48.4 3.6 %collective-permute-start.16 = (f32[1,384]{1,0:T(1,128)S(1)}, f32[1,384]{1,0:T(1,128)S(1)}, u32[]{:S(2)}, u32[]{:S(2)}) collective-permute-start(f32[1,384]{1,0:T(1,128)S(1)} %get-tuple-element.68), channel_id=1, source_target_pairs={{2,0},{3,1},{0,2},{1,3},{6,4},{7,5},{4,6},{5,7},{10,8},{11,9},{8,1... | collective-permute-start | bytes 4616 | tf_op jit(solution)/shard_map/ppermute | solution.py:260
  49.8 3.6 %collective-permute-start.17 = (f32[1,384]{1,0:T(1,128)S(1)}, f32[1,384]{1,0:T(1,128)S(1)}, u32[]{:S(2)}, u32[]{:S(2)}) collective-permute-start(f32[1,384]{1,0:T(1,128)S(1)} %get-tuple-element.69), channel_id=1, source_target_pairs={{4,0},{5,1},{6,2},{7,3},{0,4},{1,5},{2,6},{3,7},{12,8},{13,9},{14,... | collective-permute-start | bytes 4616 | tf_op jit(solution)/shard_map/ppermute | solution.py:260
  51.3 4.5 %collective-permute-start.18 = (f32[1,384]{1,0:T(1,128)S(1)}, f32[1,384]{1,0:T(1,128)S(1)}, u32[]{:S(2)}, u32[]{:S(2)}) collective-permute-start(f32[1,384]{1,0:T(1,128)S(1)} %get-tuple-element.70), channel_id=1, source_target_pairs={{6,0},{7,1},{4,2},{5,3},{2,4},{3,5},{0,6},{1,7},{14,8},{15,9},{12,... | collective-permute-start | bytes 4616 | tf_op jit(solution)/shard_map/ppermute | solution.py:260

commit v4 on v3

--- a/solution.py
+++ b/solution.py
@@ -143,52 +143,50 @@
     return jnp.where(order == 0.0, FAR, order)
 
 
-def match_body(tasks, groups, initial, final, n_blocks, *refs):
+def match_body(tasks, groups, n_blocks, n_rows, initial, *refs):
     blocks, refs = refs[:n_blocks], refs[n_blocks:]
-    before, refs = (None, refs) if initial else (refs[:3], refs[3:])
-    row_out, col_out, col_acc = refs[:-3], refs[-3:-1], refs[-1]
+    before, after, col_acc = refs[: len(refs) - n_rows - 3], refs[-n_rows - 3 : -1], refs[-1]
+    row_out, col_out = after[:n_rows], after[n_rows:]
     lanes = 128
-
-    def result(row):
-        return (row_out[row], 0) if final else (row_out[0], row)
-
-    for side in range(2):
-        if initial:
-            col_out[side][...] = jnp.full(col_out[side].shape, -1.0, jnp.float32)
-        else:
-            col_out[side][...] = before[1 + side][...]
-    for k in range(len(row_out)):
-        if initial:
-            row_out[k][...] = jnp.full(row_out[k].shape, -1.0, jnp.float32)
-        else:
-            row_out[k][...] = before[0][k : k + 1, :] if final else before[0][...]
+    for k, ref in enumerate(after):
+        ref[...] = jnp.full(ref.shape, -1.0, jnp.float32) if initial else before[k][...]
+
+    def units_of(numbers):
+        parts = [blocks[k][: blocks[k].shape[0] - PAD, :] for k in numbers]
+        return parts[0] if len(parts) == 1 else jnp.concatenate(parts, axis=0)
+
     fresh = set()
-    for block, row, lane, counted, meets in tasks:
-        n = blocks[block].shape[0] - PAD
-        own_orders = lane_orders(blocks[block])
-        own_order = jnp.broadcast_to(own_orders, (lanes, n)).T[:, 0:1]
-        best = jnp.full((n, lanes), -1.0, jnp.float32)
+    for rows, meets in tasks:
+        row_units = units_of([row[0] for row in rows])
+        sizes = [blocks[row[0]].shape[0] - PAD for row in rows]
+        row_orders = [lane_orders(blocks[row[0]]) for row in rows]
+        columns = [jnp.broadcast_to(orders, (lanes, n)).T[:, 0:1] for orders, n in zip(row_orders, sizes)]
+        best = [jnp.full((n, lanes), -1.0, jnp.float32) for n in sizes]
         for g in meets:
-            cols = [blocks[col[0]] for col in groups[g]]
-            units = jnp.concatenate([ref[: ref.shape[0] - PAD, :] for ref in cols], axis=0)
-            orders = jnp.concatenate([lane_orders(ref) for ref in cols], axis=1)
+            numbers = [col[0] for col in groups[g]]
+            orders = jnp.concatenate([lane_orders(blocks[k]) for k in numbers], axis=1)
             score = lax.dot_general(
-                blocks[block][:n, :], units, (((1,), (1,)), ((), ())), preferred_element_type=jnp.float32
+                row_units, units_of(numbers), (((1,), (1,)), ((), ())), preferred_element_type=jnp.float32
             )
-            for k in range(0, units.shape[0], lanes):
-                part = score[:, k : k + lanes]
-                earlier = orders[:, k : k + lanes] < own_order
-                best = jnp.maximum(best, jnp.where(earlier, part, -1.0))
-                if counted:
-                    other = jnp.max(jnp.where(earlier, -1.0, part).reshape(n // 8, 8, lanes), axis=0)
-                    if g in fresh:
-                        other = jnp.maximum(col_acc[g, :, k : k + lanes], other)
-                    col_acc[g, :, k : k + lanes] = other
-            if counted:
+            for k in range(0, score.shape[1], lanes):
+                first = 0
+                kept = [col_acc[g, :, k : k + lanes]] if g in fresh else []
+                for r, (_, _, _, counted) in enumerate(rows):
+                    n = sizes[r]
+                    part = score[first : first + n, k : k + lanes]
+                    earlier = orders[:, k : k + lanes] < columns[r]
+                    best[r] = jnp.maximum(best[r], jnp.where(earlier, part, -1.0))
+                    if counted:
+                        kept.append(jnp.max(jnp.where(earlier, -1.0, part).reshape(n // 8, 8, lanes), axis=0))
+                    first += n
+                if any(row[3] for row in rows):
+                    col_acc[g, :, k : k + lanes] = functools.reduce(jnp.maximum, kept)
+            if any(row[3] for row in rows):
                 fresh.add(g)
-        value = jnp.where(own_orders == FAR, -1.0, jnp.max(best.T, axis=0, keepdims=True))
-        ref, at = result(row)
-        ref[at : at + 1, lane : lane + n] = jnp.maximum(ref[at : at + 1, lane : lane + n], value)
+        for r, (_, row, lane, _) in enumerate(rows):
+            value = jnp.where(row_orders[r] == FAR, -1.0, jnp.max(best[r].T, axis=0, keepdims=True))
+            at = slice(lane, lane + sizes[r])
+            row_out[row][:, at] = jnp.maximum(row_out[row][:, at], value)
     for g in sorted(fresh):
         start = 0
         for col, side, chip, lane in groups[g]:
@@ -203,32 +201,31 @@
     return [pltpu.with_memory_space_constraint(v, pltpu.VMEM) for v in values]
 
 
-def match(state, tasks, shape, final=False):
+def match(state, tasks, shape):
     blocks, groups, plan = [], [], []
 
-    def place(value, values):
-        for k, known in enumerate(values):
+    def place(value):
+        for k, known in enumerate(blocks):
             if known is value:
                 return k
-        values.append(value)
-        return len(values) - 1
-
-    for block, row, lane, counted, meets in tasks:
+        blocks.append(value)
+        return len(blocks) - 1
+
+    for rows, meets in tasks:
         found = []
         for group in meets:
-            group = [(place(col, blocks), *where) for col, *where in group]
+            group = [(place(col), *where) for col, *where in group]
             if group not in groups:
                 groups.append(group)
             found.append(groups.index(group))
-        plan.append((place(block, blocks), row, lane, counted, found))
+        plan.append(([(place(row), *where) for row, *where in rows], found))
     rows, chips, n = shape
     width = blocks[0].shape[1]
     widest = max(sum(blocks[col[0]].shape[0] - PAD for col in group) for group in groups)
-    pairs = sum(blocks[p[0]].shape[0] * blocks[col[0]].shape[0] for p in plan for g in p[4] for col in groups[g])
-    best = [pltpu.VMEM((1, n), jnp.float32)] * rows if final else [pltpu.VMEM((rows, n), jnp.float32)]
+    pairs = sum(blocks[r[0]].shape[0] * blocks[col[0]].shape[0] for p in plan for r in p[0] for g in p[1] for col in groups[g])
     return pl.pallas_call(
-        functools.partial(match_body, plan, groups, state is None, final, len(blocks)),
-        out_shape=best + [pltpu.VMEM((chips, n), jnp.float32)] * 2,
+        functools.partial(match_body, plan, groups, len(blocks), rows, state is None),
+        out_shape=[pltpu.VMEM((1, n), jnp.float32)] * rows + [pltpu.VMEM((chips, n), jnp.float32)] * 2,
         scratch_shapes=[pltpu.VMEM((len(groups), 8, widest), jnp.float32)],
         cost_estimate=pl.CostEstimate(flops=2 * pairs * width, bytes_accessed=2 * len(blocks) * n * width, transcendentals=0),
         compiler_params=pltpu.CompilerParams(vmem_limit_bytes=VMEM_GRANT),
@@ -298,18 +295,19 @@
         early = [(block, k + 1, at, True) for k, step in enumerate(line[:-1]) for block, at in zip(step, lanes)]
         half_a, half_b = [(block, len(line), at, True) for block, at in zip(line[-1], lanes)]
         shape = (len(line) + 1, far + 1, n)
-        state = match(None, [(*r, own_cols) for r in mine], shape)
+        near_cols = own_cols + plane_cols + twin_cols
+        state = match(None, [(mine, own_cols)], shape)
         if early:
-            state = match(state, [(*early[0], own_cols)], shape)
-        rows = [(*r, own_cols * (k > 0) + plane_cols) for k, r in enumerate(early)]
-        state = match(state, rows + [(*r, plane_cols) for r in mine], shape)
-        state = match(state, [(*r, twin_cols) for r in mine + early], shape)
-        near_cols = own_cols + plane_cols + twin_cols
-        state = match(state, [(*half_a, near_cols)], shape)
-        state = match(state, [(*r, corner_cols) for r in [*mine, *early, half_a]], shape)
-        state = match(state, [(*half_b, near_cols + corner_cols)], shape)
-        everyone = [*mine, *early, half_a, half_b]
-        *best, ours, theirs = match(state, [(*r, ctwin_cols) for r in everyone], shape, True)
+            state = match(state, [(early[:1], own_cols)], shape)
+        rest = [(early[1:], own_cols)] if early else []
+        state = match(state, rest + [(mine + early, plane_cols)], shape)
+        state = match(state, [(mine + early, twin_cols)], shape)
+        state = match(state, [([half_a], near_cols)], shape)
+        state = match(state, [([*mine, *early, half_a], corner_cols)], shape)
+        state = match(state, [([*mine, *early, half_a], ctwin_cols)], shape)
+        best = list(state[: len(line)])
+        *_, late, ours, theirs = match(state, [([half_b], near_cols + corner_cols + ctwin_cols)], shape)
+        best.append(late)
 
         theirs = send(theirs, swap)
         back = [best[0]]

time: 56.5 us -> 64.9 us (1.15)
  starting transfers between devices: 18.8 us -> 23.6 us
  waiting for transfers between devices: 25.5 us -> 29.1 us
    ppermute x19, starting transfers between devices: 18.8 us -> 23.6 us  [send(): return lax.ppermute(value, AXES, pairs)]
    ppermute x19, waiting for transfers between devices: 25.5 us -> 29.1 us  [send(): return lax.ppermute(value, AXES, pairs)]
  transfers between devices with their start and end apart: 19 -> 19, of which waited for: 9 -> 7; matrix products, arithmetic and copies ran while one was open for 0% -> 0% of each run, Pallas kernels for 15% -> 12%
where the time goes in v4:
time: 64.9 us; the launch traced here: 64.8 us
  waiting for transfers between devices  29.1 us (45%)
  starting transfers between devices  23.6 us (36%)
  Pallas kernels  11.3 us (17%)
    ppermute x19, waiting for transfers between devices, send(): return lax.ppermute(value, AXES, pairs)  29.1 us
    ppermute x19, starting transfers between devices, send(): return lax.ppermute(value, AXES, pairs)  23.6 us
    pallas_call x8, Pallas kernels, match(): pl.pallas_call(functools.partial(match_body, plan, groups, len(blocks), r...  9.82 us
    pallas_call x1, Pallas kernels, pack(): call(*(pltpu.with_memory_space_constraint(v, pltpu.HBM) for v in (embeddi...  1.38 us
  transfers between devices with their start and end apart: 19, of which 7 were waited for; matrix products, arithmetic and copies ran while one was open for 0% of the time, Pallas kernels for 12%

profile of v4, /device:TPU:0, one launch (start us, length us, event | category | flops | bytes accessed | tf_op | source)
XLA Modules:
  0.0 64.8 jit_solution(6777248018587873741)
XLA Ops:
  0.0 1.4 %pack.1 = (bf16[400,768]{1,0:T(8,128)(2,1)S(1)}, bf16[144,768]{1,0:T(8,128)(2,1)S(1)}, bf16[272,768]{1,0:T(8,128)(2,1)S(1)}) custom-call(bf16[384,768]{1,0:T(8,128)(2,1)} %emb_hbm.1, s32[384]{0:T(512)} %order_hbm.1), custom_call_target="tpu_custom_call" | custom-call | tf_op jit(solution)/shard_map/pack/pallas_call | solution.py:116
  1.4 3.0 %collective-permute-start = (bf16[400,768]{1,0:T(8,128)(2,1)S(1)}, bf16[400,768]{1,0:T(8,128)(2,1)S(1)}, u32[]{:S(2)}, u32[]{:S(2)}) collective-permute-start(bf16[400,768]{1,0:T(8,128)(2,1)S(1)} %get-tuple-element.50.refs_0_.refs_2_), channel_id=1, source_target_pairs={{0,2},{1,3},{2,0},{3,1},{4,6},{5,7},{6,4},{7,5},{8,10},{9,11},{10,... | collective-permute-start | bytes 1843208 | tf_op jit(solution)/shard_map/ppermute | solution.py:257
  4.4 1.5 %collective-permute-start.3 = (bf16[400,768]{1,0:T(8,128)(2,1)S(1)}, bf16[400,768]{1,0:T(8,128)(2,1)S(1)}, u32[]{:S(2)}, u32[]{:S(2)}) collective-permute-start(bf16[400,768]{1,0:T(8,128)(2,1)S(1)} %get-tuple-element.50.refs_0_.refs_2_), channel_id=1, source_target_pairs={{0,4},{1,5},{2,6},{3,7},{4,0},{5,1},{6,2},{7,3},{8,12},{9,13},{10,... | collective-permute-start | bytes 1843208 | tf_op jit(solution)/shard_map/ppermute | solution.py:257
  5.9 1.6 %collective-permute-start.6 = (bf16[144,768]{1,0:T(8,128)(2,1)S(1)}, bf16[144,768]{1,0:T(8,128)(2,1)S(1)}, u32[]{:S(2)}, u32[]{:S(2)}) collective-permute-start(bf16[144,768]{1,0:T(8,128)(2,1)S(1)} %get-tuple-element.51), channel_id=1, source_target_pairs={{0,8},{1,9},{2,10},{3,11},{4,12},{5,13},{6,14},{7,15},{8,16},{9,17... | collective-permute-start | bytes 663560 | tf_op jit(solution)/shard_map/ppermute | solution.py:257
  7.5 1.6 %collective-permute-start.7 = (bf16[272,768]{1,0:T(8,128)(2,1)S(1)}, bf16[272,768]{1,0:T(8,128)(2,1)S(1)}, u32[]{:S(2)}, u32[]{:S(2)}) collective-permute-start(bf16[272,768]{1,0:T(8,128)(2,1)S(1)} %get-tuple-element.52), channel_id=1, source_target_pairs={{0,8},{1,9},{2,10},{3,11},{4,12},{5,13},{6,14},{7,15},{8,16},{9,17... | collective-permute-start | bytes 1253384 | tf_op jit(solution)/shard_map/ppermute | solution.py:257
  9.1 9.2 %collective-permute-done.ref.refs_3_.refs_2_ = bf16[400,768]{1,0:T(8,128)(2,1)S(1)} collective-permute-done((bf16[400,768]{1,0:T(8,128)(2,1)S(1)}, bf16[400,768]{1,0:T(8,128)(2,1)S(1)}, u32[]{:S(2)}, u32[]{:S(2)}) %collective-permute-start) | collective-permute-done | bytes 614432 | tf_op jit(solution)/shard_map/ppermute | solution.py:257
  18.3 1.8 %collective-permute-start.1 = (bf16[272,768]{1,0:T(8,128)(2,1)S(1)}, bf16[272,768]{1,0:T(8,128)(2,1)S(1)}, u32[]{:S(2)}, u32[]{:S(2)}) collective-permute-start(bf16[272,768]{1,0:T(8,128)(2,1)S(1)} %piece.2), channel_id=1, source_target_pairs={{0,4},{1,5},{2,6},{3,7},{4,0},{5,1},{6,2},{7,3},{8,12},{9,13},{10,... | collective-permute-start | bytes 1253384 | tf_op jit(solution)/shard_map/ppermute | solution.py:257
  20.2 0.2 collective-permute-start.11
  20.4 3.0 %collective-permute-done.7.refs_2_.refs_4_ = bf16[272,768]{1,0:T(8,128)(2,1)S(1)} collective-permute-done((bf16[272,768]{1,0:T(8,128)(2,1)S(1)}, bf16[272,768]{1,0:T(8,128)(2,1)S(1)}, u32[]{:S(2)}, u32[]{:S(2)}) %collective-permute-start.7) | collective-permute-done | bytes 417824 | tf_op jit(solution)/shard_map/ppermute | solution.py:257
  23.4 0.5 collective-permute-start.4
  23.9 6.6 %collective-permute-done.1.refs_0_.refs_6_ = bf16[272,768]{1,0:T(8,128)(2,1)S(1)} collective-permute-done((bf16[272,768]{1,0:T(8,128)(2,1)S(1)}, bf16[272,768]{1,0:T(8,128)(2,1)S(1)}, u32[]{:S(2)}, u32[]{:S(2)}) %collective-permute-start.1) | collective-permute-done | bytes 417824 | tf_op jit(solution)/shard_map/ppermute | solution.py:257
  30.5 0.0 collective-permute-start.2
  30.5 3.7 %collective-permute-start.13 = (bf16[272,768]{1,0:T(8,128)(2,1)S(1)}, bf16[272,768]{1,0:T(8,128)(2,1)S(1)}, u32[]{:S(2)}, u32[]{:S(2)}) collective-permute-start(bf16[272,768]{1,0:T(8,128)(2,1)S(1)} %collective-permute-done.7.refs_2_.refs_4_), channel_id=1, source_target_pairs={{0,8},{1,9},{2,10},{3,11},{4,12},{5,13},{6,14},{7,15},{8,16},{9,17... | collective-permute-start | bytes 1253384 | tf_op jit(solution)/shard_map/ppermute | solution.py:257
  34.2 0.8 %shard_map.28 = (f32[1,384]{1,0:T(1,128)S(1)}, f32[1,384]{1,0:T(1,128)S(1)}, f32[1,384]{1,0:T(1,128)S(1)}, f32[4,384]{1,0:T(4,128)S(1)}, f32[4,384]{1,0:T(4,128)S(1)}) custom-call(bf16[400,768]{1,0:T(8,128)(2,1)S(1)} %get-tuple-element.50.refs_0_.refs_2_, bf16[400,768]{1,0:T(8,128)(2,1)S(1)} %collective-permute-done.9.refs_1_), custom_call_target="tpu_custom_call" | custom-call | flops 491520000 | bytes 1179648 | tf_op jit(solution)/shard_map/pallas_call | solution.py:226
  35.0 3.5 %collective-permute-start.8 = (bf16[144,768]{1,0:T(8,128)(2,1)S(1)}, bf16[144,768]{1,0:T(8,128)(2,1)S(1)}, u32[]{:S(2)}, u32[]{:S(2)}) collective-permute-start(bf16[144,768]{1,0:T(8,128)(2,1)S(1)} %collective-permute-done.6.refs_2_.refs_5_.refs_3_), channel_id=1, source_target_pairs={{0,8},{1,9},{2,10},{3,11},{4,12},{5,13},{6,14},{7,15},{8,16},{9,17... | collective-permute-start | bytes 663560 | tf_op jit(solution)/shard_map/ppermute | solution.py:257
  38.5 0.6 shard_map.29
  39.2 0.1 collective-permute-start.5
  39.2 1.6 %shard_map.30 = (f32[1,384]{1,0:T(1,128)S(1)}, f32[1,384]{1,0:T(1,128)S(1)}, f32[1,384]{1,0:T(1,128)S(1)}, f32[4,384]{1,0:T(4,128)S(1)}, f32[4,384]{1,0:T(4,128)S(1)}) custom-call(bf16[400,768]{1,0:T(8,128)(2,1)S(1)} %get-tuple-element.50.refs_0_.refs_2_, bf16[400,768]{1,0:T(8,128)(2,1)S(1)} %collective-permute-done.9.refs_1_, ...), custom_call_target="tpu_custom_call" | custom-call | flops 1336934400 | bytes 3538944 | tf_op jit(solution)/shard_map/pallas_call | solution.py:226
  40.8 1.2 %shard_map.31 = (f32[1,384]{1,0:T(1,128)S(1)}, f32[1,384]{1,0:T(1,128)S(1)}, f32[1,384]{1,0:T(1,128)S(1)}, f32[4,384]{1,0:T(4,128)S(1)}, f32[4,384]{1,0:T(4,128)S(1)}) custom-call(bf16[400,768]{1,0:T(8,128)(2,1)S(1)} %collective-permute-done.10.refs_0_.refs_4_, bf16[400,768]{1,0:T(8,128)(2,1)S(1)} %collective-permute-done.11.refs_1_.refs_5_, ...), custom_call_target="tpu_custom_call" | custom-call | flops 1002700800 | bytes 2949120 | tf_op jit(solution)/shard_map/pallas_call | solution.py:226
  42.1 6.4 %collective-permute-done.8.refs_6_.refs_5_ = bf16[144,768]{1,0:T(8,128)(2,1)S(1)} collective-permute-done((bf16[144,768]{1,0:T(8,128)(2,1)S(1)}, bf16[144,768]{1,0:T(8,128)(2,1)S(1)}, u32[]{:S(2)}, u32[]{:S(2)}) %collective-permute-start.8) | collective-permute-done | bytes 221216 | tf_op jit(solution)/shard_map/ppermute | solution.py:257
  48.5 1.4 %shard_map.32 = (f32[1,384]{1,0:T(1,128)S(1)}, f32[1,384]{1,0:T(1,128)S(1)}, f32[1,384]{1,0:T(1,128)S(1)}, f32[4,384]{1,0:T(4,128)S(1)}, f32[4,384]{1,0:T(4,128)S(1)}) custom-call(bf16[400,768]{1,0:T(8,128)(2,1)S(1)} %get-tuple-element.50.refs_0_.refs_2_, bf16[400,768]{1,0:T(8,128)(2,1)S(1)} %collective-permute-done.9.refs_1_, ...), custom_call_target="tpu_custom_call" | custom-call | flops 530841600 | bytes 4128768 | tf_op jit(solution)/shard_map/pallas_call | solution.py:226
  49.9 1.0 %shard_map.33 = (f32[1,384]{1,0:T(1,128)S(1)}, f32[1,384]{1,0:T(1,128)S(1)}, f32[1,384]{1,0:T(1,128)S(1)}, f32[4,384]{1,0:T(4,128)S(1)}, f32[4,384]{1,0:T(4,128)S(1)}) custom-call(bf16[272,768]{1,0:T(8,128)(2,1)S(1)} %collective-permute-done.1.refs_0_.refs_6_, bf16[144,768]{1,0:T(8,128)(2,1)S(1)} %collective-permute-done.4.refs_1_.refs_7_, ...), custom_call_target="tpu_custom_call" | custom-call | flops 613416960 | bytes 3538944 | tf_op jit(solution)/shard_map/pallas_call | solution.py:226
  50.9 1.0 %shard_map.34 = (f32[1,384]{1,0:T(1,128)S(1)}, f32[1,384]{1,0:T(1,128)S(1)}, f32[1,384]{1,0:T(1,128)S(1)}, f32[4,384]{1,0:T(4,128)S(1)}, f32[4,384]{1,0:T(4,128)S(1)}) custom-call(bf16[272,768]{1,0:T(8,128)(2,1)S(1)} %collective-permute-done.2.refs_0_.refs_8_, bf16[144,768]{1,0:T(8,128)(2,1)S(1)} %collective-permute-done.5.refs_1_.refs_9_, ...), custom_call_target="tpu_custom_call" | custom-call | flops 613416960 | bytes 3538944 | tf_op jit(solution)/shard_map/pallas_call | solution.py:226
  51.9 2.2 %shard_map.35 = (f32[1,384]{1,0:T(1,128)}, f32[1,384]{1,0:T(1,128)}, f32[1,384]{1,0:T(1,128)S(1)}, f32[4,384]{1,0:T(4,128)S(1)}, f32[4,384]{1,0:T(4,128)S(1)}) custom-call(bf16[400,768]{1,0:T(8,128)(2,1)S(1)} %get-tuple-element.50.refs_0_.refs_2_, bf16[400,768]{1,0:T(8,128)(2,1)S(1)} %collective-permute-done.9.refs_1_, ...), custom_call_target="tpu_custom_call" | custom-call | flops 1350303744 | bytes 6488064 | tf_op jit(solution)/shard_map/pallas_call | solution.py:226
  54.1 2.5 %collective-permute-start.14 = (f32[1,384]{1,0:T(1,128)S(1)}, f32[1,384]{1,0:T(1,128)S(1)}, u32[]{:S(2)}, u32[]{:S(2)}) collective-permute-start(f32[1,384]{1,0:T(1,128)S(1)} %get-tuple-element.88), channel_id=1, source_target_pairs={{0,8},{1,9},{2,10},{3,11},{4,12},{5,13},{6,14},{7,15},{8,24},{9,25... | collective-permute-start | bytes 4616 | tf_op jit(solution)/shard_map/ppermute | solution.py:257
  56.6 1.6 %collective-permute-start.16 = (f32[1,384]{1,0:T(1,128)S(1)}, f32[1,384]{1,0:T(1,128)S(1)}, u32[]{:S(2)}, u32[]{:S(2)}) collective-permute-start(f32[1,384]{1,0:T(1,128)S(1)} %get-tuple-element.92), channel_id=1, source_target_pairs={{2,0},{3,1},{0,2},{1,3},{6,4},{7,5},{4,6},{5,7},{10,8},{11,9},{8,1... | collective-permute-start | bytes 4616 | tf_op jit(solution)/shard_map/ppermute | solution.py:257
  58.2 1.5 %collective-permute-start.17 = (f32[1,384]{1,0:T(1,128)S(1)}, f32[1,384]{1,0:T(1,128)S(1)}, u32[]{:S(2)}, u32[]{:S(2)}) collective-permute-start(f32[1,384]{1,0:T(1,128)S(1)} %get-tuple-element.93), channel_id=1, source_target_pairs={{4,0},{5,1},{6,2},{7,3},{0,4},{1,5},{2,6},{3,7},{12,8},{13,9},{14,... | collective-permute-start | bytes 4616 | tf_op jit(solution)/shard_map/ppermute | solution.py:257
  59.7 0.5 collective-permute-start.18
  60.2 0.1 collective-permute-done.16
  60.2 1.5 %collective-permute-done.17 = f32[1,384]{1,0:T(1,128)S(1)} collective-permute-done((f32[1,384]{1,0:T(1,128)S(1)}, f32[1,384]{1,0:T(1,128)S(1)}, u32[]{:S(2)}, u32[]{:S(2)}) %collective-permute-start.17) | collective-permute-done | bytes 1568 | tf_op jit(solution)/shard_map/ppermute | solution.py:257
  61.7 2.4 %collective-permute-done.18 = f32[1,384]{1,0:T(1,128)S(1)} collective-permute-done((f32[1,384]{1,0:T(1,128)S(1)}, f32[1,384]{1,0:T(1,128)S(1)}, u32[]{:S(2)}, u32[]{:S(2)}) %collective-permute-start.18) | collective-permute-done | bytes 1568 | tf_op jit(solution)/shard_map/ppermute | solution.py:257
  64.2 0.6 maximum_reduce_fusion
  (19 shorter events, 0.1 us)
Async XLA Ops:
  1.4 16.9 %collective-permute-start = (bf16[400,768]{1,0:T(8,128)(2,1)S(1)}, bf16[400,768]{1,0:T(8,128)(2,1)S(1)}, u32[]{:S(2)}, u32[]{:S(2)}) collective-permute-start(bf16[400,768]{1,0:T(8,128)(2,1)S(1)} %get-tuple-element.50.refs_0_.refs_2_), channel_id=1, source_target_pairs={{0,2},{1,3},{2,0},{3,1},{4,6},{5,7},{6,4},{7,5},{8,10},{9,11},{10,... | collective-permute-start | bytes 1843208 | tf_op jit(solution)/shard_map/ppermute | solution.py:257
  4.4 15.7 %collective-permute-start.3 = (bf16[400,768]{1,0:T(8,128)(2,1)S(1)}, bf16[400,768]{1,0:T(8,128)(2,1)S(1)}, u32[]{:S(2)}, u32[]{:S(2)}) collective-permute-start(bf16[400,768]{1,0:T(8,128)(2,1)S(1)} %get-tuple-element.50.refs_0_.refs_2_), channel_id=1, source_target_pairs={{0,4},{1,5},{2,6},{3,7},{4,0},{5,1},{6,2},{7,3},{8,12},{9,13},{10,... | collective-permute-start | bytes 1843208 | tf_op jit(solution)/shard_map/ppermute | solution.py:257
  5.9 12.4 %collective-permute-start.6 = (bf16[144,768]{1,0:T(8,128)(2,1)S(1)}, bf16[144,768]{1,0:T(8,128)(2,1)S(1)}, u32[]{:S(2)}, u32[]{:S(2)}) collective-permute-start(bf16[144,768]{1,0:T(8,128)(2,1)S(1)} %get-tuple-element.51), channel_id=1, source_target_pairs={{0,8},{1,9},{2,10},{3,11},{4,12},{5,13},{6,14},{7,15},{8,16},{9,17... | collective-permute-start | bytes 663560 | tf_op jit(solution)/shard_map/ppermute | solution.py:257
  7.5 23.0 %collective-permute-start.9 = (bf16[400,768]{1,0:T(8,128)(2,1)S(1)}, bf16[400,768]{1,0:T(8,128)(2,1)S(1)}, u32[]{:S(2)}, u32[]{:S(2)}) collective-permute-start(bf16[400,768]{1,0:T(8,128)(2,1)S(1)} %get-tuple-element.50.refs_0_.refs_2_), channel_id=1, source_target_pairs={{0,1},{1,0},{2,3},{3,2},{4,5},{5,4},{6,7},{7,6},{8,9},{9,8},{10,11... | collective-permute-start | bytes 1843208 | tf_op jit(solution)/shard_map/ppermute | solution.py:257
  7.5 15.8 %collective-permute-start.7 = (bf16[272,768]{1,0:T(8,128)(2,1)S(1)}, bf16[272,768]{1,0:T(8,128)(2,1)S(1)}, u32[]{:S(2)}, u32[]{:S(2)}) collective-permute-start(bf16[272,768]{1,0:T(8,128)(2,1)S(1)} %get-tuple-element.52), channel_id=1, source_target_pairs={{0,8},{1,9},{2,10},{3,11},{4,12},{5,13},{6,14},{7,15},{8,16},{9,17... | collective-permute-start | bytes 1253384 | tf_op jit(solution)/shard_map/ppermute | solution.py:257
  18.3 20.9 %collective-permute-start.10 = (bf16[400,768]{1,0:T(8,128)(2,1)S(1)}, bf16[400,768]{1,0:T(8,128)(2,1)S(1)}, u32[]{:S(2)}, u32[]{:S(2)}) collective-permute-start(bf16[400,768]{1,0:T(8,128)(2,1)S(1)} %collective-permute-done.ref.refs_3_.refs_2_), channel_id=1, source_target_pairs={{0,1},{1,0},{2,3},{3,2},{4,5},{5,4},{6,7},{7,6},{8,9},{9,8},{10,11... | collective-permute-start | bytes 1843208 | tf_op jit(solution)/shard_map/ppermute | solution.py:257
  18.3 12.1 %collective-permute-start.1 = (bf16[272,768]{1,0:T(8,128)(2,1)S(1)}, bf16[272,768]{1,0:T(8,128)(2,1)S(1)}, u32[]{:S(2)}, u32[]{:S(2)}) collective-permute-start(bf16[272,768]{1,0:T(8,128)(2,1)S(1)} %piece.2), channel_id=1, source_target_pairs={{0,4},{1,5},{2,6},{3,7},{4,0},{5,1},{6,2},{7,3},{8,12},{9,13},{10,... | collective-permute-start | bytes 1253384 | tf_op jit(solution)/shard_map/ppermute | solution.py:257
  20.2 20.6 %collective-permute-start.11 = (bf16[400,768]{1,0:T(8,128)(2,1)S(1)}, bf16[400,768]{1,0:T(8,128)(2,1)S(1)}, u32[]{:S(2)}, u32[]{:S(2)}) collective-permute-start(bf16[400,768]{1,0:T(8,128)(2,1)S(1)} %collective-permute-done.3.ref.refs_4_.refs_3_), channel_id=1, source_target_pairs={{0,1},{1,0},{2,3},{3,2},{4,5},{5,4},{6,7},{7,6},{8,9},{9,8},{10,11... | collective-permute-start | bytes 1843208 | tf_op jit(solution)/shard_map/ppermute | solution.py:257
  23.4 11.7 %collective-permute-start.4 = (bf16[144,768]{1,0:T(8,128)(2,1)S(1)}, bf16[144,768]{1,0:T(8,128)(2,1)S(1)}, u32[]{:S(2)}, u32[]{:S(2)}) collective-permute-start(bf16[144,768]{1,0:T(8,128)(2,1)S(1)} %piece.3), channel_id=1, source_target_pairs={{0,2},{1,3},{2,0},{3,1},{4,6},{5,7},{6,4},{7,5},{8,10},{9,11},{10,... | collective-permute-start | bytes 663560 | tf_op jit(solution)/shard_map/ppermute | solution.py:257
  30.5 20.4 %collective-permute-start.2 = (bf16[272,768]{1,0:T(8,128)(2,1)S(1)}, bf16[272,768]{1,0:T(8,128)(2,1)S(1)}, u32[]{:S(2)}, u32[]{:S(2)}) collective-permute-start(bf16[272,768]{1,0:T(8,128)(2,1)S(1)} %collective-permute-done.1.refs_0_.refs_6_), channel_id=1, source_target_pairs={{0,1},{1,0},{2,3},{3,2},{4,5},{5,4},{6,7},{7,6},{8,9},{9,8},{10,11... | collective-permute-start | bytes 1253384 | tf_op jit(solution)/shard_map/ppermute | solution.py:257
  30.5 21.4 %collective-permute-start.13 = (bf16[272,768]{1,0:T(8,128)(2,1)S(1)}, bf16[272,768]{1,0:T(8,128)(2,1)S(1)}, u32[]{:S(2)}, u32[]{:S(2)}) collective-permute-start(bf16[272,768]{1,0:T(8,128)(2,1)S(1)} %collective-permute-done.7.refs_2_.refs_4_), channel_id=1, source_target_pairs={{0,8},{1,9},{2,10},{3,11},{4,12},{5,13},{6,14},{7,15},{8,16},{9,17... | collective-permute-start | bytes 1253384 | tf_op jit(solution)/shard_map/ppermute | solution.py:257
  35.0 13.4 %collective-permute-start.8 = (bf16[144,768]{1,0:T(8,128)(2,1)S(1)}, bf16[144,768]{1,0:T(8,128)(2,1)S(1)}, u32[]{:S(2)}, u32[]{:S(2)}) collective-permute-start(bf16[144,768]{1,0:T(8,128)(2,1)S(1)} %collective-permute-done.6.refs_2_.refs_5_.refs_3_), channel_id=1, source_target_pairs={{0,8},{1,9},{2,10},{3,11},{4,12},{5,13},{6,14},{7,15},{8,16},{9,17... | collective-permute-start | bytes 663560 | tf_op jit(solution)/shard_map/ppermute | solution.py:257
  39.2 11.7 %collective-permute-start.5 = (bf16[144,768]{1,0:T(8,128)(2,1)S(1)}, bf16[144,768]{1,0:T(8,128)(2,1)S(1)}, u32[]{:S(2)}, u32[]{:S(2)}) collective-permute-start(bf16[144,768]{1,0:T(8,128)(2,1)S(1)} %collective-permute-done.4.refs_1_.refs_7_), channel_id=1, source_target_pairs={{0,1},{1,0},{2,3},{3,2},{4,5},{5,4},{6,7},{7,6},{8,9},{9,8},{10,11... | collective-permute-start | bytes 663560 | tf_op jit(solution)/shard_map/ppermute | solution.py:257
  54.1 2.5 %collective-permute-start.15 = (f32[4,384]{1,0:T(4,128)S(1)}, f32[4,384]{1,0:T(4,128)S(1)}, u32[]{:S(2)}, u32[]{:S(2)}) collective-permute-start(f32[4,384]{1,0:T(4,128)S(1)} %get-tuple-element.90), channel_id=1, source_target_pairs={{0,1},{1,0},{2,3},{3,2},{4,5},{5,4},{6,7},{7,6},{8,9},{9,8},{10,11... | collective-permute-start | bytes 18440 | tf_op jit(solution)/shard_map/ppermute | solution.py:257
  54.1 6.1 %collective-permute-start.12 = (f32[1,384]{1,0:T(1,128)S(1)}, f32[1,384]{1,0:T(1,128)S(1)}, u32[]{:S(2)}, u32[]{:S(2)}) collective-permute-start(f32[1,384]{1,0:T(1,128)S(1)} %get-tuple-element.84.refs_12_), channel_id=1, source_target_pairs={{0,24},{1,25},{2,26},{3,27},{4,28},{5,29},{6,30},{7,31},{8,0},{9,1... | collective-permute-start | bytes 4616 | tf_op jit(solution)/shard_map/ppermute | solution.py:257
  54.1 6.1 %collective-permute-start.14 = (f32[1,384]{1,0:T(1,128)S(1)}, f32[1,384]{1,0:T(1,128)S(1)}, u32[]{:S(2)}, u32[]{:S(2)}) collective-permute-start(f32[1,384]{1,0:T(1,128)S(1)} %get-tuple-element.88), channel_id=1, source_target_pairs={{0,8},{1,9},{2,10},{3,11},{4,12},{5,13},{6,14},{7,15},{8,24},{9,25... | collective-permute-start | bytes 4616 | tf_op jit(solution)/shard_map/ppermute | solution.py:257
  56.6 3.6 %collective-permute-start.16 = (f32[1,384]{1,0:T(1,128)S(1)}, f32[1,384]{1,0:T(1,128)S(1)}, u32[]{:S(2)}, u32[]{:S(2)}) collective-permute-start(f32[1,384]{1,0:T(1,128)S(1)} %get-tuple-element.92), channel_id=1, source_target_pairs={{2,0},{3,1},{0,2},{1,3},{6,4},{7,5},{4,6},{5,7},{10,8},{11,9},{8,1... | collective-permute-start | bytes 4616 | tf_op jit(solution)/shard_map/ppermute | solution.py:257
  58.2 3.6 %collective-permute-start.17 = (f32[1,384]{1,0:T(1,128)S(1)}, f32[1,384]{1,0:T(1,128)S(1)}, u32[]{:S(2)}, u32[]{:S(2)}) collective-permute-start(f32[1,384]{1,0:T(1,128)S(1)} %get-tuple-element.93), channel_id=1, source_target_pairs={{4,0},{5,1},{6,2},{7,3},{0,4},{1,5},{2,6},{3,7},{12,8},{13,9},{14,... | collective-permute-start | bytes 4616 | tf_op jit(solution)/shard_map/ppermute | solution.py:257
  59.7 4.5 %collective-permute-start.18 = (f32[1,384]{1,0:T(1,128)S(1)}, f32[1,384]{1,0:T(1,128)S(1)}, u32[]{:S(2)}, u32[]{:S(2)}) collective-permute-start(f32[1,384]{1,0:T(1,128)S(1)} %get-tuple-element.94), channel_id=1, source_target_pairs={{6,0},{7,1},{4,2},{5,3},{2,4},{3,5},{0,6},{1,7},{14,8},{15,9},{12,... | collective-permute-start | bytes 4616 | tf_op jit(solution)/shard_map/ppermute | solution.py:257

commit v5 on v4

--- a/solution.py
+++ b/solution.py
@@ -9,7 +9,7 @@
 
 AXES = ("row", "col")
 CORES = 2
-PAD = 16
+PAD = 8
 FAR = 1.0e9
 VMEM_GRANT = 16 << 20
 
@@ -143,10 +143,10 @@
     return jnp.where(order == 0.0, FAR, order)
 
 
-def match_body(tasks, groups, n_blocks, n_rows, initial, *refs):
+def match_body(tasks, groups, n_blocks, initial, *refs):
     blocks, refs = refs[:n_blocks], refs[n_blocks:]
-    before, after, col_acc = refs[: len(refs) - n_rows - 3], refs[-n_rows - 3 : -1], refs[-1]
-    row_out, col_out = after[:n_rows], after[n_rows:]
+    count = len(refs) - 1 if initial else len(refs) // 2
+    before, after, col_acc = refs[: len(refs) - count - 1], refs[-count - 1 : -1], refs[-1]
     lanes = 128
     for k, ref in enumerate(after):
         ref[...] = jnp.full(ref.shape, -1.0, jnp.float32) if initial else before[k][...]
@@ -154,14 +154,20 @@
     def units_of(numbers):
         parts = [blocks[k][: blocks[k].shape[0] - PAD, :] for k in numbers]
         return parts[0] if len(parts) == 1 else jnp.concatenate(parts, axis=0)
+
+    def settle(value, block, place):
+        orders = lane_orders(blocks[block])
+        result, row, lane = place
+        at = (slice(row, row + 1), slice(lane, lane + orders.shape[1]))
+        after[result][at] = jnp.maximum(after[result][at], jnp.where(orders == FAR, -1.0, value))
 
     fresh = set()
     for rows, meets in tasks:
         row_units = units_of([row[0] for row in rows])
         sizes = [blocks[row[0]].shape[0] - PAD for row in rows]
-        row_orders = [lane_orders(blocks[row[0]]) for row in rows]
-        columns = [jnp.broadcast_to(orders, (lanes, n)).T[:, 0:1] for orders, n in zip(row_orders, sizes)]
+        columns = [jnp.broadcast_to(lane_orders(blocks[row[0]]), (lanes, n)).T[:, 0:1] for row, n in zip(rows, sizes)]
         best = [jnp.full((n, lanes), -1.0, jnp.float32) for n in sizes]
+        gives = any(row[2] for row in rows)
         for g in meets:
             numbers = [col[0] for col in groups[g]]
             orders = jnp.concatenate([lane_orders(blocks[k]) for k in numbers], axis=1)
@@ -171,29 +177,24 @@
             for k in range(0, score.shape[1], lanes):
                 first = 0
                 kept = [col_acc[g, :, k : k + lanes]] if g in fresh else []
-                for r, (_, _, _, counted) in enumerate(rows):
-                    n = sizes[r]
+                for r, n in enumerate(sizes):
                     part = score[first : first + n, k : k + lanes]
                     earlier = orders[:, k : k + lanes] < columns[r]
                     best[r] = jnp.maximum(best[r], jnp.where(earlier, part, -1.0))
-                    if counted:
+                    if rows[r][2]:
                         kept.append(jnp.max(jnp.where(earlier, -1.0, part).reshape(n // 8, 8, lanes), axis=0))
                     first += n
-                if any(row[3] for row in rows):
+                if gives:
                     col_acc[g, :, k : k + lanes] = functools.reduce(jnp.maximum, kept)
-            if any(row[3] for row in rows):
+            if gives:
                 fresh.add(g)
-        for r, (_, row, lane, _) in enumerate(rows):
-            value = jnp.where(row_orders[r] == FAR, -1.0, jnp.max(best[r].T, axis=0, keepdims=True))
-            at = slice(lane, lane + sizes[r])
-            row_out[row][:, at] = jnp.maximum(row_out[row][:, at], value)
+        for r, (block, place, _) in enumerate(rows):
+            settle(jnp.max(best[r].T, axis=0, keepdims=True), block, place)
     for g in sorted(fresh):
         start = 0
-        for col, side, chip, lane in groups[g]:
-            n = blocks[col].shape[0] - PAD
-            value = jnp.max(col_acc[g, :, start : start + n], axis=0, keepdims=True)
-            ref = col_out[side]
-            ref[chip : chip + 1, lane : lane + n] = jnp.maximum(ref[chip : chip + 1, lane : lane + n], value)
+        for block, place in groups[g]:
+            n = blocks[block].shape[0] - PAD
+            settle(jnp.max(col_acc[g, :, start : start + n], axis=0, keepdims=True), block, place)
             start += n
 
 
@@ -204,7 +205,7 @@
 def match(state, tasks, shape):
     blocks, groups, plan = [], [], []
 
-    def place(value):
+    def number(value):
         for k, known in enumerate(blocks):
             if known is value:
                 return k
@@ -214,17 +215,17 @@
     for rows, meets in tasks:
         found = []
         for group in meets:
-            group = [(place(col), *where) for col, *where in group]
+            group = [(number(block), place) for block, place in group]
             if group not in groups:
                 groups.append(group)
             found.append(groups.index(group))
-        plan.append(([(place(row), *where) for row, *where in rows], found))
+        plan.append(([(number(row), *rest) for row, *rest in rows], found))
     rows, chips, n = shape
     width = blocks[0].shape[1]
     widest = max(sum(blocks[col[0]].shape[0] - PAD for col in group) for group in groups)
     pairs = sum(blocks[r[0]].shape[0] * blocks[col[0]].shape[0] for p in plan for r in p[0] for g in p[1] for col in groups[g])
     return pl.pallas_call(
-        functools.partial(match_body, plan, groups, len(blocks), rows, state is None),
+        functools.partial(match_body, plan, groups, len(blocks), state is None),
         out_shape=[pltpu.VMEM((1, n), jnp.float32)] * rows + [pltpu.VMEM((chips, n), jnp.float32)] * 2,
         scratch_shapes=[pltpu.VMEM((len(groups), 8, widest), jnp.float32)],
         cost_estimate=pl.CostEstimate(flops=2 * pairs * width, bytes_accessed=2 * len(blocks) * n * width, transcendentals=0),
@@ -280,33 +281,41 @@
         twins = [send(block, swap) for block in [own, *plane]]
         corner_twins = [send(block, swap) for block in corner]
 
+        far = len(offsets)
+        shape = (len(line) + 1, far + 1, n)
+        side_of = [len(line) + 1, len(line) + 2]
+
         def by_two(blocks, side):
-            cols = [(block, side, k + 1, 0) for k, block in enumerate(blocks)]
+            cols = [(block, (side_of[side], k + 1, 0)) for k, block in enumerate(blocks)]
             return [cols[k : k + 2] for k in range(0, len(cols), 2)]
 
-        far = len(offsets)
-        own_cols = [[(own, 0, 0, 0), (twins[0], 1, 0, 0)]]
+        own_cols = [[(own, (side_of[0], 0, 0)), (twins[0], (side_of[1], 0, 0))]]
         plane_cols, twin_cols = by_two(plane, 0), by_two(twins[1:], 1)
-        corner_cols = [[(block, 0, far, start) for block, (start, _) in zip(corner, corner_pieces)]]
-        ctwin_cols = [[(block, 1, far, start) for block, (start, _) in zip(corner_twins, corner_pieces)]]
-
+        corner_cols, ctwin_cols = (
+            [[(block, (side_of[side], far, start)) for block, (start, _) in zip(blocks, corner_pieces)]]
+            for side, blocks in enumerate((corner, corner_twins))
+        )
         lanes = [start for start, _ in pieces]
-        mine = [(own, 0, 0, False)]
-        early = [(block, k + 1, at, True) for k, step in enumerate(line[:-1]) for block, at in zip(step, lanes)]
-        half_a, half_b = [(block, len(line), at, True) for block, at in zip(line[-1], lanes)]
-        shape = (len(line) + 1, far + 1, n)
-        near_cols = own_cols + plane_cols + twin_cols
+        mine = [(own, (0, 0, 0), False)]
+        early = [(block, (k + 1, 0, at), True) for k, step in enumerate(line[:-1]) for block, at in zip(step, lanes)]
+        half_a, half_b = [(block, (len(line), 0, at), True) for block, at in zip(line[-1], lanes)]
+
+        def streamed(groups):
+            return [(*col, True) for group in groups for col in group]
+
+        near = streamed(own_cols + plane_cols + twin_cols)
         state = match(None, [(mine, own_cols)], shape)
         if early:
             state = match(state, [(early[:1], own_cols)], shape)
         rest = [(early[1:], own_cols)] if early else []
         state = match(state, rest + [(mine + early, plane_cols)], shape)
         state = match(state, [(mine + early, twin_cols)], shape)
-        state = match(state, [([half_a], near_cols)], shape)
+        state = match(state, [(near, [[half_a[:2]]])], shape)
         state = match(state, [([*mine, *early, half_a], corner_cols)], shape)
         state = match(state, [([*mine, *early, half_a], ctwin_cols)], shape)
         best = list(state[: len(line)])
-        *_, late, ours, theirs = match(state, [([half_b], near_cols + corner_cols + ctwin_cols)], shape)
+        everything = near + streamed(corner_cols + ctwin_cols)
+        *_, late, ours, theirs = match(state, [(everything, [[half_b[:2]]])], shape)
         best.append(late)
 
         theirs = send(theirs, swap)

time: 64.9 us -> 63.7 us (0.982)
  waiting for transfers between devices: 29.1 us -> 28.1 us
    ppermute x19, waiting for transfers between devices: 29.1 us -> 28.1 us  [send(): return lax.ppermute(value, AXES, pairs)]
where the time goes in v5:
time: 63.7 us; the launch traced here: 63.5 us
  waiting for transfers between devices  28.1 us (44%)
  starting transfers between devices  23.6 us (37%)
  Pallas kernels  11.1 us (17%)
    ppermute x19, waiting for transfers between devices, send(): return lax.ppermute(value, AXES, pairs)  28.1 us
    ppermute x19, starting transfers between devices, send(): return lax.ppermute(value, AXES, pairs)  23.6 us
    pallas_call x8, Pallas kernels, match(): pl.pallas_call(functools.partial(match_body, plan, groups, len(blocks), s...  9.66 us
    pallas_call x1, Pallas kernels, pack(): call(*(pltpu.with_memory_space_constraint(v, pltpu.HBM) for v in (embeddi...  1.38 us
  transfers between devices with their start and end apart: 19, of which 7 were waited for; matrix products, arithmetic and copies ran while one was open for 0% of the time, Pallas kernels for 12%

profile of v5, /device:TPU:0, one launch (start us, length us, event | category | flops | bytes accessed | tf_op | source)
XLA Modules:
  0.0 63.5 jit_solution(12858254662419327519)
XLA Ops:
  0.0 1.4 %pack.1 = (bf16[392,768]{1,0:T(8,128)(2,1)S(1)}, bf16[136,768]{1,0:T(8,128)(2,1)S(1)}, bf16[264,768]{1,0:T(8,128)(2,1)S(1)}) custom-call(bf16[384,768]{1,0:T(8,128)(2,1)} %emb_hbm.1, s32[384]{0:T(512)} %order_hbm.1), custom_call_target="tpu_custom_call" | custom-call | tf_op jit(solution)/shard_map/pack/pallas_call | solution.py:116
  1.4 3.0 %collective-permute-start = (bf16[392,768]{1,0:T(8,128)(2,1)S(1)}, bf16[392,768]{1,0:T(8,128)(2,1)S(1)}, u32[]{:S(2)}, u32[]{:S(2)}) collective-permute-start(bf16[392,768]{1,0:T(8,128)(2,1)S(1)} %get-tuple-element.50.refs_0_.refs_2_.refs_1_), channel_id=1, source_target_pairs={{0,2},{1,3},{2,0},{3,1},{4,6},{5,7},{6,4},{7,5},{8,10},{9,11},{10,... | collective-permute-start | bytes 1806344 | tf_op jit(solution)/shard_map/ppermute | solution.py:258
  4.4 1.5 %collective-permute-start.3 = (bf16[392,768]{1,0:T(8,128)(2,1)S(1)}, bf16[392,768]{1,0:T(8,128)(2,1)S(1)}, u32[]{:S(2)}, u32[]{:S(2)}) collective-permute-start(bf16[392,768]{1,0:T(8,128)(2,1)S(1)} %get-tuple-element.50.refs_0_.refs_2_.refs_1_), channel_id=1, source_target_pairs={{0,4},{1,5},{2,6},{3,7},{4,0},{5,1},{6,2},{7,3},{8,12},{9,13},{10,... | collective-permute-start | bytes 1806344 | tf_op jit(solution)/shard_map/ppermute | solution.py:258
  5.9 1.6 %collective-permute-start.6 = (bf16[136,768]{1,0:T(8,128)(2,1)S(1)}, bf16[136,768]{1,0:T(8,128)(2,1)S(1)}, u32[]{:S(2)}, u32[]{:S(2)}) collective-permute-start(bf16[136,768]{1,0:T(8,128)(2,1)S(1)} %get-tuple-element.51), channel_id=1, source_target_pairs={{0,8},{1,9},{2,10},{3,11},{4,12},{5,13},{6,14},{7,15},{8,16},{9,17... | collective-permute-start | bytes 626696 | tf_op jit(solution)/shard_map/ppermute | solution.py:258
  7.5 1.6 %collective-permute-start.7 = (bf16[264,768]{1,0:T(8,128)(2,1)S(1)}, bf16[264,768]{1,0:T(8,128)(2,1)S(1)}, u32[]{:S(2)}, u32[]{:S(2)}) collective-permute-start(bf16[264,768]{1,0:T(8,128)(2,1)S(1)} %get-tuple-element.52), channel_id=1, source_target_pairs={{0,8},{1,9},{2,10},{3,11},{4,12},{5,13},{6,14},{7,15},{8,16},{9,17... | collective-permute-start | bytes 1216520 | tf_op jit(solution)/shard_map/ppermute | solution.py:258
  9.1 8.9 %collective-permute-done.ref.refs_3_ = bf16[392,768]{1,0:T(8,128)(2,1)S(1)} collective-permute-done((bf16[392,768]{1,0:T(8,128)(2,1)S(1)}, bf16[392,768]{1,0:T(8,128)(2,1)S(1)}, u32[]{:S(2)}, u32[]{:S(2)}) %collective-permute-start) | collective-permute-done | bytes 602144 | tf_op jit(solution)/shard_map/ppermute | solution.py:258
  18.0 0.0 collective-permute-start.10
  18.1 1.8 %collective-permute-start.1 = (bf16[264,768]{1,0:T(8,128)(2,1)S(1)}, bf16[264,768]{1,0:T(8,128)(2,1)S(1)}, u32[]{:S(2)}, u32[]{:S(2)}) collective-permute-start(bf16[264,768]{1,0:T(8,128)(2,1)S(1)} %piece.2), channel_id=1, source_target_pairs={{0,4},{1,5},{2,6},{3,7},{4,0},{5,1},{6,2},{7,3},{8,12},{9,13},{10,... | collective-permute-start | bytes 1216520 | tf_op jit(solution)/shard_map/ppermute | solution.py:258
  19.9 0.2 collective-permute-start.11
  20.1 2.7 %collective-permute-done.7.refs_2_.refs_4_ = bf16[264,768]{1,0:T(8,128)(2,1)S(1)} collective-permute-done((bf16[264,768]{1,0:T(8,128)(2,1)S(1)}, bf16[264,768]{1,0:T(8,128)(2,1)S(1)}, u32[]{:S(2)}, u32[]{:S(2)}) %collective-permute-start.7) | collective-permute-done | bytes 405536 | tf_op jit(solution)/shard_map/ppermute | solution.py:258
  22.8 0.5 collective-permute-start.4
  23.4 6.6 %collective-permute-done.1.refs_0_.refs_7_ = bf16[264,768]{1,0:T(8,128)(2,1)S(1)} collective-permute-done((bf16[264,768]{1,0:T(8,128)(2,1)S(1)}, bf16[264,768]{1,0:T(8,128)(2,1)S(1)}, u32[]{:S(2)}, u32[]{:S(2)}) %collective-permute-start.1) | collective-permute-done | bytes 405536 | tf_op jit(solution)/shard_map/ppermute | solution.py:258
  29.9 3.7 %collective-permute-start.13 = (bf16[264,768]{1,0:T(8,128)(2,1)S(1)}, bf16[264,768]{1,0:T(8,128)(2,1)S(1)}, u32[]{:S(2)}, u32[]{:S(2)}) collective-permute-start(bf16[264,768]{1,0:T(8,128)(2,1)S(1)} %collective-permute-done.7.refs_2_.refs_4_), channel_id=1, source_target_pairs={{0,8},{1,9},{2,10},{3,11},{4,12},{5,13},{6,14},{7,15},{8,16},{9,17... | collective-permute-start | bytes 1216520 | tf_op jit(solution)/shard_map/ppermute | solution.py:258
  33.7 0.8 %shard_map.28 = (f32[1,384]{1,0:T(1,128)S(1)}, f32[1,384]{1,0:T(1,128)S(1)}, f32[1,384]{1,0:T(1,128)S(1)}, f32[4,384]{1,0:T(4,128)S(1)}, f32[4,384]{1,0:T(4,128)S(1)}) custom-call(bf16[392,768]{1,0:T(8,128)(2,1)S(1)} %get-tuple-element.50.refs_0_.refs_2_.refs_1_, bf16[392,768]{1,0:T(8,128)(2,1)S(1)} %collective-permute-done.9.refs_1_.refs_2_), custom_call_target="tpu_custom_call" | custom-call | flops 472055808 | bytes 1179648 | tf_op jit(solution)/shard_map/pallas_call | solution.py:227
  34.5 0.6 %shard_map.29 = (f32[1,384]{1,0:T(1,128)S(1)}, f32[1,384]{1,0:T(1,128)S(1)}, f32[1,384]{1,0:T(1,128)S(1)}, f32[4,384]{1,0:T(4,128)S(1)}, f32[4,384]{1,0:T(4,128)S(1)}) custom-call(bf16[392,768]{1,0:T(8,128)(2,1)S(1)} %get-tuple-element.50.refs_0_.refs_2_.refs_1_, bf16[392,768]{1,0:T(8,128)(2,1)S(1)} %collective-permute-done.9.refs_1_.refs_2_, ...), custom_call_target="tpu_custom_call" | custom-call | flops 163774464 | bytes 1769472 | tf_op jit(solution)/shard_map/pallas_call | solution.py:227
  35.2 3.4 %collective-permute-start.8 = (bf16[136,768]{1,0:T(8,128)(2,1)S(1)}, bf16[136,768]{1,0:T(8,128)(2,1)S(1)}, u32[]{:S(2)}, u32[]{:S(2)}) collective-permute-start(bf16[136,768]{1,0:T(8,128)(2,1)S(1)} %collective-permute-done.6.refs_2_.refs_5_.refs_3_), channel_id=1, source_target_pairs={{0,8},{1,9},{2,10},{3,11},{4,12},{5,13},{6,14},{7,15},{8,16},{9,17... | collective-permute-start | bytes 626696 | tf_op jit(solution)/shard_map/ppermute | solution.py:258
  38.6 0.1 collective-permute-start.5
  38.7 1.6 %shard_map.30 = (f32[1,384]{1,0:T(1,128)S(1)}, f32[1,384]{1,0:T(1,128)S(1)}, f32[1,384]{1,0:T(1,128)S(1)}, f32[4,384]{1,0:T(4,128)S(1)}, f32[4,384]{1,0:T(4,128)S(1)}) custom-call(bf16[392,768]{1,0:T(8,128)(2,1)S(1)} %get-tuple-element.50.refs_0_.refs_2_.refs_1_, bf16[392,768]{1,0:T(8,128)(2,1)S(1)} %collective-permute-done.9.refs_1_.refs_2_, ...), custom_call_target="tpu_custom_call" | custom-call | flops 1271660544 | bytes 3538944 | tf_op jit(solution)/shard_map/pallas_call | solution.py:227
  40.3 1.3 %shard_map.31 = (f32[1,384]{1,0:T(1,128)S(1)}, f32[1,384]{1,0:T(1,128)S(1)}, f32[1,384]{1,0:T(1,128)S(1)}, f32[4,384]{1,0:T(4,128)S(1)}, f32[4,384]{1,0:T(4,128)S(1)}) custom-call(bf16[392,768]{1,0:T(8,128)(2,1)S(1)} %collective-permute-done.10.refs_0_.refs_5_, bf16[392,768]{1,0:T(8,128)(2,1)S(1)} %collective-permute-done.11.refs_1_.refs_6_, ...), custom_call_target="tpu_custom_call" | custom-call | flops 953745408 | bytes 2949120 | tf_op jit(solution)/shard_map/pallas_call | solution.py:227
  41.5 5.9 %collective-permute-done.8.refs_0_.refs_5_ = bf16[136,768]{1,0:T(8,128)(2,1)S(1)} collective-permute-done((bf16[136,768]{1,0:T(8,128)(2,1)S(1)}, bf16[136,768]{1,0:T(8,128)(2,1)S(1)}, u32[]{:S(2)}, u32[]{:S(2)}) %collective-permute-start.8) | collective-permute-done | bytes 208928 | tf_op jit(solution)/shard_map/ppermute | solution.py:258
  47.4 1.2 %shard_map.32 = (f32[1,384]{1,0:T(1,128)S(1)}, f32[1,384]{1,0:T(1,128)S(1)}, f32[1,384]{1,0:T(1,128)S(1)}, f32[4,384]{1,0:T(4,128)S(1)}, f32[4,384]{1,0:T(4,128)S(1)}) custom-call(bf16[136,768]{1,0:T(8,128)(2,1)S(1)} %collective-permute-done.8.refs_0_.refs_5_, bf16[392,768]{1,0:T(8,128)(2,1)S(1)} %get-tuple-element.50.refs_0_.refs_2_.refs_1_, ...), custom_call_target="tpu_custom_call" | custom-call | flops 491323392 | bytes 4128768 | tf_op jit(solution)/shard_map/pallas_call | solution.py:227
  48.6 1.0 %shard_map.33 = (f32[1,384]{1,0:T(1,128)S(1)}, f32[1,384]{1,0:T(1,128)S(1)}, f32[1,384]{1,0:T(1,128)S(1)}, f32[4,384]{1,0:T(4,128)S(1)}, f32[4,384]{1,0:T(4,128)S(1)}) custom-call(bf16[264,768]{1,0:T(8,128)(2,1)S(1)} %collective-permute-done.1.refs_0_.refs_7_, bf16[136,768]{1,0:T(8,128)(2,1)S(1)} %collective-permute-done.4.refs_1_.refs_8_, ...), custom_call_target="tpu_custom_call" | custom-call | flops 570163200 | bytes 3538944 | tf_op jit(solution)/shard_map/pallas_call | solution.py:227
  49.7 1.0 %shard_map.34 = (f32[1,384]{1,0:T(1,128)S(1)}, f32[1,384]{1,0:T(1,128)S(1)}, f32[1,384]{1,0:T(1,128)S(1)}, f32[4,384]{1,0:T(4,128)S(1)}, f32[4,384]{1,0:T(4,128)S(1)}) custom-call(bf16[264,768]{1,0:T(8,128)(2,1)S(1)} %collective-permute-done.2.refs_0_.refs_9_, bf16[136,768]{1,0:T(8,128)(2,1)S(1)} %collective-permute-done.5.refs_1_.refs_10_, ...), custom_call_target="tpu_custom_call" | custom-call | flops 570163200 | bytes 3538944 | tf_op jit(solution)/shard_map/pallas_call | solution.py:227
  50.7 2.1 %shard_map.35 = (f32[1,384]{1,0:T(1,128)}, f32[1,384]{1,0:T(1,128)}, f32[1,384]{1,0:T(1,128)S(1)}, f32[4,384]{1,0:T(4,128)S(1)}, f32[4,384]{1,0:T(4,128)S(1)}) custom-call(bf16[264,768]{1,0:T(8,128)(2,1)S(1)} %collective-permute-done.13.refs_0_, bf16[392,768]{1,0:T(8,128)(2,1)S(1)} %get-tuple-element.50.refs_0_.refs_2_.refs_1_, ...), custom_call_target="tpu_custom_call" | custom-call | flops 1278148608 | bytes 6488064 | tf_op jit(solution)/shard_map/pallas_call | solution.py:227
  52.8 2.5 %collective-permute-start.14 = (f32[1,384]{1,0:T(1,128)S(1)}, f32[1,384]{1,0:T(1,128)S(1)}, u32[]{:S(2)}, u32[]{:S(2)}) collective-permute-start(f32[1,384]{1,0:T(1,128)S(1)} %get-tuple-element.88), channel_id=1, source_target_pairs={{0,8},{1,9},{2,10},{3,11},{4,12},{5,13},{6,14},{7,15},{8,24},{9,25... | collective-permute-start | bytes 4616 | tf_op jit(solution)/shard_map/ppermute | solution.py:258
  55.3 1.6 %collective-permute-start.16 = (f32[1,384]{1,0:T(1,128)S(1)}, f32[1,384]{1,0:T(1,128)S(1)}, u32[]{:S(2)}, u32[]{:S(2)}) collective-permute-start(f32[1,384]{1,0:T(1,128)S(1)} %get-tuple-element.92), channel_id=1, source_target_pairs={{2,0},{3,1},{0,2},{1,3},{6,4},{7,5},{4,6},{5,7},{10,8},{11,9},{8,1... | collective-permute-start | bytes 4616 | tf_op jit(solution)/shard_map/ppermute | solution.py:258
  56.9 1.5 %collective-permute-start.17 = (f32[1,384]{1,0:T(1,128)S(1)}, f32[1,384]{1,0:T(1,128)S(1)}, u32[]{:S(2)}, u32[]{:S(2)}) collective-permute-start(f32[1,384]{1,0:T(1,128)S(1)} %get-tuple-element.93), channel_id=1, source_target_pairs={{4,0},{5,1},{6,2},{7,3},{0,4},{1,5},{2,6},{3,7},{12,8},{13,9},{14,... | collective-permute-start | bytes 4616 | tf_op jit(solution)/shard_map/ppermute | solution.py:258
  58.4 0.5 collective-permute-start.18
  58.9 0.1 collective-permute-done.16
  59.0 1.5 %collective-permute-done.17 = f32[1,384]{1,0:T(1,128)S(1)} collective-permute-done((f32[1,384]{1,0:T(1,128)S(1)}, f32[1,384]{1,0:T(1,128)S(1)}, u32[]{:S(2)}, u32[]{:S(2)}) %collective-permute-start.17) | collective-permute-done | bytes 1568 | tf_op jit(solution)/shard_map/ppermute | solution.py:258
  60.5 2.4 %collective-permute-done.18 = f32[1,384]{1,0:T(1,128)S(1)} collective-permute-done((f32[1,384]{1,0:T(1,128)S(1)}, f32[1,384]{1,0:T(1,128)S(1)}, u32[]{:S(2)}, u32[]{:S(2)}) %collective-permute-start.18) | collective-permute-done | bytes 1568 | tf_op jit(solution)/shard_map/ppermute | solution.py:258
  62.9 0.6 maximum_reduce_fusion
  (19 shorter events, 0.1 us)
Async XLA Ops:
  1.4 16.6 %collective-permute-start = (bf16[392,768]{1,0:T(8,128)(2,1)S(1)}, bf16[392,768]{1,0:T(8,128)(2,1)S(1)}, u32[]{:S(2)}, u32[]{:S(2)}) collective-permute-start(bf16[392,768]{1,0:T(8,128)(2,1)S(1)} %get-tuple-element.50.refs_0_.refs_2_.refs_1_), channel_id=1, source_target_pairs={{0,2},{1,3},{2,0},{3,1},{4,6},{5,7},{6,4},{7,5},{8,10},{9,11},{10,... | collective-permute-start | bytes 1806344 | tf_op jit(solution)/shard_map/ppermute | solution.py:258
  4.4 15.5 %collective-permute-start.3 = (bf16[392,768]{1,0:T(8,128)(2,1)S(1)}, bf16[392,768]{1,0:T(8,128)(2,1)S(1)}, u32[]{:S(2)}, u32[]{:S(2)}) collective-permute-start(bf16[392,768]{1,0:T(8,128)(2,1)S(1)} %get-tuple-element.50.refs_0_.refs_2_.refs_1_), channel_id=1, source_target_pairs={{0,4},{1,5},{2,6},{3,7},{4,0},{5,1},{6,2},{7,3},{8,12},{9,13},{10,... | collective-permute-start | bytes 1806344 | tf_op jit(solution)/shard_map/ppermute | solution.py:258
  5.9 12.1 %collective-permute-start.6 = (bf16[136,768]{1,0:T(8,128)(2,1)S(1)}, bf16[136,768]{1,0:T(8,128)(2,1)S(1)}, u32[]{:S(2)}, u32[]{:S(2)}) collective-permute-start(bf16[136,768]{1,0:T(8,128)(2,1)S(1)} %get-tuple-element.51), channel_id=1, source_target_pairs={{0,8},{1,9},{2,10},{3,11},{4,12},{5,13},{6,14},{7,15},{8,16},{9,17... | collective-permute-start | bytes 626696 | tf_op jit(solution)/shard_map/ppermute | solution.py:258
  7.5 22.4 %collective-permute-start.9 = (bf16[392,768]{1,0:T(8,128)(2,1)S(1)}, bf16[392,768]{1,0:T(8,128)(2,1)S(1)}, u32[]{:S(2)}, u32[]{:S(2)}) collective-permute-start(bf16[392,768]{1,0:T(8,128)(2,1)S(1)} %get-tuple-element.50.refs_0_.refs_2_.refs_1_), channel_id=1, source_target_pairs={{0,1},{1,0},{2,3},{3,2},{4,5},{5,4},{6,7},{7,6},{8,9},{9,8},{10,11... | collective-permute-start | bytes 1806344 | tf_op jit(solution)/shard_map/ppermute | solution.py:258
  7.5 15.3 %collective-permute-start.7 = (bf16[264,768]{1,0:T(8,128)(2,1)S(1)}, bf16[264,768]{1,0:T(8,128)(2,1)S(1)}, u32[]{:S(2)}, u32[]{:S(2)}) collective-permute-start(bf16[264,768]{1,0:T(8,128)(2,1)S(1)} %get-tuple-element.52), channel_id=1, source_target_pairs={{0,8},{1,9},{2,10},{3,11},{4,12},{5,13},{6,14},{7,15},{8,16},{9,17... | collective-permute-start | bytes 1216520 | tf_op jit(solution)/shard_map/ppermute | solution.py:258
  18.0 20.6 %collective-permute-start.10 = (bf16[392,768]{1,0:T(8,128)(2,1)S(1)}, bf16[392,768]{1,0:T(8,128)(2,1)S(1)}, u32[]{:S(2)}, u32[]{:S(2)}) collective-permute-start(bf16[392,768]{1,0:T(8,128)(2,1)S(1)} %collective-permute-done.ref.refs_3_), channel_id=1, source_target_pairs={{0,1},{1,0},{2,3},{3,2},{4,5},{5,4},{6,7},{7,6},{8,9},{9,8},{10,11... | collective-permute-start | bytes 1806344 | tf_op jit(solution)/shard_map/ppermute | solution.py:258
  18.1 11.9 %collective-permute-start.1 = (bf16[264,768]{1,0:T(8,128)(2,1)S(1)}, bf16[264,768]{1,0:T(8,128)(2,1)S(1)}, u32[]{:S(2)}, u32[]{:S(2)}) collective-permute-start(bf16[264,768]{1,0:T(8,128)(2,1)S(1)} %piece.2), channel_id=1, source_target_pairs={{0,4},{1,5},{2,6},{3,7},{4,0},{5,1},{6,2},{7,3},{8,12},{9,13},{10,... | collective-permute-start | bytes 1216520 | tf_op jit(solution)/shard_map/ppermute | solution.py:258
  19.9 20.4 %collective-permute-start.11 = (bf16[392,768]{1,0:T(8,128)(2,1)S(1)}, bf16[392,768]{1,0:T(8,128)(2,1)S(1)}, u32[]{:S(2)}, u32[]{:S(2)}) collective-permute-start(bf16[392,768]{1,0:T(8,128)(2,1)S(1)} %collective-permute-done.3.ref.refs_4_), channel_id=1, source_target_pairs={{0,1},{1,0},{2,3},{3,2},{4,5},{5,4},{6,7},{7,6},{8,9},{9,8},{10,11... | collective-permute-start | bytes 1806344 | tf_op jit(solution)/shard_map/ppermute | solution.py:258
  22.8 12.3 %collective-permute-start.4 = (bf16[136,768]{1,0:T(8,128)(2,1)S(1)}, bf16[136,768]{1,0:T(8,128)(2,1)S(1)}, u32[]{:S(2)}, u32[]{:S(2)}) collective-permute-start(bf16[136,768]{1,0:T(8,128)(2,1)S(1)} %piece.3), channel_id=1, source_target_pairs={{0,2},{1,3},{2,0},{3,1},{4,6},{5,7},{6,4},{7,5},{8,10},{9,11},{10,... | collective-permute-start | bytes 626696 | tf_op jit(solution)/shard_map/ppermute | solution.py:258
  29.9 19.7 %collective-permute-start.2 = (bf16[264,768]{1,0:T(8,128)(2,1)S(1)}, bf16[264,768]{1,0:T(8,128)(2,1)S(1)}, u32[]{:S(2)}, u32[]{:S(2)}) collective-permute-start(bf16[264,768]{1,0:T(8,128)(2,1)S(1)} %collective-permute-done.1.refs_0_.refs_7_), channel_id=1, source_target_pairs={{0,1},{1,0},{2,3},{3,2},{4,5},{5,4},{6,7},{7,6},{8,9},{9,8},{10,11... | collective-permute-start | bytes 1216520 | tf_op jit(solution)/shard_map/ppermute | solution.py:258
  29.9 20.7 %collective-permute-start.13 = (bf16[264,768]{1,0:T(8,128)(2,1)S(1)}, bf16[264,768]{1,0:T(8,128)(2,1)S(1)}, u32[]{:S(2)}, u32[]{:S(2)}) collective-permute-start(bf16[264,768]{1,0:T(8,128)(2,1)S(1)} %collective-permute-done.7.refs_2_.refs_4_), channel_id=1, source_target_pairs={{0,8},{1,9},{2,10},{3,11},{4,12},{5,13},{6,14},{7,15},{8,16},{9,17... | collective-permute-start | bytes 1216520 | tf_op jit(solution)/shard_map/ppermute | solution.py:258
  35.2 12.3 %collective-permute-start.8 = (bf16[136,768]{1,0:T(8,128)(2,1)S(1)}, bf16[136,768]{1,0:T(8,128)(2,1)S(1)}, u32[]{:S(2)}, u32[]{:S(2)}) collective-permute-start(bf16[136,768]{1,0:T(8,128)(2,1)S(1)} %collective-permute-done.6.refs_2_.refs_5_.refs_3_), channel_id=1, source_target_pairs={{0,8},{1,9},{2,10},{3,11},{4,12},{5,13},{6,14},{7,15},{8,16},{9,17... | collective-permute-start | bytes 626696 | tf_op jit(solution)/shard_map/ppermute | solution.py:258
  38.6 11.0 %collective-permute-start.5 = (bf16[136,768]{1,0:T(8,128)(2,1)S(1)}, bf16[136,768]{1,0:T(8,128)(2,1)S(1)}, u32[]{:S(2)}, u32[]{:S(2)}) collective-permute-start(bf16[136,768]{1,0:T(8,128)(2,1)S(1)} %collective-permute-done.4.refs_1_.refs_8_), channel_id=1, source_target_pairs={{0,1},{1,0},{2,3},{3,2},{4,5},{5,4},{6,7},{7,6},{8,9},{9,8},{10,11... | collective-permute-start | bytes 626696 | tf_op jit(solution)/shard_map/ppermute | solution.py:258
  52.8 2.5 %collective-permute-start.15 = (f32[4,384]{1,0:T(4,128)S(1)}, f32[4,384]{1,0:T(4,128)S(1)}, u32[]{:S(2)}, u32[]{:S(2)}) collective-permute-start(f32[4,384]{1,0:T(4,128)S(1)} %get-tuple-element.90), channel_id=1, source_target_pairs={{0,1},{1,0},{2,3},{3,2},{4,5},{5,4},{6,7},{7,6},{8,9},{9,8},{10,11... | collective-permute-start | bytes 18440 | tf_op jit(solution)/shard_map/ppermute | solution.py:258
  52.8 6.1 %collective-permute-start.12 = (f32[1,384]{1,0:T(1,128)S(1)}, f32[1,384]{1,0:T(1,128)S(1)}, u32[]{:S(2)}, u32[]{:S(2)}) collective-permute-start(f32[1,384]{1,0:T(1,128)S(1)} %get-tuple-element.84.refs_12_), channel_id=1, source_target_pairs={{0,24},{1,25},{2,26},{3,27},{4,28},{5,29},{6,30},{7,31},{8,0},{9,1... | collective-permute-start | bytes 4616 | tf_op jit(solution)/shard_map/ppermute | solution.py:258
  52.8 6.1 %collective-permute-start.14 = (f32[1,384]{1,0:T(1,128)S(1)}, f32[1,384]{1,0:T(1,128)S(1)}, u32[]{:S(2)}, u32[]{:S(2)}) collective-permute-start(f32[1,384]{1,0:T(1,128)S(1)} %get-tuple-element.88), channel_id=1, source_target_pairs={{0,8},{1,9},{2,10},{3,11},{4,12},{5,13},{6,14},{7,15},{8,24},{9,25... | collective-permute-start | bytes 4616 | tf_op jit(solution)/shard_map/ppermute | solution.py:258
  55.3 3.6 %collective-permute-start.16 = (f32[1,384]{1,0:T(1,128)S(1)}, f32[1,384]{1,0:T(1,128)S(1)}, u32[]{:S(2)}, u32[]{:S(2)}) collective-permute-start(f32[1,384]{1,0:T(1,128)S(1)} %get-tuple-element.92), channel_id=1, source_target_pairs={{2,0},{3,1},{0,2},{1,3},{6,4},{7,5},{4,6},{5,7},{10,8},{11,9},{8,1... | collective-permute-start | bytes 4616 | tf_op jit(solution)/shard_map/ppermute | solution.py:258
  56.9 3.6 %collective-permute-start.17 = (f32[1,384]{1,0:T(1,128)S(1)}, f32[1,384]{1,0:T(1,128)S(1)}, u32[]{:S(2)}, u32[]{:S(2)}) collective-permute-start(f32[1,384]{1,0:T(1,128)S(1)} %get-tuple-element.93), channel_id=1, source_target_pairs={{4,0},{5,1},{6,2},{7,3},{0,4},{1,5},{2,6},{3,7},{12,8},{13,9},{14,... | collective-permute-start | bytes 4616 | tf_op jit(solution)/shard_map/ppermute | solution.py:258
  58.4 4.5 %collective-permute-start.18 = (f32[1,384]{1,0:T(1,128)S(1)}, f32[1,384]{1,0:T(1,128)S(1)}, u32[]{:S(2)}, u32[]{:S(2)}) collective-permute-start(f32[1,384]{1,0:T(1,128)S(1)} %get-tuple-element.94), channel_id=1, source_target_pairs={{6,0},{7,1},{4,2},{5,3},{2,4},{3,5},{0,6},{1,7},{14,8},{15,9},{12,... | collective-permute-start | bytes 4616 | tf_op jit(solution)/shard_map/ppermute | solution.py:258

commit v6 on v5

--- a/solution.py
+++ b/solution.py
@@ -143,7 +143,7 @@
     return jnp.where(order == 0.0, FAR, order)
 
 
-def match_body(tasks, groups, n_blocks, initial, *refs):
+def match_body(tasks, groups, n_blocks, initial, needed, *refs):
     blocks, refs = refs[:n_blocks], refs[n_blocks:]
     count = len(refs) - 1 if initial else len(refs) // 2
     before, after, col_acc = refs[: len(refs) - count - 1], refs[-count - 1 : -1], refs[-1]
@@ -151,58 +151,64 @@
     for k, ref in enumerate(after):
         ref[...] = jnp.full(ref.shape, -1.0, jnp.float32) if initial else before[k][...]
 
-    def units_of(numbers):
-        parts = [blocks[k][: blocks[k].shape[0] - PAD, :] for k in numbers]
-        return parts[0] if len(parts) == 1 else jnp.concatenate(parts, axis=0)
-
-    def settle(value, block, place):
-        orders = lane_orders(blocks[block])
-        result, row, lane = place
-        at = (slice(row, row + 1), slice(lane, lane + orders.shape[1]))
-        after[result][at] = jnp.maximum(after[result][at], jnp.where(orders == FAR, -1.0, value))
-
-    fresh = set()
-    for rows, meets in tasks:
-        row_units = units_of([row[0] for row in rows])
-        sizes = [blocks[row[0]].shape[0] - PAD for row in rows]
-        columns = [jnp.broadcast_to(lane_orders(blocks[row[0]]), (lanes, n)).T[:, 0:1] for row, n in zip(rows, sizes)]
-        best = [jnp.full((n, lanes), -1.0, jnp.float32) for n in sizes]
-        gives = any(row[2] for row in rows)
-        for g in meets:
-            numbers = [col[0] for col in groups[g]]
-            orders = jnp.concatenate([lane_orders(blocks[k]) for k in numbers], axis=1)
-            score = lax.dot_general(
-                row_units, units_of(numbers), (((1,), (1,)), ((), ())), preferred_element_type=jnp.float32
-            )
-            for k in range(0, score.shape[1], lanes):
-                first = 0
-                kept = [col_acc[g, :, k : k + lanes]] if g in fresh else []
-                for r, n in enumerate(sizes):
-                    part = score[first : first + n, k : k + lanes]
-                    earlier = orders[:, k : k + lanes] < columns[r]
-                    best[r] = jnp.maximum(best[r], jnp.where(earlier, part, -1.0))
-                    if rows[r][2]:
-                        kept.append(jnp.max(jnp.where(earlier, -1.0, part).reshape(n // 8, 8, lanes), axis=0))
-                    first += n
+    def work():
+        def units_of(numbers):
+            parts = [blocks[k][: blocks[k].shape[0] - PAD, :] for k in numbers]
+            return parts[0] if len(parts) == 1 else jnp.concatenate(parts, axis=0)
+
+        def settle(value, block, place):
+            orders = lane_orders(blocks[block])
+            result, row, lane = place
+            at = (slice(row, row + 1), slice(lane, lane + orders.shape[1]))
+            after[result][at] = jnp.maximum(after[result][at], jnp.where(orders == FAR, -1.0, value))
+
+        fresh = set()
+        for rows, meets in tasks:
+            row_units = units_of([row[0] for row in rows])
+            sizes = [blocks[row[0]].shape[0] - PAD for row in rows]
+            columns = [jnp.broadcast_to(lane_orders(blocks[row[0]]), (lanes, n)).T[:, 0:1] for row, n in zip(rows, sizes)]
+            best = [jnp.full((n, lanes), -1.0, jnp.float32) for n in sizes]
+            gives = any(row[2] for row in rows)
+            for g in meets:
+                numbers = [col[0] for col in groups[g]]
+                orders = jnp.concatenate([lane_orders(blocks[k]) for k in numbers], axis=1)
+                score = lax.dot_general(
+                    row_units, units_of(numbers), (((1,), (1,)), ((), ())), preferred_element_type=jnp.float32
+                )
+                for k in range(0, score.shape[1], lanes):
+                    first = 0
+                    kept = [col_acc[g, :, k : k + lanes]] if g in fresh else []
+                    for r, n in enumerate(sizes):
+                        part = score[first : first + n, k : k + lanes]
+                        earlier = orders[:, k : k + lanes] < columns[r]
+                        best[r] = jnp.maximum(best[r], jnp.where(earlier, part, -1.0))
+                        if rows[r][2]:
+                            kept.append(jnp.max(jnp.where(earlier, -1.0, part).reshape(n // 8, 8, lanes), axis=0))
+                        first += n
+                    if gives:
+                        col_acc[g, :, k : k + lanes] = functools.reduce(jnp.maximum, kept)
                 if gives:
-                    col_acc[g, :, k : k + lanes] = functools.reduce(jnp.maximum, kept)
-            if gives:
-                fresh.add(g)
-        for r, (block, place, _) in enumerate(rows):
-            settle(jnp.max(best[r].T, axis=0, keepdims=True), block, place)
-    for g in sorted(fresh):
-        start = 0
-        for block, place in groups[g]:
-            n = blocks[block].shape[0] - PAD
-            settle(jnp.max(col_acc[g, :, start : start + n], axis=0, keepdims=True), block, place)
-            start += n
+                    fresh.add(g)
+            for r, (block, place, _) in enumerate(rows):
+                settle(jnp.max(best[r].T, axis=0, keepdims=True), block, place)
+        for g in sorted(fresh):
+            start = 0
+            for block, place in groups[g]:
+                n = blocks[block].shape[0] - PAD
+                settle(jnp.max(col_acc[g, :, start : start + n], axis=0, keepdims=True), block, place)
+                start += n
+
+    if needed is None:
+        work()
+    else:
+        pl.when(jnp.min(lane_orders(blocks[needed])) < FAR)(work)
 
 
 def in_vmem(values):
     return [pltpu.with_memory_space_constraint(v, pltpu.VMEM) for v in values]
 
 
-def match(state, tasks, shape):
+def match(state, tasks, shape, needed=None):
     blocks, groups, plan = [], [], []
 
     def number(value):
@@ -225,7 +231,7 @@
     widest = max(sum(blocks[col[0]].shape[0] - PAD for col in group) for group in groups)
     pairs = sum(blocks[r[0]].shape[0] * blocks[col[0]].shape[0] for p in plan for r in p[0] for g in p[1] for col in groups[g])
     return pl.pallas_call(
-        functools.partial(match_body, plan, groups, len(blocks), state is None),
+        functools.partial(match_body, plan, groups, len(blocks), state is None, None if needed is None else number(needed)),
         out_shape=[pltpu.VMEM((1, n), jnp.float32)] * rows + [pltpu.VMEM((chips, n), jnp.float32)] * 2,
         scratch_shapes=[pltpu.VMEM((len(groups), 8, widest), jnp.float32)],
         cost_estimate=pl.CostEstimate(flops=2 * pairs * width, bytes_accessed=2 * len(blocks) * n * width, transcendentals=0),
@@ -266,9 +272,10 @@
 
         own, *parts = pack(embeddings, doc_order, pieces)
         line = []
-        for hop in layout.line_hops():
-            parts = [send(part, layout.line_move(hop)) for part in parts]
-            line.append(parts)
+        for hop in layout.line_hops()[:-1]:
+            source = line[-1] if line else parts
+            line.append([send(part, layout.line_move(hop)) for part in source])
+        line.append([send(part, layout.line_move(maps[-1])) for part in parts])
         plane = [send(own, layout.plane_move(*d)) for d in offsets[:-1]]
 
         dy, dx = offsets[-1]
@@ -310,12 +317,14 @@
         rest = [(early[1:], own_cols)] if early else []
         state = match(state, rest + [(mine + early, plane_cols)], shape)
         state = match(state, [(mine + early, twin_cols)], shape)
-        state = match(state, [(near, [[half_a[:2]]])], shape)
+        state = match(state, [(near, [[half_a[:2]]])], shape, half_a[0])
         state = match(state, [([*mine, *early, half_a], corner_cols)], shape)
         state = match(state, [([*mine, *early, half_a], ctwin_cols)], shape)
         best = list(state[: len(line)])
-        everything = near + streamed(corner_cols + ctwin_cols)
-        *_, late, ours, theirs = match(state, [(everything, [[half_b[:2]]])], shape)
+        shift = len(line)
+        streams = [(b, (at[0] - shift, *at[1:]), gives) for b, at, gives in near + streamed(corner_cols + ctwin_cols)]
+        piece_at = (half_b[0], (0, *half_b[1][1:]))
+        late, ours, theirs = match(state[shift:], [(streams, [[piece_at]])], (1, *shape[1:]), half_b[0])
         best.append(late)
 
         theirs = send(theirs, swap)

time: 63.7 us -> 64.5 us (1.013)
  waiting for transfers between devices: 28.1 us -> 31.5 us
  Pallas kernels: 11.1 us -> 7.97 us
    ppermute x19, waiting for transfers between devices: 28.1 us -> 31.5 us  [send(): return lax.ppermute(value, AXES, pairs)]
    pallas_call x8, Pallas kernels: 9.66 us -> 6.53 us  [match(): pl.pallas_call(functools.partial(match_body, plan, groups, len(blocks), s...]
  transfers between devices with their start and end apart: 19 -> 19, of which waited for: 7 -> 8; matrix products, arithmetic and copies ran while one was open for 0% -> 0% of each run, Pallas kernels for 12% -> 10%
where the time goes in v6:
time: 64.5 us; the launch traced here: 64.3 us
  waiting for transfers between devices  31.5 us (49%)
  starting transfers between devices  24.1 us (37%)
  Pallas kernels  7.97 us (12%)
    ppermute x19, waiting for transfers between devices, send(): return lax.ppermute(value, AXES, pairs)  31.5 us
    ppermute x19, starting transfers between devices, send(): return lax.ppermute(value, AXES, pairs)  24.1 us
    pallas_call x8, Pallas kernels, match(): pl.pallas_call(functools.partial(match_body, plan, groups, len(blocks), s...  6.53 us
    pallas_call x1, Pallas kernels, pack(): call(*(pltpu.with_memory_space_constraint(v, pltpu.HBM) for v in (embeddi...  1.38 us
  transfers between devices with their start and end apart: 19, of which 8 were waited for; matrix products, arithmetic and copies ran while one was open for 0% of the time, Pallas kernels for 10%

profile of v6, /device:TPU:0, one launch (start us, length us, event | category | flops | bytes accessed | tf_op | source)
XLA Modules:
  0.0 64.3 jit_solution(17367190476122150985)
XLA Ops:
  0.0 1.4 %pack.1 = (bf16[392,768]{1,0:T(8,128)(2,1)S(1)}, bf16[136,768]{1,0:T(8,128)(2,1)S(1)}, bf16[264,768]{1,0:T(8,128)(2,1)S(1)}) custom-call(bf16[384,768]{1,0:T(8,128)(2,1)} %emb_hbm.1, s32[384]{0:T(512)} %order_hbm.1), custom_call_target="tpu_custom_call" | custom-call | tf_op jit(solution)/shard_map/pack/pallas_call | solution.py:116
  1.4 3.1 %collective-permute-start.3 = (bf16[392,768]{1,0:T(8,128)(2,1)S(1)}, bf16[392,768]{1,0:T(8,128)(2,1)S(1)}, u32[]{:S(2)}, u32[]{:S(2)}) collective-permute-start(bf16[392,768]{1,0:T(8,128)(2,1)S(1)} %get-tuple-element.50.refs_0_.refs_2_.refs_1_), channel_id=1, source_target_pairs={{0,4},{1,5},{2,6},{3,7},{4,0},{5,1},{6,2},{7,3},{8,12},{9,13},{10,... | collective-permute-start | bytes 1806344 | tf_op jit(solution)/shard_map/ppermute | solution.py:264
  4.5 1.5 %collective-permute-start = (bf16[392,768]{1,0:T(8,128)(2,1)S(1)}, bf16[392,768]{1,0:T(8,128)(2,1)S(1)}, u32[]{:S(2)}, u32[]{:S(2)}) collective-permute-start(bf16[392,768]{1,0:T(8,128)(2,1)S(1)} %get-tuple-element.50.refs_0_.refs_2_.refs_1_), channel_id=1, source_target_pairs={{0,2},{1,3},{2,0},{3,1},{4,6},{5,7},{6,4},{7,5},{8,10},{9,11},{10,... | collective-permute-start | bytes 1806344 | tf_op jit(solution)/shard_map/ppermute | solution.py:264
  5.9 1.6 %collective-permute-start.6 = (bf16[136,768]{1,0:T(8,128)(2,1)S(1)}, bf16[136,768]{1,0:T(8,128)(2,1)S(1)}, u32[]{:S(2)}, u32[]{:S(2)}) collective-permute-start(bf16[136,768]{1,0:T(8,128)(2,1)S(1)} %get-tuple-element.51), channel_id=1, source_target_pairs={{0,8},{1,9},{2,10},{3,11},{4,12},{5,13},{6,14},{7,15},{8,16},{9,17... | collective-permute-start | bytes 626696 | tf_op jit(solution)/shard_map/ppermute | solution.py:264
  7.5 1.6 %collective-permute-start.7 = (bf16[264,768]{1,0:T(8,128)(2,1)S(1)}, bf16[264,768]{1,0:T(8,128)(2,1)S(1)}, u32[]{:S(2)}, u32[]{:S(2)}) collective-permute-start(bf16[264,768]{1,0:T(8,128)(2,1)S(1)} %get-tuple-element.52), channel_id=1, source_target_pairs={{0,8},{1,9},{2,10},{3,11},{4,12},{5,13},{6,14},{7,15},{8,16},{9,17... | collective-permute-start | bytes 1216520 | tf_op jit(solution)/shard_map/ppermute | solution.py:264
  9.1 8.9 %collective-permute-done.3.ref.refs_4_ = bf16[392,768]{1,0:T(8,128)(2,1)S(1)} collective-permute-done((bf16[392,768]{1,0:T(8,128)(2,1)S(1)}, bf16[392,768]{1,0:T(8,128)(2,1)S(1)}, u32[]{:S(2)}, u32[]{:S(2)}) %collective-permute-start.3) | collective-permute-done | bytes 602144 | tf_op jit(solution)/shard_map/ppermute | solution.py:264
  18.0 1.5 %collective-permute-done.ref.refs_3_ = bf16[392,768]{1,0:T(8,128)(2,1)S(1)} collective-permute-done((bf16[392,768]{1,0:T(8,128)(2,1)S(1)}, bf16[392,768]{1,0:T(8,128)(2,1)S(1)}, u32[]{:S(2)}, u32[]{:S(2)}) %collective-permute-start) | collective-permute-done | bytes 602144 | tf_op jit(solution)/shard_map/ppermute | solution.py:264
  19.5 0.4 collective-permute-start.1
  20.0 0.2 collective-permute-start.10
  20.1 2.7 %collective-permute-done.7.refs_2_.refs_4_ = bf16[264,768]{1,0:T(8,128)(2,1)S(1)} collective-permute-done((bf16[264,768]{1,0:T(8,128)(2,1)S(1)}, bf16[264,768]{1,0:T(8,128)(2,1)S(1)}, u32[]{:S(2)}, u32[]{:S(2)}) %collective-permute-start.7) | collective-permute-done | bytes 405536 | tf_op jit(solution)/shard_map/ppermute | solution.py:264
  22.8 0.5 collective-permute-start.4
  23.4 6.6 %collective-permute-done.1.refs_0_.refs_7_ = bf16[264,768]{1,0:T(8,128)(2,1)S(1)} collective-permute-done((bf16[264,768]{1,0:T(8,128)(2,1)S(1)}, bf16[264,768]{1,0:T(8,128)(2,1)S(1)}, u32[]{:S(2)}, u32[]{:S(2)}) %collective-permute-start.1) | collective-permute-done | bytes 405536 | tf_op jit(solution)/shard_map/ppermute | solution.py:264
  29.9 4.7 %collective-permute-start.13 = (bf16[264,768]{1,0:T(8,128)(2,1)S(1)}, bf16[264,768]{1,0:T(8,128)(2,1)S(1)}, u32[]{:S(2)}, u32[]{:S(2)}) collective-permute-start(bf16[264,768]{1,0:T(8,128)(2,1)S(1)} %get-tuple-element.52), channel_id=1, source_target_pairs={{0,16},{1,17},{2,18},{3,19},{4,20},{5,21},{6,22},{7,23},{24,8},{25... | collective-permute-start | bytes 1216520 | tf_op jit(solution)/shard_map/ppermute | solution.py:264
  34.7 0.8 %shard_map.28 = (f32[1,384]{1,0:T(1,128)S(1)}, f32[1,384]{1,0:T(1,128)S(1)}, f32[1,384]{1,0:T(1,128)S(1)}, f32[4,384]{1,0:T(4,128)S(1)}, f32[4,384]{1,0:T(4,128)S(1)}) custom-call(bf16[392,768]{1,0:T(8,128)(2,1)S(1)} %get-tuple-element.50.refs_0_.refs_2_.refs_1_, bf16[392,768]{1,0:T(8,128)(2,1)S(1)} %collective-permute-done.9.refs_1_.refs_2_), custom_call_target="tpu_custom_call" | custom-call | flops 472055808 | bytes 1179648 | tf_op jit(solution)/shard_map/pallas_call | solution.py:233
  35.5 0.6 shard_map.29
  36.1 1.3 %collective-permute-start.8 = (bf16[136,768]{1,0:T(8,128)(2,1)S(1)}, bf16[136,768]{1,0:T(8,128)(2,1)S(1)}, u32[]{:S(2)}, u32[]{:S(2)}) collective-permute-start(bf16[136,768]{1,0:T(8,128)(2,1)S(1)} %get-tuple-element.51), channel_id=1, source_target_pairs={{0,16},{1,17},{2,18},{3,19},{4,20},{5,21},{6,22},{7,23},{24,8},{25... | collective-permute-start | bytes 626696 | tf_op jit(solution)/shard_map/ppermute | solution.py:264
  37.5 0.3 collective-permute-start.5
  37.8 1.6 %shard_map.30 = (f32[1,384]{1,0:T(1,128)S(1)}, f32[1,384]{1,0:T(1,128)S(1)}, f32[1,384]{1,0:T(1,128)S(1)}, f32[4,384]{1,0:T(4,128)S(1)}, f32[4,384]{1,0:T(4,128)S(1)}) custom-call(bf16[392,768]{1,0:T(8,128)(2,1)S(1)} %get-tuple-element.50.refs_0_.refs_2_.refs_1_, bf16[392,768]{1,0:T(8,128)(2,1)S(1)} %collective-permute-done.9.refs_1_.refs_2_, ...), custom_call_target="tpu_custom_call" | custom-call | flops 1271660544 | bytes 3538944 | tf_op jit(solution)/shard_map/pallas_call | solution.py:233
  39.4 1.3 %shard_map.31 = (f32[1,384]{1,0:T(1,128)S(1)}, f32[1,384]{1,0:T(1,128)S(1)}, f32[1,384]{1,0:T(1,128)S(1)}, f32[4,384]{1,0:T(4,128)S(1)}, f32[4,384]{1,0:T(4,128)S(1)}) custom-call(bf16[392,768]{1,0:T(8,128)(2,1)S(1)} %collective-permute-done.10.refs_0_.refs_5_, bf16[392,768]{1,0:T(8,128)(2,1)S(1)} %collective-permute-done.11.refs_1_.refs_6_, ...), custom_call_target="tpu_custom_call" | custom-call | flops 953745408 | bytes 2949120 | tf_op jit(solution)/shard_map/pallas_call | solution.py:233
  40.6 7.8 %collective-permute-done.8.refs_0_.refs_5_ = bf16[136,768]{1,0:T(8,128)(2,1)S(1)} collective-permute-done((bf16[136,768]{1,0:T(8,128)(2,1)S(1)}, bf16[136,768]{1,0:T(8,128)(2,1)S(1)}, u32[]{:S(2)}, u32[]{:S(2)}) %collective-permute-start.8) | collective-permute-done | bytes 208928 | tf_op jit(solution)/shard_map/ppermute | solution.py:264
  48.4 0.1 shard_map.32
  48.6 1.0 %shard_map.33 = (f32[1,384]{1,0:T(1,128)S(1)}, f32[1,384]{1,0:T(1,128)S(1)}, f32[1,384]{1,0:T(1,128)S(1)}, f32[4,384]{1,0:T(4,128)S(1)}, f32[4,384]{1,0:T(4,128)S(1)}) custom-call(bf16[264,768]{1,0:T(8,128)(2,1)S(1)} %collective-permute-done.1.refs_0_.refs_7_, bf16[136,768]{1,0:T(8,128)(2,1)S(1)} %collective-permute-done.4.refs_1_.refs_8_, ...), custom_call_target="tpu_custom_call" | custom-call | flops 570163200 | bytes 3538944 | tf_op jit(solution)/shard_map/pallas_call | solution.py:233
  49.6 1.0 %shard_map.34 = (f32[1,384]{1,0:T(1,128)S(1)}, f32[1,384]{1,0:T(1,128)S(1)}, f32[1,384]{1,0:T(1,128)S(1)}, f32[4,384]{1,0:T(4,128)S(1)}, f32[4,384]{1,0:T(4,128)S(1)}) custom-call(bf16[264,768]{1,0:T(8,128)(2,1)S(1)} %collective-permute-done.2.refs_0_.refs_9_, bf16[136,768]{1,0:T(8,128)(2,1)S(1)} %collective-permute-done.5.refs_1_.refs_10_, ...), custom_call_target="tpu_custom_call" | custom-call | flops 570163200 | bytes 3538944 | tf_op jit(solution)/shard_map/pallas_call | solution.py:233
  50.6 0.1 shard_map.35
  50.8 1.4 %collective-permute-start.12 = (f32[1,384]{1,0:T(1,128)S(1)}, f32[1,384]{1,0:T(1,128)S(1)}, u32[]{:S(2)}, u32[]{:S(2)}) collective-permute-start(f32[1,384]{1,0:T(1,128)S(1)} %get-tuple-element.84), channel_id=1, source_target_pairs={{0,24},{1,25},{2,26},{3,27},{4,28},{5,29},{6,30},{7,31},{8,0},{9,1... | collective-permute-start | bytes 4616 | tf_op jit(solution)/shard_map/ppermute | solution.py:264
  52.2 3.9 %collective-permute-start.14 = (f32[1,384]{1,0:T(1,128)S(1)}, f32[1,384]{1,0:T(1,128)S(1)}, u32[]{:S(2)}, u32[]{:S(2)}) collective-permute-start(f32[1,384]{1,0:T(1,128)S(1)} %get-tuple-element.88), channel_id=1, source_target_pairs={{0,8},{1,9},{2,10},{3,11},{4,12},{5,13},{6,14},{7,15},{8,24},{9,25... | collective-permute-start | bytes 4616 | tf_op jit(solution)/shard_map/ppermute | solution.py:264
  56.1 1.6 %collective-permute-start.16 = (f32[1,384]{1,0:T(1,128)S(1)}, f32[1,384]{1,0:T(1,128)S(1)}, u32[]{:S(2)}, u32[]{:S(2)}) collective-permute-start(f32[1,384]{1,0:T(1,128)S(1)} %get-tuple-element.92), channel_id=1, source_target_pairs={{2,0},{3,1},{0,2},{1,3},{6,4},{7,5},{4,6},{5,7},{10,8},{11,9},{8,1... | collective-permute-start | bytes 4616 | tf_op jit(solution)/shard_map/ppermute | solution.py:264
  57.7 1.5 %collective-permute-start.17 = (f32[1,384]{1,0:T(1,128)S(1)}, f32[1,384]{1,0:T(1,128)S(1)}, u32[]{:S(2)}, u32[]{:S(2)}) collective-permute-start(f32[1,384]{1,0:T(1,128)S(1)} %get-tuple-element.93), channel_id=1, source_target_pairs={{4,0},{5,1},{6,2},{7,3},{0,4},{1,5},{2,6},{3,7},{12,8},{13,9},{14,... | collective-permute-start | bytes 4616 | tf_op jit(solution)/shard_map/ppermute | solution.py:264
  59.2 0.5 collective-permute-start.18
  59.8 1.5 %collective-permute-done.17 = f32[1,384]{1,0:T(1,128)S(1)} collective-permute-done((f32[1,384]{1,0:T(1,128)S(1)}, f32[1,384]{1,0:T(1,128)S(1)}, u32[]{:S(2)}, u32[]{:S(2)}) %collective-permute-start.17) | collective-permute-done | bytes 1568 | tf_op jit(solution)/shard_map/ppermute | solution.py:264
  61.3 2.4 %collective-permute-done.18 = f32[1,384]{1,0:T(1,128)S(1)} collective-permute-done((f32[1,384]{1,0:T(1,128)S(1)}, f32[1,384]{1,0:T(1,128)S(1)}, u32[]{:S(2)}, u32[]{:S(2)}) %collective-permute-start.18) | collective-permute-done | bytes 1568 | tf_op jit(solution)/shard_map/ppermute | solution.py:264
  63.7 0.6 maximum_reduce_fusion
  (19 shorter events, 0.2 us)
Async XLA Ops:
  1.4 16.7 %collective-permute-start.3 = (bf16[392,768]{1,0:T(8,128)(2,1)S(1)}, bf16[392,768]{1,0:T(8,128)(2,1)S(1)}, u32[]{:S(2)}, u32[]{:S(2)}) collective-permute-start(bf16[392,768]{1,0:T(8,128)(2,1)S(1)} %get-tuple-element.50.refs_0_.refs_2_.refs_1_), channel_id=1, source_target_pairs={{0,4},{1,5},{2,6},{3,7},{4,0},{5,1},{6,2},{7,3},{8,12},{9,13},{10,... | collective-permute-start | bytes 1806344 | tf_op jit(solution)/shard_map/ppermute | solution.py:264
  4.5 15.1 %collective-permute-start = (bf16[392,768]{1,0:T(8,128)(2,1)S(1)}, bf16[392,768]{1,0:T(8,128)(2,1)S(1)}, u32[]{:S(2)}, u32[]{:S(2)}) collective-permute-start(bf16[392,768]{1,0:T(8,128)(2,1)S(1)} %get-tuple-element.50.refs_0_.refs_2_.refs_1_), channel_id=1, source_target_pairs={{0,2},{1,3},{2,0},{3,1},{4,6},{5,7},{6,4},{7,5},{8,10},{9,11},{10,... | collective-permute-start | bytes 1806344 | tf_op jit(solution)/shard_map/ppermute | solution.py:264
  5.9 14.0 %collective-permute-start.6 = (bf16[136,768]{1,0:T(8,128)(2,1)S(1)}, bf16[136,768]{1,0:T(8,128)(2,1)S(1)}, u32[]{:S(2)}, u32[]{:S(2)}) collective-permute-start(bf16[136,768]{1,0:T(8,128)(2,1)S(1)} %get-tuple-element.51), channel_id=1, source_target_pairs={{0,8},{1,9},{2,10},{3,11},{4,12},{5,13},{6,14},{7,15},{8,16},{9,17... | collective-permute-start | bytes 626696 | tf_op jit(solution)/shard_map/ppermute | solution.py:264
  7.5 22.4 %collective-permute-start.9 = (bf16[392,768]{1,0:T(8,128)(2,1)S(1)}, bf16[392,768]{1,0:T(8,128)(2,1)S(1)}, u32[]{:S(2)}, u32[]{:S(2)}) collective-permute-start(bf16[392,768]{1,0:T(8,128)(2,1)S(1)} %get-tuple-element.50.refs_0_.refs_2_.refs_1_), channel_id=1, source_target_pairs={{0,1},{1,0},{2,3},{3,2},{4,5},{5,4},{6,7},{7,6},{8,9},{9,8},{10,11... | collective-permute-start | bytes 1806344 | tf_op jit(solution)/shard_map/ppermute | solution.py:264
  7.5 15.3 %collective-permute-start.7 = (bf16[264,768]{1,0:T(8,128)(2,1)S(1)}, bf16[264,768]{1,0:T(8,128)(2,1)S(1)}, u32[]{:S(2)}, u32[]{:S(2)}) collective-permute-start(bf16[264,768]{1,0:T(8,128)(2,1)S(1)} %get-tuple-element.52), channel_id=1, source_target_pairs={{0,8},{1,9},{2,10},{3,11},{4,12},{5,13},{6,14},{7,15},{8,16},{9,17... | collective-permute-start | bytes 1216520 | tf_op jit(solution)/shard_map/ppermute | solution.py:264
  18.0 19.4 %collective-permute-start.11 = (bf16[392,768]{1,0:T(8,128)(2,1)S(1)}, bf16[392,768]{1,0:T(8,128)(2,1)S(1)}, u32[]{:S(2)}, u32[]{:S(2)}) collective-permute-start(bf16[392,768]{1,0:T(8,128)(2,1)S(1)} %collective-permute-done.3.ref.refs_4_), channel_id=1, source_target_pairs={{0,1},{1,0},{2,3},{3,2},{4,5},{5,4},{6,7},{7,6},{8,9},{9,8},{10,11... | collective-permute-start | bytes 1806344 | tf_op jit(solution)/shard_map/ppermute | solution.py:264
  19.5 10.4 %collective-permute-start.1 = (bf16[264,768]{1,0:T(8,128)(2,1)S(1)}, bf16[264,768]{1,0:T(8,128)(2,1)S(1)}, u32[]{:S(2)}, u32[]{:S(2)}) collective-permute-start(bf16[264,768]{1,0:T(8,128)(2,1)S(1)} %piece.2), channel_id=1, source_target_pairs={{0,4},{1,5},{2,6},{3,7},{4,0},{5,1},{6,2},{7,3},{8,12},{9,13},{10,... | collective-permute-start | bytes 1216520 | tf_op jit(solution)/shard_map/ppermute | solution.py:264
  20.0 19.4 %collective-permute-start.10 = (bf16[392,768]{1,0:T(8,128)(2,1)S(1)}, bf16[392,768]{1,0:T(8,128)(2,1)S(1)}, u32[]{:S(2)}, u32[]{:S(2)}) collective-permute-start(bf16[392,768]{1,0:T(8,128)(2,1)S(1)} %collective-permute-done.ref.refs_3_), channel_id=1, source_target_pairs={{0,1},{1,0},{2,3},{3,2},{4,5},{5,4},{6,7},{7,6},{8,9},{9,8},{10,11... | collective-permute-start | bytes 1806344 | tf_op jit(solution)/shard_map/ppermute | solution.py:264
  22.8 13.3 %collective-permute-start.4 = (bf16[136,768]{1,0:T(8,128)(2,1)S(1)}, bf16[136,768]{1,0:T(8,128)(2,1)S(1)}, u32[]{:S(2)}, u32[]{:S(2)}) collective-permute-start(bf16[136,768]{1,0:T(8,128)(2,1)S(1)} %piece.3), channel_id=1, source_target_pairs={{0,2},{1,3},{2,0},{3,1},{4,6},{5,7},{6,4},{7,5},{8,10},{9,11},{10,... | collective-permute-start | bytes 626696 | tf_op jit(solution)/shard_map/ppermute | solution.py:264
  29.9 19.6 %collective-permute-start.2 = (bf16[264,768]{1,0:T(8,128)(2,1)S(1)}, bf16[264,768]{1,0:T(8,128)(2,1)S(1)}, u32[]{:S(2)}, u32[]{:S(2)}) collective-permute-start(bf16[264,768]{1,0:T(8,128)(2,1)S(1)} %collective-permute-done.1.refs_0_.refs_7_), channel_id=1, source_target_pairs={{0,1},{1,0},{2,3},{3,2},{4,5},{5,4},{6,7},{7,6},{8,9},{9,8},{10,11... | collective-permute-start | bytes 1216520 | tf_op jit(solution)/shard_map/ppermute | solution.py:264
  29.9 20.6 %collective-permute-start.13 = (bf16[264,768]{1,0:T(8,128)(2,1)S(1)}, bf16[264,768]{1,0:T(8,128)(2,1)S(1)}, u32[]{:S(2)}, u32[]{:S(2)}) collective-permute-start(bf16[264,768]{1,0:T(8,128)(2,1)S(1)} %get-tuple-element.52), channel_id=1, source_target_pairs={{0,16},{1,17},{2,18},{3,19},{4,20},{5,21},{6,22},{7,23},{24,8},{25... | collective-permute-start | bytes 1216520 | tf_op jit(solution)/shard_map/ppermute | solution.py:264
  36.1 12.3 %collective-permute-start.8 = (bf16[136,768]{1,0:T(8,128)(2,1)S(1)}, bf16[136,768]{1,0:T(8,128)(2,1)S(1)}, u32[]{:S(2)}, u32[]{:S(2)}) collective-permute-start(bf16[136,768]{1,0:T(8,128)(2,1)S(1)} %get-tuple-element.51), channel_id=1, source_target_pairs={{0,16},{1,17},{2,18},{3,19},{4,20},{5,21},{6,22},{7,23},{24,8},{25... | collective-permute-start | bytes 626696 | tf_op jit(solution)/shard_map/ppermute | solution.py:264
  37.5 12.1 %collective-permute-start.5 = (bf16[136,768]{1,0:T(8,128)(2,1)S(1)}, bf16[136,768]{1,0:T(8,128)(2,1)S(1)}, u32[]{:S(2)}, u32[]{:S(2)}) collective-permute-start(bf16[136,768]{1,0:T(8,128)(2,1)S(1)} %collective-permute-done.4.refs_1_.refs_8_), channel_id=1, source_target_pairs={{0,1},{1,0},{2,3},{3,2},{4,5},{5,4},{6,7},{7,6},{8,9},{9,8},{10,11... | collective-permute-start | bytes 626696 | tf_op jit(solution)/shard_map/ppermute | solution.py:264
  50.7 5.4 %collective-permute-start.15 = (f32[4,384]{1,0:T(4,128)S(1)}, f32[4,384]{1,0:T(4,128)S(1)}, u32[]{:S(2)}, u32[]{:S(2)}) collective-permute-start(f32[4,384]{1,0:T(4,128)S(1)} %get-tuple-element.90), channel_id=1, source_target_pairs={{0,1},{1,0},{2,3},{3,2},{4,5},{5,4},{6,7},{7,6},{8,9},{9,8},{10,11... | collective-permute-start | bytes 18440 | tf_op jit(solution)/shard_map/ppermute | solution.py:264
  50.8 8.9 %collective-permute-start.12 = (f32[1,384]{1,0:T(1,128)S(1)}, f32[1,384]{1,0:T(1,128)S(1)}, u32[]{:S(2)}, u32[]{:S(2)}) collective-permute-start(f32[1,384]{1,0:T(1,128)S(1)} %get-tuple-element.84), channel_id=1, source_target_pairs={{0,24},{1,25},{2,26},{3,27},{4,28},{5,29},{6,30},{7,31},{8,0},{9,1... | collective-permute-start | bytes 4616 | tf_op jit(solution)/shard_map/ppermute | solution.py:264
  52.2 7.5 %collective-permute-start.14 = (f32[1,384]{1,0:T(1,128)S(1)}, f32[1,384]{1,0:T(1,128)S(1)}, u32[]{:S(2)}, u32[]{:S(2)}) collective-permute-start(f32[1,384]{1,0:T(1,128)S(1)} %get-tuple-element.88), channel_id=1, source_target_pairs={{0,8},{1,9},{2,10},{3,11},{4,12},{5,13},{6,14},{7,15},{8,24},{9,25... | collective-permute-start | bytes 4616 | tf_op jit(solution)/shard_map/ppermute | solution.py:264
  56.1 3.6 %collective-permute-start.16 = (f32[1,384]{1,0:T(1,128)S(1)}, f32[1,384]{1,0:T(1,128)S(1)}, u32[]{:S(2)}, u32[]{:S(2)}) collective-permute-start(f32[1,384]{1,0:T(1,128)S(1)} %get-tuple-element.92), channel_id=1, source_target_pairs={{2,0},{3,1},{0,2},{1,3},{6,4},{7,5},{4,6},{5,7},{10,8},{11,9},{8,1... | collective-permute-start | bytes 4616 | tf_op jit(solution)/shard_map/ppermute | solution.py:264
  57.7 3.6 %collective-permute-start.17 = (f32[1,384]{1,0:T(1,128)S(1)}, f32[1,384]{1,0:T(1,128)S(1)}, u32[]{:S(2)}, u32[]{:S(2)}) collective-permute-start(f32[1,384]{1,0:T(1,128)S(1)} %get-tuple-element.93), channel_id=1, source_target_pairs={{4,0},{5,1},{6,2},{7,3},{0,4},{1,5},{2,6},{3,7},{12,8},{13,9},{14,... | collective-permute-start | bytes 4616 | tf_op jit(solution)/shard_map/ppermute | solution.py:264
  59.2 4.5 %collective-permute-start.18 = (f32[1,384]{1,0:T(1,128)S(1)}, f32[1,384]{1,0:T(1,128)S(1)}, u32[]{:S(2)}, u32[]{:S(2)}) collective-permute-start(f32[1,384]{1,0:T(1,128)S(1)} %get-tuple-element.94), channel_id=1, source_target_pairs={{6,0},{7,1},{4,2},{5,3},{2,4},{3,5},{0,6},{1,7},{14,8},{15,9},{12,... | collective-permute-start | bytes 4616 | tf_op jit(solution)/shard_map/ppermute | solution.py:264

commit v7 on v6

--- a/solution.py
+++ b/solution.py
@@ -271,10 +271,10 @@
         swap = layout.swap()
 
         own, *parts = pack(embeddings, doc_order, pieces)
-        line = []
+        line = [[own]]
         for hop in layout.line_hops()[:-1]:
-            source = line[-1] if line else parts
-            line.append([send(part, layout.line_move(hop)) for part in source])
+            line.append([send(line[-1][0], layout.line_move(hop))])
+        line = line[1:]
         line.append([send(part, layout.line_move(maps[-1])) for part in parts])
         plane = [send(own, layout.plane_move(*d)) for d in offsets[:-1]]
 
@@ -304,7 +304,7 @@
         )
         lanes = [start for start, _ in pieces]
         mine = [(own, (0, 0, 0), False)]
-        early = [(block, (k + 1, 0, at), True) for k, step in enumerate(line[:-1]) for block, at in zip(step, lanes)]
+        early = [(step[0], (k + 1, 0, 0), True) for k, step in enumerate(line[:-1])]
         half_a, half_b = [(block, (len(line), 0, at), True) for block, at in zip(line[-1], lanes)]
 
         def streamed(groups):
@@ -312,9 +312,7 @@
 
         near = streamed(own_cols + plane_cols + twin_cols)
         state = match(None, [(mine, own_cols)], shape)
-        if early:
-            state = match(state, [(early[:1], own_cols)], shape)
-        rest = [(early[1:], own_cols)] if early else []
+        rest = [(early, own_cols)] if early else []
         state = match(state, rest + [(mine + early, plane_cols)], shape)
         state = match(state, [(mine + early, twin_cols)], shape)
         state = match(state, [(near, [[half_a[:2]]])], shape, half_a[0])

time: 64.5 us -> 64.5 us (level)
  waiting for transfers between devices: 31.5 us -> 32.5 us
    ppermute x19 -> x18, waiting for transfers between devices: 31.5 us -> 32.5 us  [send(): return lax.ppermute(value, AXES, pairs)]
    ppermute x19 -> x18, starting transfers between devices: 24.1 us -> 23.6 us  [send(): return lax.ppermute(value, AXES, pairs)]
    pallas_call x8 -> x7, Pallas kernels: 6.53 us -> 6.08 us  [match(): pl.pallas_call(functools.partial(match_body, plan, groups, len(blocks), s...]
  transfers between devices with their start and end apart: 19 -> 18, of which waited for: 8 -> 7; matrix products, arithmetic and copies ran while one was open for 0% -> 0% of each run, Pallas kernels for 10% -> 9%
where the time goes in v7:
time: 64.5 us; the launch traced here: 64.3 us
  waiting for transfers between devices  32.5 us (50%)
  starting transfers between devices  23.6 us (37%)
  Pallas kernels  7.51 us (12%)
    ppermute x18, waiting for transfers between devices, send(): return lax.ppermute(value, AXES, pairs)  32.5 us
    ppermute x18, starting transfers between devices, send(): return lax.ppermute(value, AXES, pairs)  23.6 us
    pallas_call x7, Pallas kernels, match(): pl.pallas_call(functools.partial(match_body, plan, groups, len(blocks), s...  6.08 us
    pallas_call x1, Pallas kernels, pack(): call(*(pltpu.with_memory_space_constraint(v, pltpu.HBM) for v in (embeddi...  1.38 us
  transfers between devices with their start and end apart: 18, of which 7 were waited for; matrix products, arithmetic and copies ran while one was open for 0% of the time, Pallas kernels for 9%

profile of v7, /device:TPU:0, one launch (start us, length us, event | category | flops | bytes accessed | tf_op | source)
XLA Modules:
  0.0 64.3 jit_solution(18129154799282938545)
XLA Ops:
  0.0 1.4 %pack.1 = (bf16[392,768]{1,0:T(8,128)(2,1)S(1)}, bf16[136,768]{1,0:T(8,128)(2,1)S(1)}, bf16[264,768]{1,0:T(8,128)(2,1)S(1)}) custom-call(bf16[384,768]{1,0:T(8,128)(2,1)} %emb_hbm.1, s32[384]{0:T(512)} %order_hbm.1), custom_call_target="tpu_custom_call" | custom-call | tf_op jit(solution)/shard_map/pack/pallas_call | solution.py:116
  1.4 3.1 %collective-permute-start.3 = (bf16[392,768]{1,0:T(8,128)(2,1)S(1)}, bf16[392,768]{1,0:T(8,128)(2,1)S(1)}, u32[]{:S(2)}, u32[]{:S(2)}) collective-permute-start(bf16[392,768]{1,0:T(8,128)(2,1)S(1)} %get-tuple-element.45.refs_0_.refs_2_.refs_1_), channel_id=1, source_target_pairs={{0,4},{1,5},{2,6},{3,7},{4,0},{5,1},{6,2},{7,3},{8,12},{9,13},{10,... | collective-permute-start | bytes 1806344 | tf_op jit(solution)/shard_map/ppermute | solution.py:264
  4.5 1.5 %collective-permute-start = (bf16[392,768]{1,0:T(8,128)(2,1)S(1)}, bf16[392,768]{1,0:T(8,128)(2,1)S(1)}, u32[]{:S(2)}, u32[]{:S(2)}) collective-permute-start(bf16[392,768]{1,0:T(8,128)(2,1)S(1)} %get-tuple-element.45.refs_0_.refs_2_.refs_1_), channel_id=1, source_target_pairs={{0,2},{1,3},{2,0},{3,1},{4,6},{5,7},{6,4},{7,5},{8,10},{9,11},{10,... | collective-permute-start | bytes 1806344 | tf_op jit(solution)/shard_map/ppermute | solution.py:264
  5.9 0.0 collective-permute-start.8
  5.9 1.6 %collective-permute-start.6 = (bf16[392,768]{1,0:T(8,128)(2,1)S(1)}, bf16[392,768]{1,0:T(8,128)(2,1)S(1)}, u32[]{:S(2)}, u32[]{:S(2)}) collective-permute-start(bf16[392,768]{1,0:T(8,128)(2,1)S(1)} %get-tuple-element.45.refs_0_.refs_2_.refs_1_), channel_id=1, source_target_pairs={{0,8},{1,9},{2,10},{3,11},{4,12},{5,13},{6,14},{7,15},{8,16},{9,17... | collective-permute-start | bytes 1806344 | tf_op jit(solution)/shard_map/ppermute | solution.py:264
  7.5 10.5 %collective-permute-done.3.ref.refs_4_ = bf16[392,768]{1,0:T(8,128)(2,1)S(1)} collective-permute-done((bf16[392,768]{1,0:T(8,128)(2,1)S(1)}, bf16[392,768]{1,0:T(8,128)(2,1)S(1)}, u32[]{:S(2)}, u32[]{:S(2)}) %collective-permute-start.3) | collective-permute-done | bytes 602144 | tf_op jit(solution)/shard_map/ppermute | solution.py:264
  18.0 1.5 %collective-permute-done.ref.refs_3_ = bf16[392,768]{1,0:T(8,128)(2,1)S(1)} collective-permute-done((bf16[392,768]{1,0:T(8,128)(2,1)S(1)}, bf16[392,768]{1,0:T(8,128)(2,1)S(1)}, u32[]{:S(2)}, u32[]{:S(2)}) %collective-permute-start) | collective-permute-done | bytes 602144 | tf_op jit(solution)/shard_map/ppermute | solution.py:264
  19.5 0.4 collective-permute-start.1
  20.0 0.2 collective-permute-start.9
  20.1 1.6 %collective-permute-start.4 = (bf16[136,768]{1,0:T(8,128)(2,1)S(1)}, bf16[136,768]{1,0:T(8,128)(2,1)S(1)}, u32[]{:S(2)}, u32[]{:S(2)}) collective-permute-start(bf16[136,768]{1,0:T(8,128)(2,1)S(1)} %piece.3), channel_id=1, source_target_pairs={{0,2},{1,3},{2,0},{3,1},{4,6},{5,7},{6,4},{7,5},{8,10},{9,11},{10,... | collective-permute-start | bytes 626696 | tf_op jit(solution)/shard_map/ppermute | solution.py:264
  21.7 8.2 %collective-permute-done.1.refs_0_.refs_7_ = bf16[264,768]{1,0:T(8,128)(2,1)S(1)} collective-permute-done((bf16[264,768]{1,0:T(8,128)(2,1)S(1)}, bf16[264,768]{1,0:T(8,128)(2,1)S(1)}, u32[]{:S(2)}, u32[]{:S(2)}) %collective-permute-start.1) | collective-permute-done | bytes 405536 | tf_op jit(solution)/shard_map/ppermute | solution.py:264
  29.9 4.7 %collective-permute-start.12 = (bf16[264,768]{1,0:T(8,128)(2,1)S(1)}, bf16[264,768]{1,0:T(8,128)(2,1)S(1)}, u32[]{:S(2)}, u32[]{:S(2)}) collective-permute-start(bf16[264,768]{1,0:T(8,128)(2,1)S(1)} %get-tuple-element.74), channel_id=1, source_target_pairs={{0,16},{1,17},{2,18},{3,19},{4,20},{5,21},{6,22},{7,23},{24,8},{25... | collective-permute-start | bytes 1216520 | tf_op jit(solution)/shard_map/ppermute | solution.py:264
  34.7 0.8 %shard_map.28 = (f32[1,384]{1,0:T(1,128)S(1)}, f32[1,384]{1,0:T(1,128)S(1)}, f32[1,384]{1,0:T(1,128)S(1)}, f32[4,384]{1,0:T(4,128)S(1)}, f32[4,384]{1,0:T(4,128)S(1)}) custom-call(bf16[392,768]{1,0:T(8,128)(2,1)S(1)} %get-tuple-element.45.refs_0_.refs_2_.refs_1_, bf16[392,768]{1,0:T(8,128)(2,1)S(1)} %collective-permute-done.8.refs_1_.refs_2_), custom_call_target="tpu_custom_call" | custom-call | flops 472055808 | bytes 1179648 | tf_op jit(solution)/shard_map/pallas_call | solution.py:233
  35.5 1.3 %collective-permute-start.7 = (bf16[136,768]{1,0:T(8,128)(2,1)S(1)}, bf16[136,768]{1,0:T(8,128)(2,1)S(1)}, u32[]{:S(2)}, u32[]{:S(2)}) collective-permute-start(bf16[136,768]{1,0:T(8,128)(2,1)S(1)} %get-tuple-element.46), channel_id=1, source_target_pairs={{0,16},{1,17},{2,18},{3,19},{4,20},{5,21},{6,22},{7,23},{24,8},{25... | collective-permute-start | bytes 626696 | tf_op jit(solution)/shard_map/ppermute | solution.py:264
  36.8 0.3 collective-permute-start.5
  37.1 1.8 %shard_map.29 = (f32[1,384]{1,0:T(1,128)S(1)}, f32[1,384]{1,0:T(1,128)S(1)}, f32[1,384]{1,0:T(1,128)S(1)}, f32[4,384]{1,0:T(4,128)S(1)}, f32[4,384]{1,0:T(4,128)S(1)}) custom-call(bf16[392,768]{1,0:T(8,128)(2,1)S(1)} %get-tuple-element.45.refs_0_.refs_2_.refs_1_, bf16[392,768]{1,0:T(8,128)(2,1)S(1)} %collective-permute-done.8.refs_1_.refs_2_, ...), custom_call_target="tpu_custom_call" | custom-call | flops 1416167424 | bytes 2949120 | tf_op jit(solution)/shard_map/pallas_call | solution.py:233
  38.9 1.2 %shard_map.30 = (f32[1,384]{1,0:T(1,128)S(1)}, f32[1,384]{1,0:T(1,128)S(1)}, f32[1,384]{1,0:T(1,128)S(1)}, f32[4,384]{1,0:T(4,128)S(1)}, f32[4,384]{1,0:T(4,128)S(1)}) custom-call(bf16[392,768]{1,0:T(8,128)(2,1)S(1)} %collective-permute-done.9.refs_0_.refs_5_, bf16[392,768]{1,0:T(8,128)(2,1)S(1)} %collective-permute-done.10.refs_1_.refs_6_, ...), custom_call_target="tpu_custom_call" | custom-call | flops 944111616 | bytes 2359296 | tf_op jit(solution)/shard_map/pallas_call | solution.py:233
  40.2 8.3 %collective-permute-done.7.refs_0_.refs_4_ = bf16[136,768]{1,0:T(8,128)(2,1)S(1)} collective-permute-done((bf16[136,768]{1,0:T(8,128)(2,1)S(1)}, bf16[136,768]{1,0:T(8,128)(2,1)S(1)}, u32[]{:S(2)}, u32[]{:S(2)}) %collective-permute-start.7) | collective-permute-done | bytes 208928 | tf_op jit(solution)/shard_map/ppermute | solution.py:264
  48.4 0.1 shard_map.31
  48.6 1.0 %shard_map.32 = (f32[1,384]{1,0:T(1,128)S(1)}, f32[1,384]{1,0:T(1,128)S(1)}, f32[1,384]{1,0:T(1,128)S(1)}, f32[4,384]{1,0:T(4,128)S(1)}, f32[4,384]{1,0:T(4,128)S(1)}) custom-call(bf16[264,768]{1,0:T(8,128)(2,1)S(1)} %collective-permute-done.1.refs_0_.refs_7_, bf16[136,768]{1,0:T(8,128)(2,1)S(1)} %collective-permute-done.4.refs_1_.refs_8_, ...), custom_call_target="tpu_custom_call" | custom-call | flops 565248000 | bytes 2949120 | tf_op jit(solution)/shard_map/pallas_call | solution.py:233
  49.6 1.0 %shard_map.33 = (f32[1,384]{1,0:T(1,128)S(1)}, f32[1,384]{1,0:T(1,128)S(1)}, f32[1,384]{1,0:T(1,128)S(1)}, f32[4,384]{1,0:T(4,128)S(1)}, f32[4,384]{1,0:T(4,128)S(1)}) custom-call(bf16[264,768]{1,0:T(8,128)(2,1)S(1)} %collective-permute-done.2.refs_0_.refs_9_, bf16[136,768]{1,0:T(8,128)(2,1)S(1)} %collective-permute-done.5.refs_1_.refs_10_, ...), custom_call_target="tpu_custom_call" | custom-call | flops 565248000 | bytes 2949120 | tf_op jit(solution)/shard_map/pallas_call | solution.py:233
  50.6 0.1 shard_map.34
  50.7 0.1 collective-permute-start.14
  50.8 1.4 %collective-permute-start.11 = (f32[1,384]{1,0:T(1,128)S(1)}, f32[1,384]{1,0:T(1,128)S(1)}, u32[]{:S(2)}, u32[]{:S(2)}) collective-permute-start(f32[1,384]{1,0:T(1,128)S(1)} %get-tuple-element.73), channel_id=1, source_target_pairs={{0,24},{1,25},{2,26},{3,27},{4,28},{5,29},{6,30},{7,31},{8,0},{9,1... | collective-permute-start | bytes 4616 | tf_op jit(solution)/shard_map/ppermute | solution.py:264
  52.2 3.9 %collective-permute-start.13 = (f32[1,384]{1,0:T(1,128)S(1)}, f32[1,384]{1,0:T(1,128)S(1)}, u32[]{:S(2)}, u32[]{:S(2)}) collective-permute-start(f32[1,384]{1,0:T(1,128)S(1)} %get-tuple-element.78), channel_id=1, source_target_pairs={{0,8},{1,9},{2,10},{3,11},{4,12},{5,13},{6,14},{7,15},{8,24},{9,25... | collective-permute-start | bytes 4616 | tf_op jit(solution)/shard_map/ppermute | solution.py:264
  56.1 1.6 %collective-permute-start.15 = (f32[1,384]{1,0:T(1,128)S(1)}, f32[1,384]{1,0:T(1,128)S(1)}, u32[]{:S(2)}, u32[]{:S(2)}) collective-permute-start(f32[1,384]{1,0:T(1,128)S(1)} %get-tuple-element.82), channel_id=1, source_target_pairs={{2,0},{3,1},{0,2},{1,3},{6,4},{7,5},{4,6},{5,7},{10,8},{11,9},{8,1... | collective-permute-start | bytes 4616 | tf_op jit(solution)/shard_map/ppermute | solution.py:264
  57.7 1.5 %collective-permute-start.16 = (f32[1,384]{1,0:T(1,128)S(1)}, f32[1,384]{1,0:T(1,128)S(1)}, u32[]{:S(2)}, u32[]{:S(2)}) collective-permute-start(f32[1,384]{1,0:T(1,128)S(1)} %get-tuple-element.83), channel_id=1, source_target_pairs={{4,0},{5,1},{6,2},{7,3},{0,4},{1,5},{2,6},{3,7},{12,8},{13,9},{14,... | collective-permute-start | bytes 4616 | tf_op jit(solution)/shard_map/ppermute | solution.py:264
  59.2 0.5 collective-permute-start.17
  59.7 0.1 collective-permute-done.15
  59.8 1.5 %collective-permute-done.16 = f32[1,384]{1,0:T(1,128)S(1)} collective-permute-done((f32[1,384]{1,0:T(1,128)S(1)}, f32[1,384]{1,0:T(1,128)S(1)}, u32[]{:S(2)}, u32[]{:S(2)}) %collective-permute-start.16) | collective-permute-done | bytes 1568 | tf_op jit(solution)/shard_map/ppermute | solution.py:264
  61.3 2.4 %collective-permute-done.17 = f32[1,384]{1,0:T(1,128)S(1)} collective-permute-done((f32[1,384]{1,0:T(1,128)S(1)}, f32[1,384]{1,0:T(1,128)S(1)}, u32[]{:S(2)}, u32[]{:S(2)}) %collective-permute-start.17) | collective-permute-done | bytes 1568 | tf_op jit(solution)/shard_map/ppermute | solution.py:264
  63.7 0.6 maximum_reduce_fusion
  (16 shorter events, 0.1 us)
Async XLA Ops:
  1.4 16.7 %collective-permute-start.3 = (bf16[392,768]{1,0:T(8,128)(2,1)S(1)}, bf16[392,768]{1,0:T(8,128)(2,1)S(1)}, u32[]{:S(2)}, u32[]{:S(2)}) collective-permute-start(bf16[392,768]{1,0:T(8,128)(2,1)S(1)} %get-tuple-element.45.refs_0_.refs_2_.refs_1_), channel_id=1, source_target_pairs={{0,4},{1,5},{2,6},{3,7},{4,0},{5,1},{6,2},{7,3},{8,12},{9,13},{10,... | collective-permute-start | bytes 1806344 | tf_op jit(solution)/shard_map/ppermute | solution.py:264
  4.5 15.1 %collective-permute-start = (bf16[392,768]{1,0:T(8,128)(2,1)S(1)}, bf16[392,768]{1,0:T(8,128)(2,1)S(1)}, u32[]{:S(2)}, u32[]{:S(2)}) collective-permute-start(bf16[392,768]{1,0:T(8,128)(2,1)S(1)} %get-tuple-element.45.refs_0_.refs_2_.refs_1_), channel_id=1, source_target_pairs={{0,2},{1,3},{2,0},{3,1},{4,6},{5,7},{6,4},{7,5},{8,10},{9,11},{10,... | collective-permute-start | bytes 1806344 | tf_op jit(solution)/shard_map/ppermute | solution.py:264
  5.9 14.2 %collective-permute-start.8 = (bf16[392,768]{1,0:T(8,128)(2,1)S(1)}, bf16[392,768]{1,0:T(8,128)(2,1)S(1)}, u32[]{:S(2)}, u32[]{:S(2)}) collective-permute-start(bf16[392,768]{1,0:T(8,128)(2,1)S(1)} %get-tuple-element.45.refs_0_.refs_2_.refs_1_), channel_id=1, source_target_pairs={{0,1},{1,0},{2,3},{3,2},{4,5},{5,4},{6,7},{7,6},{8,9},{9,8},{10,11... | collective-permute-start | bytes 1806344 | tf_op jit(solution)/shard_map/ppermute | solution.py:264
  5.9 24.0 %collective-permute-start.6 = (bf16[392,768]{1,0:T(8,128)(2,1)S(1)}, bf16[392,768]{1,0:T(8,128)(2,1)S(1)}, u32[]{:S(2)}, u32[]{:S(2)}) collective-permute-start(bf16[392,768]{1,0:T(8,128)(2,1)S(1)} %get-tuple-element.45.refs_0_.refs_2_.refs_1_), channel_id=1, source_target_pairs={{0,8},{1,9},{2,10},{3,11},{4,12},{5,13},{6,14},{7,15},{8,16},{9,17... | collective-permute-start | bytes 1806344 | tf_op jit(solution)/shard_map/ppermute | solution.py:264
  18.0 18.8 %collective-permute-start.10 = (bf16[392,768]{1,0:T(8,128)(2,1)S(1)}, bf16[392,768]{1,0:T(8,128)(2,1)S(1)}, u32[]{:S(2)}, u32[]{:S(2)}) collective-permute-start(bf16[392,768]{1,0:T(8,128)(2,1)S(1)} %collective-permute-done.3.ref.refs_4_), channel_id=1, source_target_pairs={{0,1},{1,0},{2,3},{3,2},{4,5},{5,4},{6,7},{7,6},{8,9},{9,8},{10,11... | collective-permute-start | bytes 1806344 | tf_op jit(solution)/shard_map/ppermute | solution.py:264
  19.5 10.4 %collective-permute-start.1 = (bf16[264,768]{1,0:T(8,128)(2,1)S(1)}, bf16[264,768]{1,0:T(8,128)(2,1)S(1)}, u32[]{:S(2)}, u32[]{:S(2)}) collective-permute-start(bf16[264,768]{1,0:T(8,128)(2,1)S(1)} %piece.2), channel_id=1, source_target_pairs={{0,4},{1,5},{2,6},{3,7},{4,0},{5,1},{6,2},{7,3},{8,12},{9,13},{10,... | collective-permute-start | bytes 1216520 | tf_op jit(solution)/shard_map/ppermute | solution.py:264
  20.0 18.9 %collective-permute-start.9 = (bf16[392,768]{1,0:T(8,128)(2,1)S(1)}, bf16[392,768]{1,0:T(8,128)(2,1)S(1)}, u32[]{:S(2)}, u32[]{:S(2)}) collective-permute-start(bf16[392,768]{1,0:T(8,128)(2,1)S(1)} %collective-permute-done.ref.refs_3_), channel_id=1, source_target_pairs={{0,1},{1,0},{2,3},{3,2},{4,5},{5,4},{6,7},{7,6},{8,9},{9,8},{10,11... | collective-permute-start | bytes 1806344 | tf_op jit(solution)/shard_map/ppermute | solution.py:264
  20.1 15.3 %collective-permute-start.4 = (bf16[136,768]{1,0:T(8,128)(2,1)S(1)}, bf16[136,768]{1,0:T(8,128)(2,1)S(1)}, u32[]{:S(2)}, u32[]{:S(2)}) collective-permute-start(bf16[136,768]{1,0:T(8,128)(2,1)S(1)} %piece.3), channel_id=1, source_target_pairs={{0,2},{1,3},{2,0},{3,1},{4,6},{5,7},{6,4},{7,5},{8,10},{9,11},{10,... | collective-permute-start | bytes 626696 | tf_op jit(solution)/shard_map/ppermute | solution.py:264
  29.9 19.6 %collective-permute-start.2 = (bf16[264,768]{1,0:T(8,128)(2,1)S(1)}, bf16[264,768]{1,0:T(8,128)(2,1)S(1)}, u32[]{:S(2)}, u32[]{:S(2)}) collective-permute-start(bf16[264,768]{1,0:T(8,128)(2,1)S(1)} %collective-permute-done.1.refs_0_.refs_7_), channel_id=1, source_target_pairs={{0,1},{1,0},{2,3},{3,2},{4,5},{5,4},{6,7},{7,6},{8,9},{9,8},{10,11... | collective-permute-start | bytes 1216520 | tf_op jit(solution)/shard_map/ppermute | solution.py:264
  29.9 20.6 %collective-permute-start.12 = (bf16[264,768]{1,0:T(8,128)(2,1)S(1)}, bf16[264,768]{1,0:T(8,128)(2,1)S(1)}, u32[]{:S(2)}, u32[]{:S(2)}) collective-permute-start(bf16[264,768]{1,0:T(8,128)(2,1)S(1)} %get-tuple-element.74), channel_id=1, source_target_pairs={{0,16},{1,17},{2,18},{3,19},{4,20},{5,21},{6,22},{7,23},{24,8},{25... | collective-permute-start | bytes 1216520 | tf_op jit(solution)/shard_map/ppermute | solution.py:264
  35.5 12.9 %collective-permute-start.7 = (bf16[136,768]{1,0:T(8,128)(2,1)S(1)}, bf16[136,768]{1,0:T(8,128)(2,1)S(1)}, u32[]{:S(2)}, u32[]{:S(2)}) collective-permute-start(bf16[136,768]{1,0:T(8,128)(2,1)S(1)} %get-tuple-element.46), channel_id=1, source_target_pairs={{0,16},{1,17},{2,18},{3,19},{4,20},{5,21},{6,22},{7,23},{24,8},{25... | collective-permute-start | bytes 626696 | tf_op jit(solution)/shard_map/ppermute | solution.py:264
  36.8 12.7 %collective-permute-start.5 = (bf16[136,768]{1,0:T(8,128)(2,1)S(1)}, bf16[136,768]{1,0:T(8,128)(2,1)S(1)}, u32[]{:S(2)}, u32[]{:S(2)}) collective-permute-start(bf16[136,768]{1,0:T(8,128)(2,1)S(1)} %collective-permute-done.4.refs_1_.refs_8_), channel_id=1, source_target_pairs={{0,1},{1,0},{2,3},{3,2},{4,5},{5,4},{6,7},{7,6},{8,9},{9,8},{10,11... | collective-permute-start | bytes 626696 | tf_op jit(solution)/shard_map/ppermute | solution.py:264
  50.7 5.4 %collective-permute-start.14 = (f32[4,384]{1,0:T(4,128)S(1)}, f32[4,384]{1,0:T(4,128)S(1)}, u32[]{:S(2)}, u32[]{:S(2)}) collective-permute-start(f32[4,384]{1,0:T(4,128)S(1)} %get-tuple-element.80), channel_id=1, source_target_pairs={{0,1},{1,0},{2,3},{3,2},{4,5},{5,4},{6,7},{7,6},{8,9},{9,8},{10,11... | collective-permute-start | bytes 18440 | tf_op jit(solution)/shard_map/ppermute | solution.py:264
  50.8 8.9 %collective-permute-start.11 = (f32[1,384]{1,0:T(1,128)S(1)}, f32[1,384]{1,0:T(1,128)S(1)}, u32[]{:S(2)}, u32[]{:S(2)}) collective-permute-start(f32[1,384]{1,0:T(1,128)S(1)} %get-tuple-element.73), channel_id=1, source_target_pairs={{0,24},{1,25},{2,26},{3,27},{4,28},{5,29},{6,30},{7,31},{8,0},{9,1... | collective-permute-start | bytes 4616 | tf_op jit(solution)/shard_map/ppermute | solution.py:264
  52.2 7.5 %collective-permute-start.13 = (f32[1,384]{1,0:T(1,128)S(1)}, f32[1,384]{1,0:T(1,128)S(1)}, u32[]{:S(2)}, u32[]{:S(2)}) collective-permute-start(f32[1,384]{1,0:T(1,128)S(1)} %get-tuple-element.78), channel_id=1, source_target_pairs={{0,8},{1,9},{2,10},{3,11},{4,12},{5,13},{6,14},{7,15},{8,24},{9,25... | collective-permute-start | bytes 4616 | tf_op jit(solution)/shard_map/ppermute | solution.py:264
  56.1 3.6 %collective-permute-start.15 = (f32[1,384]{1,0:T(1,128)S(1)}, f32[1,384]{1,0:T(1,128)S(1)}, u32[]{:S(2)}, u32[]{:S(2)}) collective-permute-start(f32[1,384]{1,0:T(1,128)S(1)} %get-tuple-element.82), channel_id=1, source_target_pairs={{2,0},{3,1},{0,2},{1,3},{6,4},{7,5},{4,6},{5,7},{10,8},{11,9},{8,1... | collective-permute-start | bytes 4616 | tf_op jit(solution)/shard_map/ppermute | solution.py:264
  57.7 3.6 %collective-permute-start.16 = (f32[1,384]{1,0:T(1,128)S(1)}, f32[1,384]{1,0:T(1,128)S(1)}, u32[]{:S(2)}, u32[]{:S(2)}) collective-permute-start(f32[1,384]{1,0:T(1,128)S(1)} %get-tuple-element.83), channel_id=1, source_target_pairs={{4,0},{5,1},{6,2},{7,3},{0,4},{1,5},{2,6},{3,7},{12,8},{13,9},{14,... | collective-permute-start | bytes 4616 | tf_op jit(solution)/shard_map/ppermute | solution.py:264
  59.2 4.5 %collective-permute-start.17 = (f32[1,384]{1,0:T(1,128)S(1)}, f32[1,384]{1,0:T(1,128)S(1)}, u32[]{:S(2)}, u32[]{:S(2)}) collective-permute-start(f32[1,384]{1,0:T(1,128)S(1)} %get-tuple-element.84), channel_id=1, source_target_pairs={{6,0},{7,1},{4,2},{5,3},{2,4},{3,5},{0,6},{1,7},{14,8},{15,9},{12,... | collective-permute-start | bytes 4616 | tf_op jit(solution)/shard_map/ppermute | solution.py:264

commit v8 on v7

--- a/solution.py
+++ b/solution.py
@@ -50,14 +50,11 @@
             maps.append({i: (i + step) % self.lines for i in range(self.lines)})
         if self.lines % 2 == 0:
             half = self.lines // 2
-            maps.append({(i if i % 2 == 0 else i + half): (i + half if i % 2 == 0 else i) for i in range(half)})
+            maps.append({(i + half if i % 2 == 0 else i): (i if i % 2 == 0 else i + half) for i in range(half)})
         return maps
 
     def line_move(self, line_map):
         return self.pairs(lambda l, y, x, c: (line_map[l], y, x, c) if l in line_map else None)
-
-    def line_hops(self):
-        return [{(b - 1) % self.lines: b for b in m.values()} for m in self.line_maps()]
 
     def line_return(self, line_map):
         back = {b: a for a, b in line_map.items()}
@@ -271,10 +268,7 @@
         swap = layout.swap()
 
         own, *parts = pack(embeddings, doc_order, pieces)
-        line = [[own]]
-        for hop in layout.line_hops()[:-1]:
-            line.append([send(line[-1][0], layout.line_move(hop))])
-        line = line[1:]
+        line = [[send(own, layout.line_move(m))] for m in maps[:-1]]
         line.append([send(part, layout.line_move(maps[-1])) for part in parts])
         plane = [send(own, layout.plane_move(*d)) for d in offsets[:-1]]
 

time: 64.5 us -> 66.5 us (1.031)
  starting transfers between devices: 23.6 us -> 18.9 us
  waiting for transfers between devices: 32.5 us -> 36.2 us
  Pallas kernels: 7.51 us -> 10.4 us
    ppermute x18, starting transfers between devices: 23.6 us -> 18.9 us  [send(): return lax.ppermute(value, AXES, pairs)]
    ppermute x18, waiting for transfers between devices: 32.5 us -> 36.2 us  [send(): return lax.ppermute(value, AXES, pairs)]
    pallas_call x7, Pallas kernels: 6.08 us -> 8.94 us  [match(): pl.pallas_call(functools.partial(match_body, plan, groups, len(blocks), s...]
  transfers between devices with their start and end apart: 18 -> 18, of which waited for: 7 -> 7; matrix products, arithmetic and copies ran while one was open for 0% -> 0% of each run, Pallas kernels for 9% -> 11%
where the time goes in v8:
time: 66.5 us; the launch traced here: 66.3 us
  waiting for transfers between devices  36.2 us (54%)
  starting transfers between devices  18.9 us (28%)
  Pallas kernels  10.4 us (16%)
    ppermute x18, waiting for transfers between devices, send(): return lax.ppermute(value, AXES, pairs)  36.2 us
    ppermute x18, starting transfers between devices, send(): return lax.ppermute(value, AXES, pairs)  18.9 us
    pallas_call x7, Pallas kernels, match(): pl.pallas_call(functools.partial(match_body, plan, groups, len(blocks), s...  8.94 us
    pallas_call x1, Pallas kernels, pack(): call(*(pltpu.with_memory_space_constraint(v, pltpu.HBM) for v in (embeddi...  1.38 us
  transfers between devices with their start and end apart: 18, of which 7 were waited for; matrix products, arithmetic and copies ran while one was open for 0% of the time, Pallas kernels for 11%

profile of v8, /device:TPU:0, one launch (start us, length us, event | category | flops | bytes accessed | tf_op | source)
XLA Modules:
  0.0 66.3 jit_solution(3374301660399935942)
XLA Ops:
  0.0 1.4 %pack.1 = (bf16[392,768]{1,0:T(8,128)(2,1)S(1)}, bf16[136,768]{1,0:T(8,128)(2,1)S(1)}, bf16[264,768]{1,0:T(8,128)(2,1)S(1)}) custom-call(bf16[384,768]{1,0:T(8,128)(2,1)} %emb_hbm.1, s32[384]{0:T(512)} %order_hbm.1), custom_call_target="tpu_custom_call" | custom-call | tf_op jit(solution)/shard_map/pack/pallas_call | solution.py:113
  1.4 3.1 %collective-permute-start.3 = (bf16[392,768]{1,0:T(8,128)(2,1)S(1)}, bf16[392,768]{1,0:T(8,128)(2,1)S(1)}, u32[]{:S(2)}, u32[]{:S(2)}) collective-permute-start(bf16[392,768]{1,0:T(8,128)(2,1)S(1)} %get-tuple-element.45.refs_0_.refs_2_.refs_1_), channel_id=1, source_target_pairs={{0,4},{1,5},{2,6},{3,7},{4,0},{5,1},{6,2},{7,3},{8,12},{9,13},{10,... | collective-permute-start | bytes 1806344 | tf_op jit(solution)/shard_map/ppermute | solution.py:261
  4.5 1.5 %collective-permute-start = (bf16[392,768]{1,0:T(8,128)(2,1)S(1)}, bf16[392,768]{1,0:T(8,128)(2,1)S(1)}, u32[]{:S(2)}, u32[]{:S(2)}) collective-permute-start(bf16[392,768]{1,0:T(8,128)(2,1)S(1)} %get-tuple-element.45.refs_0_.refs_2_.refs_1_), channel_id=1, source_target_pairs={{0,2},{1,3},{2,0},{3,1},{4,6},{5,7},{6,4},{7,5},{8,10},{9,11},{10,... | collective-permute-start | bytes 1806344 | tf_op jit(solution)/shard_map/ppermute | solution.py:261
  5.9 0.0 collective-permute-start.8
  5.9 1.6 %collective-permute-start.6 = (bf16[392,768]{1,0:T(8,128)(2,1)S(1)}, bf16[392,768]{1,0:T(8,128)(2,1)S(1)}, u32[]{:S(2)}, u32[]{:S(2)}) collective-permute-start(bf16[392,768]{1,0:T(8,128)(2,1)S(1)} %get-tuple-element.45.refs_0_.refs_2_.refs_1_), channel_id=1, source_target_pairs={{0,8},{1,9},{2,10},{3,11},{4,12},{5,13},{6,14},{7,15},{8,16},{9,17... | collective-permute-start | bytes 1806344 | tf_op jit(solution)/shard_map/ppermute | solution.py:261
  7.5 10.5 %collective-permute-done.3.ref.refs_4_ = bf16[392,768]{1,0:T(8,128)(2,1)S(1)} collective-permute-done((bf16[392,768]{1,0:T(8,128)(2,1)S(1)}, bf16[392,768]{1,0:T(8,128)(2,1)S(1)}, u32[]{:S(2)}, u32[]{:S(2)}) %collective-permute-start.3) | collective-permute-done | bytes 602144 | tf_op jit(solution)/shard_map/ppermute | solution.py:261
  18.0 1.5 %collective-permute-done.ref.refs_3_ = bf16[392,768]{1,0:T(8,128)(2,1)S(1)} collective-permute-done((bf16[392,768]{1,0:T(8,128)(2,1)S(1)}, bf16[392,768]{1,0:T(8,128)(2,1)S(1)}, u32[]{:S(2)}, u32[]{:S(2)}) %collective-permute-start) | collective-permute-done | bytes 602144 | tf_op jit(solution)/shard_map/ppermute | solution.py:261
  19.5 0.4 collective-permute-start.1
  20.0 0.2 collective-permute-start.9
  20.1 1.6 %collective-permute-start.4 = (bf16[136,768]{1,0:T(8,128)(2,1)S(1)}, bf16[136,768]{1,0:T(8,128)(2,1)S(1)}, u32[]{:S(2)}, u32[]{:S(2)}) collective-permute-start(bf16[136,768]{1,0:T(8,128)(2,1)S(1)} %piece.3), channel_id=1, source_target_pairs={{0,2},{1,3},{2,0},{3,1},{4,6},{5,7},{6,4},{7,5},{8,10},{9,11},{10,... | collective-permute-start | bytes 626696 | tf_op jit(solution)/shard_map/ppermute | solution.py:261
  21.7 8.2 %collective-permute-done.1.refs_0_.refs_7_ = bf16[264,768]{1,0:T(8,128)(2,1)S(1)} collective-permute-done((bf16[264,768]{1,0:T(8,128)(2,1)S(1)}, bf16[264,768]{1,0:T(8,128)(2,1)S(1)}, u32[]{:S(2)}, u32[]{:S(2)}) %collective-permute-start.1) | collective-permute-done | bytes 405536 | tf_op jit(solution)/shard_map/ppermute | solution.py:261
  29.9 1.3 %collective-permute-start.12 = (bf16[264,768]{1,0:T(8,128)(2,1)S(1)}, bf16[264,768]{1,0:T(8,128)(2,1)S(1)}, u32[]{:S(2)}, u32[]{:S(2)}) collective-permute-start(bf16[264,768]{1,0:T(8,128)(2,1)S(1)} %get-tuple-element.74), channel_id=1, source_target_pairs={{8,24},{9,25},{10,26},{11,27},{12,28},{13,29},{14,30},{15,31},{16,... | collective-permute-start | bytes 1216520 | tf_op jit(solution)/shard_map/ppermute | solution.py:261
  31.2 0.8 %shard_map.28 = (f32[1,384]{1,0:T(1,128)S(1)}, f32[1,384]{1,0:T(1,128)S(1)}, f32[1,384]{1,0:T(1,128)S(1)}, f32[4,384]{1,0:T(4,128)S(1)}, f32[4,384]{1,0:T(4,128)S(1)}) custom-call(bf16[392,768]{1,0:T(8,128)(2,1)S(1)} %get-tuple-element.45.refs_0_.refs_2_.refs_1_, bf16[392,768]{1,0:T(8,128)(2,1)S(1)} %collective-permute-done.8.refs_1_.refs_2_), custom_call_target="tpu_custom_call" | custom-call | flops 472055808 | bytes 1179648 | tf_op jit(solution)/shard_map/pallas_call | solution.py:230
  32.1 1.3 %collective-permute-start.7 = (bf16[136,768]{1,0:T(8,128)(2,1)S(1)}, bf16[136,768]{1,0:T(8,128)(2,1)S(1)}, u32[]{:S(2)}, u32[]{:S(2)}) collective-permute-start(bf16[136,768]{1,0:T(8,128)(2,1)S(1)} %get-tuple-element.46), channel_id=1, source_target_pairs={{8,24},{9,25},{10,26},{11,27},{12,28},{13,29},{14,30},{15,31},{16,... | collective-permute-start | bytes 626696 | tf_op jit(solution)/shard_map/ppermute | solution.py:261
  33.4 0.6 collective-permute-start.5
  33.9 1.8 %shard_map.29 = (f32[1,384]{1,0:T(1,128)S(1)}, f32[1,384]{1,0:T(1,128)S(1)}, f32[1,384]{1,0:T(1,128)S(1)}, f32[4,384]{1,0:T(4,128)S(1)}, f32[4,384]{1,0:T(4,128)S(1)}) custom-call(bf16[392,768]{1,0:T(8,128)(2,1)S(1)} %get-tuple-element.45.refs_0_.refs_2_.refs_1_, bf16[392,768]{1,0:T(8,128)(2,1)S(1)} %collective-permute-done.8.refs_1_.refs_2_, ...), custom_call_target="tpu_custom_call" | custom-call | flops 1416167424 | bytes 2949120 | tf_op jit(solution)/shard_map/pallas_call | solution.py:230
  35.7 1.3 %shard_map.30 = (f32[1,384]{1,0:T(1,128)S(1)}, f32[1,384]{1,0:T(1,128)S(1)}, f32[1,384]{1,0:T(1,128)S(1)}, f32[4,384]{1,0:T(4,128)S(1)}, f32[4,384]{1,0:T(4,128)S(1)}) custom-call(bf16[392,768]{1,0:T(8,128)(2,1)S(1)} %collective-permute-done.9.refs_0_.refs_5_, bf16[392,768]{1,0:T(8,128)(2,1)S(1)} %collective-permute-done.10.refs_1_.refs_6_, ...), custom_call_target="tpu_custom_call" | custom-call | flops 944111616 | bytes 2359296 | tf_op jit(solution)/shard_map/pallas_call | solution.py:230
  37.0 12.0 %collective-permute-done.7.refs_0_.refs_4_ = bf16[136,768]{1,0:T(8,128)(2,1)S(1)} collective-permute-done((bf16[136,768]{1,0:T(8,128)(2,1)S(1)}, bf16[136,768]{1,0:T(8,128)(2,1)S(1)}, u32[]{:S(2)}, u32[]{:S(2)}) %collective-permute-start.7) | collective-permute-done | bytes 208928 | tf_op jit(solution)/shard_map/ppermute | solution.py:261
  49.0 1.4 %shard_map.31 = (f32[1,384]{1,0:T(1,128)S(1)}, f32[1,384]{1,0:T(1,128)S(1)}, f32[1,384]{1,0:T(1,128)S(1)}, f32[4,384]{1,0:T(4,128)S(1)}, f32[4,384]{1,0:T(4,128)S(1)}) custom-call(bf16[136,768]{1,0:T(8,128)(2,1)S(1)} %collective-permute-done.7.refs_0_.refs_4_, bf16[392,768]{1,0:T(8,128)(2,1)S(1)} %get-tuple-element.45.refs_0_.refs_2_.refs_1_, ...), custom_call_target="tpu_custom_call" | custom-call | flops 491323392 | bytes 4128768 | tf_op jit(solution)/shard_map/pallas_call | solution.py:230
  50.3 1.0 %shard_map.32 = (f32[1,384]{1,0:T(1,128)S(1)}, f32[1,384]{1,0:T(1,128)S(1)}, f32[1,384]{1,0:T(1,128)S(1)}, f32[4,384]{1,0:T(4,128)S(1)}, f32[4,384]{1,0:T(4,128)S(1)}) custom-call(bf16[264,768]{1,0:T(8,128)(2,1)S(1)} %collective-permute-done.1.refs_0_.refs_7_, bf16[136,768]{1,0:T(8,128)(2,1)S(1)} %collective-permute-done.4.refs_1_.refs_8_, ...), custom_call_target="tpu_custom_call" | custom-call | flops 565248000 | bytes 2949120 | tf_op jit(solution)/shard_map/pallas_call | solution.py:230
  51.4 1.0 %shard_map.33 = (f32[1,384]{1,0:T(1,128)S(1)}, f32[1,384]{1,0:T(1,128)S(1)}, f32[1,384]{1,0:T(1,128)S(1)}, f32[4,384]{1,0:T(4,128)S(1)}, f32[4,384]{1,0:T(4,128)S(1)}) custom-call(bf16[264,768]{1,0:T(8,128)(2,1)S(1)} %collective-permute-done.2.refs_0_.refs_9_, bf16[136,768]{1,0:T(8,128)(2,1)S(1)} %collective-permute-done.5.refs_1_.refs_10_, ...), custom_call_target="tpu_custom_call" | custom-call | flops 565248000 | bytes 2949120 | tf_op jit(solution)/shard_map/pallas_call | solution.py:230
  52.4 1.8 %shard_map.34 = (f32[1,384]{1,0:T(1,128)S(1)}, f32[4,384]{1,0:T(4,128)S(1)}, f32[4,384]{1,0:T(4,128)S(1)}) custom-call(bf16[264,768]{1,0:T(8,128)(2,1)S(1)} %collective-permute-done.12.refs_0_, bf16[392,768]{1,0:T(8,128)(2,1)S(1)} %get-tuple-element.45.refs_0_.refs_2_.refs_1_, bf16[392,768]{1,0:T(8,128)(2,1)S(1)} %collective-permute-done.8.refs_1_.refs_2_, ...), custom_call_target="tpu_custom_call" | custom-call | flops 1278148608 | bytes 6488064 | tf_op jit(solution)/shard_map/pallas_call | solution.py:230
  54.1 0.1 collective-permute-start.14
  54.2 3.9 %collective-permute-start.11 = (f32[1,384]{1,0:T(1,128)S(1)}, f32[1,384]{1,0:T(1,128)S(1)}, u32[]{:S(2)}, u32[]{:S(2)}) collective-permute-start(f32[1,384]{1,0:T(1,128)S(1)} %get-tuple-element.73), channel_id=1, source_target_pairs={{0,24},{1,25},{2,26},{3,27},{4,28},{5,29},{6,30},{7,31},{8,0},{9,1... | collective-permute-start | bytes 4616 | tf_op jit(solution)/shard_map/ppermute | solution.py:261
  58.1 1.6 %collective-permute-start.15 = (f32[1,384]{1,0:T(1,128)S(1)}, f32[1,384]{1,0:T(1,128)S(1)}, u32[]{:S(2)}, u32[]{:S(2)}) collective-permute-start(f32[1,384]{1,0:T(1,128)S(1)} %get-tuple-element.82), channel_id=1, source_target_pairs={{2,0},{3,1},{0,2},{1,3},{6,4},{7,5},{4,6},{5,7},{10,8},{11,9},{8,1... | collective-permute-start | bytes 4616 | tf_op jit(solution)/shard_map/ppermute | solution.py:261
  59.7 1.5 %collective-permute-start.16 = (f32[1,384]{1,0:T(1,128)S(1)}, f32[1,384]{1,0:T(1,128)S(1)}, u32[]{:S(2)}, u32[]{:S(2)}) collective-permute-start(f32[1,384]{1,0:T(1,128)S(1)} %get-tuple-element.83), channel_id=1, source_target_pairs={{4,0},{5,1},{6,2},{7,3},{0,4},{1,5},{2,6},{3,7},{12,8},{13,9},{14,... | collective-permute-start | bytes 4616 | tf_op jit(solution)/shard_map/ppermute | solution.py:261
  61.2 0.5 collective-permute-start.17
  61.7 0.0 collective-permute-done.13
  61.7 0.1 collective-permute-done.15
  61.8 1.5 %collective-permute-done.16 = f32[1,384]{1,0:T(1,128)S(1)} collective-permute-done((f32[1,384]{1,0:T(1,128)S(1)}, f32[1,384]{1,0:T(1,128)S(1)}, u32[]{:S(2)}, u32[]{:S(2)}) %collective-permute-start.16) | collective-permute-done | bytes 1568 | tf_op jit(solution)/shard_map/ppermute | solution.py:261
  63.2 2.4 %collective-permute-done.17 = f32[1,384]{1,0:T(1,128)S(1)} collective-permute-done((f32[1,384]{1,0:T(1,128)S(1)}, f32[1,384]{1,0:T(1,128)S(1)}, u32[]{:S(2)}, u32[]{:S(2)}) %collective-permute-start.17) | collective-permute-done | bytes 1568 | tf_op jit(solution)/shard_map/ppermute | solution.py:261
  65.7 0.6 maximum_reduce_fusion
  (16 shorter events, 0.1 us)
Async XLA Ops:
  1.4 16.7 %collective-permute-start.3 = (bf16[392,768]{1,0:T(8,128)(2,1)S(1)}, bf16[392,768]{1,0:T(8,128)(2,1)S(1)}, u32[]{:S(2)}, u32[]{:S(2)}) collective-permute-start(bf16[392,768]{1,0:T(8,128)(2,1)S(1)} %get-tuple-element.45.refs_0_.refs_2_.refs_1_), channel_id=1, source_target_pairs={{0,4},{1,5},{2,6},{3,7},{4,0},{5,1},{6,2},{7,3},{8,12},{9,13},{10,... | collective-permute-start | bytes 1806344 | tf_op jit(solution)/shard_map/ppermute | solution.py:261
  4.5 15.1 %collective-permute-start = (bf16[392,768]{1,0:T(8,128)(2,1)S(1)}, bf16[392,768]{1,0:T(8,128)(2,1)S(1)}, u32[]{:S(2)}, u32[]{:S(2)}) collective-permute-start(bf16[392,768]{1,0:T(8,128)(2,1)S(1)} %get-tuple-element.45.refs_0_.refs_2_.refs_1_), channel_id=1, source_target_pairs={{0,2},{1,3},{2,0},{3,1},{4,6},{5,7},{6,4},{7,5},{8,10},{9,11},{10,... | collective-permute-start | bytes 1806344 | tf_op jit(solution)/shard_map/ppermute | solution.py:261
  5.9 14.2 %collective-permute-start.8 = (bf16[392,768]{1,0:T(8,128)(2,1)S(1)}, bf16[392,768]{1,0:T(8,128)(2,1)S(1)}, u32[]{:S(2)}, u32[]{:S(2)}) collective-permute-start(bf16[392,768]{1,0:T(8,128)(2,1)S(1)} %get-tuple-element.45.refs_0_.refs_2_.refs_1_), channel_id=1, source_target_pairs={{0,1},{1,0},{2,3},{3,2},{4,5},{5,4},{6,7},{7,6},{8,9},{9,8},{10,11... | collective-permute-start | bytes 1806344 | tf_op jit(solution)/shard_map/ppermute | solution.py:261
  5.9 24.0 %collective-permute-start.6 = (bf16[392,768]{1,0:T(8,128)(2,1)S(1)}, bf16[392,768]{1,0:T(8,128)(2,1)S(1)}, u32[]{:S(2)}, u32[]{:S(2)}) collective-permute-start(bf16[392,768]{1,0:T(8,128)(2,1)S(1)} %get-tuple-element.45.refs_0_.refs_2_.refs_1_), channel_id=1, source_target_pairs={{0,8},{1,9},{2,10},{3,11},{4,12},{5,13},{6,14},{7,15},{8,16},{9,17... | collective-permute-start | bytes 1806344 | tf_op jit(solution)/shard_map/ppermute | solution.py:261
  18.0 15.3 %collective-permute-start.10 = (bf16[392,768]{1,0:T(8,128)(2,1)S(1)}, bf16[392,768]{1,0:T(8,128)(2,1)S(1)}, u32[]{:S(2)}, u32[]{:S(2)}) collective-permute-start(bf16[392,768]{1,0:T(8,128)(2,1)S(1)} %collective-permute-done.3.ref.refs_4_), channel_id=1, source_target_pairs={{0,1},{1,0},{2,3},{3,2},{4,5},{5,4},{6,7},{7,6},{8,9},{9,8},{10,11... | collective-permute-start | bytes 1806344 | tf_op jit(solution)/shard_map/ppermute | solution.py:261
  19.5 10.4 %collective-permute-start.1 = (bf16[264,768]{1,0:T(8,128)(2,1)S(1)}, bf16[264,768]{1,0:T(8,128)(2,1)S(1)}, u32[]{:S(2)}, u32[]{:S(2)}) collective-permute-start(bf16[264,768]{1,0:T(8,128)(2,1)S(1)} %piece.2), channel_id=1, source_target_pairs={{0,4},{1,5},{2,6},{3,7},{4,0},{5,1},{6,2},{7,3},{8,12},{9,13},{10,... | collective-permute-start | bytes 1216520 | tf_op jit(solution)/shard_map/ppermute | solution.py:261
  20.0 15.8 %collective-permute-start.9 = (bf16[392,768]{1,0:T(8,128)(2,1)S(1)}, bf16[392,768]{1,0:T(8,128)(2,1)S(1)}, u32[]{:S(2)}, u32[]{:S(2)}) collective-permute-start(bf16[392,768]{1,0:T(8,128)(2,1)S(1)} %collective-permute-done.ref.refs_3_), channel_id=1, source_target_pairs={{0,1},{1,0},{2,3},{3,2},{4,5},{5,4},{6,7},{7,6},{8,9},{9,8},{10,11... | collective-permute-start | bytes 1806344 | tf_op jit(solution)/shard_map/ppermute | solution.py:261
  20.1 11.9 %collective-permute-start.4 = (bf16[136,768]{1,0:T(8,128)(2,1)S(1)}, bf16[136,768]{1,0:T(8,128)(2,1)S(1)}, u32[]{:S(2)}, u32[]{:S(2)}) collective-permute-start(bf16[136,768]{1,0:T(8,128)(2,1)S(1)} %piece.3), channel_id=1, source_target_pairs={{0,2},{1,3},{2,0},{3,1},{4,6},{5,7},{6,4},{7,5},{8,10},{9,11},{10,... | collective-permute-start | bytes 626696 | tf_op jit(solution)/shard_map/ppermute | solution.py:261
  29.9 21.4 %collective-permute-start.2 = (bf16[264,768]{1,0:T(8,128)(2,1)S(1)}, bf16[264,768]{1,0:T(8,128)(2,1)S(1)}, u32[]{:S(2)}, u32[]{:S(2)}) collective-permute-start(bf16[264,768]{1,0:T(8,128)(2,1)S(1)} %collective-permute-done.1.refs_0_.refs_7_), channel_id=1, source_target_pairs={{0,1},{1,0},{2,3},{3,2},{4,5},{5,4},{6,7},{7,6},{8,9},{9,8},{10,11... | collective-permute-start | bytes 1216520 | tf_op jit(solution)/shard_map/ppermute | solution.py:261
  29.9 22.4 %collective-permute-start.12 = (bf16[264,768]{1,0:T(8,128)(2,1)S(1)}, bf16[264,768]{1,0:T(8,128)(2,1)S(1)}, u32[]{:S(2)}, u32[]{:S(2)}) collective-permute-start(bf16[264,768]{1,0:T(8,128)(2,1)S(1)} %get-tuple-element.74), channel_id=1, source_target_pairs={{8,24},{9,25},{10,26},{11,27},{12,28},{13,29},{14,30},{15,31},{16,... | collective-permute-start | bytes 1216520 | tf_op jit(solution)/shard_map/ppermute | solution.py:261
  32.1 16.9 %collective-permute-start.7 = (bf16[136,768]{1,0:T(8,128)(2,1)S(1)}, bf16[136,768]{1,0:T(8,128)(2,1)S(1)}, u32[]{:S(2)}, u32[]{:S(2)}) collective-permute-start(bf16[136,768]{1,0:T(8,128)(2,1)S(1)} %get-tuple-element.46), channel_id=1, source_target_pairs={{8,24},{9,25},{10,26},{11,27},{12,28},{13,29},{14,30},{15,31},{16,... | collective-permute-start | bytes 626696 | tf_op jit(solution)/shard_map/ppermute | solution.py:261
  33.4 18.0 %collective-permute-start.5 = (bf16[136,768]{1,0:T(8,128)(2,1)S(1)}, bf16[136,768]{1,0:T(8,128)(2,1)S(1)}, u32[]{:S(2)}, u32[]{:S(2)}) collective-permute-start(bf16[136,768]{1,0:T(8,128)(2,1)S(1)} %collective-permute-done.4.refs_1_.refs_8_), channel_id=1, source_target_pairs={{0,1},{1,0},{2,3},{3,2},{4,5},{5,4},{6,7},{7,6},{8,9},{9,8},{10,11... | collective-permute-start | bytes 626696 | tf_op jit(solution)/shard_map/ppermute | solution.py:261
  54.1 4.0 %collective-permute-start.14 = (f32[4,384]{1,0:T(4,128)S(1)}, f32[4,384]{1,0:T(4,128)S(1)}, u32[]{:S(2)}, u32[]{:S(2)}) collective-permute-start(f32[4,384]{1,0:T(4,128)S(1)} %get-tuple-element.80), channel_id=1, source_target_pairs={{0,1},{1,0},{2,3},{3,2},{4,5},{5,4},{6,7},{7,6},{8,9},{9,8},{10,11... | collective-permute-start | bytes 18440 | tf_op jit(solution)/shard_map/ppermute | solution.py:261
  54.2 7.5 %collective-permute-start.11 = (f32[1,384]{1,0:T(1,128)S(1)}, f32[1,384]{1,0:T(1,128)S(1)}, u32[]{:S(2)}, u32[]{:S(2)}) collective-permute-start(f32[1,384]{1,0:T(1,128)S(1)} %get-tuple-element.73), channel_id=1, source_target_pairs={{0,24},{1,25},{2,26},{3,27},{4,28},{5,29},{6,30},{7,31},{8,0},{9,1... | collective-permute-start | bytes 4616 | tf_op jit(solution)/shard_map/ppermute | solution.py:261
  58.1 3.6 %collective-permute-start.13 = (f32[1,384]{1,0:T(1,128)S(1)}, f32[1,384]{1,0:T(1,128)S(1)}, u32[]{:S(2)}, u32[]{:S(2)}) collective-permute-start(f32[1,384]{1,0:T(1,128)S(1)} %get-tuple-element.78), channel_id=1, source_target_pairs={{0,16},{1,17},{2,18},{3,19},{4,20},{5,21},{6,22},{7,23},{8,0},{9,1... | collective-permute-start | bytes 4616 | tf_op jit(solution)/shard_map/ppermute | solution.py:261
  58.1 3.6 %collective-permute-start.15 = (f32[1,384]{1,0:T(1,128)S(1)}, f32[1,384]{1,0:T(1,128)S(1)}, u32[]{:S(2)}, u32[]{:S(2)}) collective-permute-start(f32[1,384]{1,0:T(1,128)S(1)} %get-tuple-element.82), channel_id=1, source_target_pairs={{2,0},{3,1},{0,2},{1,3},{6,4},{7,5},{4,6},{5,7},{10,8},{11,9},{8,1... | collective-permute-start | bytes 4616 | tf_op jit(solution)/shard_map/ppermute | solution.py:261
  59.7 3.6 %collective-permute-start.16 = (f32[1,384]{1,0:T(1,128)S(1)}, f32[1,384]{1,0:T(1,128)S(1)}, u32[]{:S(2)}, u32[]{:S(2)}) collective-permute-start(f32[1,384]{1,0:T(1,128)S(1)} %get-tuple-element.83), channel_id=1, source_target_pairs={{4,0},{5,1},{6,2},{7,3},{0,4},{1,5},{2,6},{3,7},{12,8},{13,9},{14,... | collective-permute-start | bytes 4616 | tf_op jit(solution)/shard_map/ppermute | solution.py:261
  61.2 4.5 %collective-permute-start.17 = (f32[1,384]{1,0:T(1,128)S(1)}, f32[1,384]{1,0:T(1,128)S(1)}, u32[]{:S(2)}, u32[]{:S(2)}) collective-permute-start(f32[1,384]{1,0:T(1,128)S(1)} %get-tuple-element.84), channel_id=1, source_target_pairs={{6,0},{7,1},{4,2},{5,3},{2,4},{3,5},{0,6},{1,7},{14,8},{15,9},{12,... | collective-permute-start | bytes 4616 | tf_op jit(solution)/shard_map/ppermute | solution.py:261

commit v9 on v8

--- a/solution.py
+++ b/solution.py
@@ -97,7 +97,7 @@
 
 def pack(embeddings, doc_order, pieces):
     n, width = embeddings.shape
-    chunk = 128 if n % 128 == 0 else n
+    chunk = n
     call = pl.pallas_call(
         functools.partial(pack_body, pieces, chunk),
         in_specs=[pl.BlockSpec(memory_space=pltpu.HBM)] * 2,
@@ -236,6 +236,20 @@
     )(*in_vmem([*blocks, *(state or ())]))
 
 
+def final_body(*refs):
+    best = functools.reduce(jnp.maximum, [ref[...] for ref in refs[:-1]])
+    refs[-1][...] = jnp.maximum(best, -1.0).reshape(refs[-1].shape)
+
+
+def final(parts):
+    return pl.pallas_call(
+        final_body,
+        out_shape=jax.ShapeDtypeStruct((parts[0].shape[1],), jnp.float32),
+        compiler_params=pltpu.CompilerParams(vmem_limit_bytes=VMEM_GRANT),
+        name="final",
+    )(*in_vmem(parts))
+
+
 def merge_body(ours_ref, theirs_ref, *out_refs):
     value = jnp.maximum(ours_ref[...], theirs_ref[...])
     for k, ref in enumerate(out_refs):
@@ -327,8 +341,7 @@
         back.append(own_best)
         for value, d in zip(others, offsets):
             back.append(send(value, backward(layout.plane_move(*d))))
-        best = functools.reduce(jnp.maximum, back)
-        return jnp.maximum(best, -1.0).reshape(doc_order.shape)
+        return final(back)
 
     return jax.shard_map(
         nearest,

time: 66.5 us -> 66.3 us (level)
  no operation moved by 1% of the time
where the time goes in v9:
time: 66.3 us; the launch traced here: 66.2 us
  waiting for transfers between devices  36.3 us (55%)
  starting transfers between devices  18.9 us (29%)
  Pallas kernels  10.8 us (16%)
    ppermute x18, waiting for transfers between devices, send(): return lax.ppermute(value, AXES, pairs)  36.3 us
    ppermute x18, starting transfers between devices, send(): return lax.ppermute(value, AXES, pairs)  18.9 us
    pallas_call x7, Pallas kernels, match(): pl.pallas_call(functools.partial(match_body, plan, groups, len(blocks), s...  8.93 us
  transfers between devices with their start and end apart: 18, of which 7 were waited for; matrix products, arithmetic and copies ran while one was open for 0% of the time, Pallas kernels for 11%

profile of v9, /device:TPU:0, one launch (start us, length us, event | category | flops | bytes accessed | tf_op | source)
XLA Modules:
  0.0 66.2 jit_solution(12685090580545411214)
XLA Ops:
  0.0 1.3 %pack.1 = (bf16[392,768]{1,0:T(8,128)(2,1)S(1)}, bf16[136,768]{1,0:T(8,128)(2,1)S(1)}, bf16[264,768]{1,0:T(8,128)(2,1)S(1)}) custom-call(bf16[384,768]{1,0:T(8,128)(2,1)} %emb_hbm.1, s32[384]{0:T(512)} %order_hbm.1), custom_call_target="tpu_custom_call" | custom-call | tf_op jit(solution)/shard_map/pack/pallas_call | solution.py:113
  1.3 3.1 %collective-permute-start.3 = (bf16[392,768]{1,0:T(8,128)(2,1)S(1)}, bf16[392,768]{1,0:T(8,128)(2,1)S(1)}, u32[]{:S(2)}, u32[]{:S(2)}) collective-permute-start(bf16[392,768]{1,0:T(8,128)(2,1)S(1)} %get-tuple-element.45.refs_0_.refs_2_.refs_1_), channel_id=1, source_target_pairs={{0,4},{1,5},{2,6},{3,7},{4,0},{5,1},{6,2},{7,3},{8,12},{9,13},{10,... | collective-permute-start | bytes 1806344 | tf_op jit(solution)/shard_map/ppermute | solution.py:275
  4.4 1.5 %collective-permute-start = (bf16[392,768]{1,0:T(8,128)(2,1)S(1)}, bf16[392,768]{1,0:T(8,128)(2,1)S(1)}, u32[]{:S(2)}, u32[]{:S(2)}) collective-permute-start(bf16[392,768]{1,0:T(8,128)(2,1)S(1)} %get-tuple-element.45.refs_0_.refs_2_.refs_1_), channel_id=1, source_target_pairs={{0,2},{1,3},{2,0},{3,1},{4,6},{5,7},{6,4},{7,5},{8,10},{9,11},{10,... | collective-permute-start | bytes 1806344 | tf_op jit(solution)/shard_map/ppermute | solution.py:275
  5.9 0.0 collective-permute-start.8
  5.9 1.6 %collective-permute-start.6 = (bf16[392,768]{1,0:T(8,128)(2,1)S(1)}, bf16[392,768]{1,0:T(8,128)(2,1)S(1)}, u32[]{:S(2)}, u32[]{:S(2)}) collective-permute-start(bf16[392,768]{1,0:T(8,128)(2,1)S(1)} %get-tuple-element.45.refs_0_.refs_2_.refs_1_), channel_id=1, source_target_pairs={{0,8},{1,9},{2,10},{3,11},{4,12},{5,13},{6,14},{7,15},{8,16},{9,17... | collective-permute-start | bytes 1806344 | tf_op jit(solution)/shard_map/ppermute | solution.py:275
  7.4 10.5 %collective-permute-done.3.ref.refs_4_ = bf16[392,768]{1,0:T(8,128)(2,1)S(1)} collective-permute-done((bf16[392,768]{1,0:T(8,128)(2,1)S(1)}, bf16[392,768]{1,0:T(8,128)(2,1)S(1)}, u32[]{:S(2)}, u32[]{:S(2)}) %collective-permute-start.3) | collective-permute-done | bytes 602144 | tf_op jit(solution)/shard_map/ppermute | solution.py:275
  18.0 1.5 %collective-permute-done.ref.refs_3_ = bf16[392,768]{1,0:T(8,128)(2,1)S(1)} collective-permute-done((bf16[392,768]{1,0:T(8,128)(2,1)S(1)}, bf16[392,768]{1,0:T(8,128)(2,1)S(1)}, u32[]{:S(2)}, u32[]{:S(2)}) %collective-permute-start) | collective-permute-done | bytes 602144 | tf_op jit(solution)/shard_map/ppermute | solution.py:275
  19.5 0.4 collective-permute-start.1
  19.9 0.2 collective-permute-start.9
  20.1 1.6 %collective-permute-start.4 = (bf16[136,768]{1,0:T(8,128)(2,1)S(1)}, bf16[136,768]{1,0:T(8,128)(2,1)S(1)}, u32[]{:S(2)}, u32[]{:S(2)}) collective-permute-start(bf16[136,768]{1,0:T(8,128)(2,1)S(1)} %piece.3), channel_id=1, source_target_pairs={{0,2},{1,3},{2,0},{3,1},{4,6},{5,7},{6,4},{7,5},{8,10},{9,11},{10,... | collective-permute-start | bytes 626696 | tf_op jit(solution)/shard_map/ppermute | solution.py:275
  21.6 8.2 %collective-permute-done.1.refs_0_.refs_7_ = bf16[264,768]{1,0:T(8,128)(2,1)S(1)} collective-permute-done((bf16[264,768]{1,0:T(8,128)(2,1)S(1)}, bf16[264,768]{1,0:T(8,128)(2,1)S(1)}, u32[]{:S(2)}, u32[]{:S(2)}) %collective-permute-start.1) | collective-permute-done | bytes 405536 | tf_op jit(solution)/shard_map/ppermute | solution.py:275
  29.9 1.3 %collective-permute-start.12 = (bf16[264,768]{1,0:T(8,128)(2,1)S(1)}, bf16[264,768]{1,0:T(8,128)(2,1)S(1)}, u32[]{:S(2)}, u32[]{:S(2)}) collective-permute-start(bf16[264,768]{1,0:T(8,128)(2,1)S(1)} %get-tuple-element.74), channel_id=1, source_target_pairs={{8,24},{9,25},{10,26},{11,27},{12,28},{13,29},{14,30},{15,31},{16,... | collective-permute-start | bytes 1216520 | tf_op jit(solution)/shard_map/ppermute | solution.py:275
  31.2 0.8 %shard_map.28 = (f32[1,384]{1,0:T(1,128)S(1)}, f32[1,384]{1,0:T(1,128)S(1)}, f32[1,384]{1,0:T(1,128)S(1)}, f32[4,384]{1,0:T(4,128)S(1)}, f32[4,384]{1,0:T(4,128)S(1)}) custom-call(bf16[392,768]{1,0:T(8,128)(2,1)S(1)} %get-tuple-element.45.refs_0_.refs_2_.refs_1_, bf16[392,768]{1,0:T(8,128)(2,1)S(1)} %collective-permute-done.8.refs_1_.refs_2_), custom_call_target="tpu_custom_call" | custom-call | flops 472055808 | bytes 1179648 | tf_op jit(solution)/shard_map/pallas_call | solution.py:230
  32.0 1.3 %collective-permute-start.7 = (bf16[136,768]{1,0:T(8,128)(2,1)S(1)}, bf16[136,768]{1,0:T(8,128)(2,1)S(1)}, u32[]{:S(2)}, u32[]{:S(2)}) collective-permute-start(bf16[136,768]{1,0:T(8,128)(2,1)S(1)} %get-tuple-element.46), channel_id=1, source_target_pairs={{8,24},{9,25},{10,26},{11,27},{12,28},{13,29},{14,30},{15,31},{16,... | collective-permute-start | bytes 626696 | tf_op jit(solution)/shard_map/ppermute | solution.py:275
  33.3 0.6 collective-permute-start.5
  33.9 1.8 %shard_map.29 = (f32[1,384]{1,0:T(1,128)S(1)}, f32[1,384]{1,0:T(1,128)S(1)}, f32[1,384]{1,0:T(1,128)S(1)}, f32[4,384]{1,0:T(4,128)S(1)}, f32[4,384]{1,0:T(4,128)S(1)}) custom-call(bf16[392,768]{1,0:T(8,128)(2,1)S(1)} %get-tuple-element.45.refs_0_.refs_2_.refs_1_, bf16[392,768]{1,0:T(8,128)(2,1)S(1)} %collective-permute-done.8.refs_1_.refs_2_, ...), custom_call_target="tpu_custom_call" | custom-call | flops 1416167424 | bytes 2949120 | tf_op jit(solution)/shard_map/pallas_call | solution.py:230
  35.6 1.2 %shard_map.30 = (f32[1,384]{1,0:T(1,128)S(1)}, f32[1,384]{1,0:T(1,128)S(1)}, f32[1,384]{1,0:T(1,128)S(1)}, f32[4,384]{1,0:T(4,128)S(1)}, f32[4,384]{1,0:T(4,128)S(1)}) custom-call(bf16[392,768]{1,0:T(8,128)(2,1)S(1)} %collective-permute-done.9.refs_0_.refs_5_, bf16[392,768]{1,0:T(8,128)(2,1)S(1)} %collective-permute-done.10.refs_1_.refs_6_, ...), custom_call_target="tpu_custom_call" | custom-call | flops 944111616 | bytes 2359296 | tf_op jit(solution)/shard_map/pallas_call | solution.py:230
  36.9 12.0 %collective-permute-done.7.refs_0_.refs_4_ = bf16[136,768]{1,0:T(8,128)(2,1)S(1)} collective-permute-done((bf16[136,768]{1,0:T(8,128)(2,1)S(1)}, bf16[136,768]{1,0:T(8,128)(2,1)S(1)}, u32[]{:S(2)}, u32[]{:S(2)}) %collective-permute-start.7) | collective-permute-done | bytes 208928 | tf_op jit(solution)/shard_map/ppermute | solution.py:275
  48.9 1.4 %shard_map.31 = (f32[1,384]{1,0:T(1,128)S(1)}, f32[1,384]{1,0:T(1,128)S(1)}, f32[1,384]{1,0:T(1,128)S(1)}, f32[4,384]{1,0:T(4,128)S(1)}, f32[4,384]{1,0:T(4,128)S(1)}) custom-call(bf16[136,768]{1,0:T(8,128)(2,1)S(1)} %collective-permute-done.7.refs_0_.refs_4_, bf16[392,768]{1,0:T(8,128)(2,1)S(1)} %get-tuple-element.45.refs_0_.refs_2_.refs_1_, ...), custom_call_target="tpu_custom_call" | custom-call | flops 491323392 | bytes 4128768 | tf_op jit(solution)/shard_map/pallas_call | solution.py:230
  50.3 1.0 %shard_map.32 = (f32[1,384]{1,0:T(1,128)S(1)}, f32[1,384]{1,0:T(1,128)S(1)}, f32[1,384]{1,0:T(1,128)S(1)}, f32[4,384]{1,0:T(4,128)S(1)}, f32[4,384]{1,0:T(4,128)S(1)}) custom-call(bf16[264,768]{1,0:T(8,128)(2,1)S(1)} %collective-permute-done.1.refs_0_.refs_7_, bf16[136,768]{1,0:T(8,128)(2,1)S(1)} %collective-permute-done.4.refs_1_.refs_8_, ...), custom_call_target="tpu_custom_call" | custom-call | flops 565248000 | bytes 2949120 | tf_op jit(solution)/shard_map/pallas_call | solution.py:230
  51.3 1.0 %shard_map.33 = (f32[1,384]{1,0:T(1,128)S(1)}, f32[1,384]{1,0:T(1,128)S(1)}, f32[1,384]{1,0:T(1,128)S(1)}, f32[4,384]{1,0:T(4,128)S(1)}, f32[4,384]{1,0:T(4,128)S(1)}) custom-call(bf16[264,768]{1,0:T(8,128)(2,1)S(1)} %collective-permute-done.2.refs_0_.refs_9_, bf16[136,768]{1,0:T(8,128)(2,1)S(1)} %collective-permute-done.5.refs_1_.refs_10_, ...), custom_call_target="tpu_custom_call" | custom-call | flops 565248000 | bytes 2949120 | tf_op jit(solution)/shard_map/pallas_call | solution.py:230
  52.3 1.8 %shard_map.34 = (f32[1,384]{1,0:T(1,128)S(1)}, f32[4,384]{1,0:T(4,128)S(1)}, f32[4,384]{1,0:T(4,128)S(1)}) custom-call(bf16[264,768]{1,0:T(8,128)(2,1)S(1)} %collective-permute-done.12.refs_0_, bf16[392,768]{1,0:T(8,128)(2,1)S(1)} %get-tuple-element.45.refs_0_.refs_2_.refs_1_, bf16[392,768]{1,0:T(8,128)(2,1)S(1)} %collective-permute-done.8.refs_1_.refs_2_, ...), custom_call_target="tpu_custom_call" | custom-call | flops 1278148608 | bytes 6488064 | tf_op jit(solution)/shard_map/pallas_call | solution.py:230
  54.1 0.1 collective-permute-start.14
  54.1 3.9 %collective-permute-start.11 = (f32[1,384]{1,0:T(1,128)S(1)}, f32[1,384]{1,0:T(1,128)S(1)}, u32[]{:S(2)}, u32[]{:S(2)}) collective-permute-start(f32[1,384]{1,0:T(1,128)S(1)} %get-tuple-element.73), channel_id=1, source_target_pairs={{0,24},{1,25},{2,26},{3,27},{4,28},{5,29},{6,30},{7,31},{8,0},{9,1... | collective-permute-start | bytes 4616 | tf_op jit(solution)/shard_map/ppermute | solution.py:275
  58.0 1.6 %collective-permute-start.15 = (f32[1,384]{1,0:T(1,128)S(1)}, f32[1,384]{1,0:T(1,128)S(1)}, u32[]{:S(2)}, u32[]{:S(2)}) collective-permute-start(f32[1,384]{1,0:T(1,128)S(1)} %get-tuple-element.82), channel_id=1, source_target_pairs={{2,0},{3,1},{0,2},{1,3},{6,4},{7,5},{4,6},{5,7},{10,8},{11,9},{8,1... | collective-permute-start | bytes 4616 | tf_op jit(solution)/shard_map/ppermute | solution.py:275
  59.6 1.5 %collective-permute-start.16 = (f32[1,384]{1,0:T(1,128)S(1)}, f32[1,384]{1,0:T(1,128)S(1)}, u32[]{:S(2)}, u32[]{:S(2)}) collective-permute-start(f32[1,384]{1,0:T(1,128)S(1)} %get-tuple-element.83), channel_id=1, source_target_pairs={{4,0},{5,1},{6,2},{7,3},{0,4},{1,5},{2,6},{3,7},{12,8},{13,9},{14,... | collective-permute-start | bytes 4616 | tf_op jit(solution)/shard_map/ppermute | solution.py:275
  61.1 0.5 collective-permute-start.17
  61.6 0.0 collective-permute-done.13.refs_2_
  61.6 0.1 collective-permute-done.15.refs_4_
  61.7 1.5 %collective-permute-done.16.refs_5_ = f32[1,384]{1,0:T(1,128)S(1)} collective-permute-done((f32[1,384]{1,0:T(1,128)S(1)}, f32[1,384]{1,0:T(1,128)S(1)}, u32[]{:S(2)}, u32[]{:S(2)}) %collective-permute-start.16) | collective-permute-done | bytes 1568 | tf_op jit(solution)/shard_map/ppermute | solution.py:275
  63.2 2.4 %collective-permute-done.17.refs_6_ = f32[1,384]{1,0:T(1,128)S(1)} collective-permute-done((f32[1,384]{1,0:T(1,128)S(1)}, f32[1,384]{1,0:T(1,128)S(1)}, u32[]{:S(2)}, u32[]{:S(2)}) %collective-permute-start.17) | collective-permute-done | bytes 1568 | tf_op jit(solution)/shard_map/ppermute | solution.py:275
  65.6 0.6 final.1
  (16 shorter events, 0.1 us)
Async XLA Ops:
  1.3 16.7 %collective-permute-start.3 = (bf16[392,768]{1,0:T(8,128)(2,1)S(1)}, bf16[392,768]{1,0:T(8,128)(2,1)S(1)}, u32[]{:S(2)}, u32[]{:S(2)}) collective-permute-start(bf16[392,768]{1,0:T(8,128)(2,1)S(1)} %get-tuple-element.45.refs_0_.refs_2_.refs_1_), channel_id=1, source_target_pairs={{0,4},{1,5},{2,6},{3,7},{4,0},{5,1},{6,2},{7,3},{8,12},{9,13},{10,... | collective-permute-start | bytes 1806344 | tf_op jit(solution)/shard_map/ppermute | solution.py:275
  4.4 15.1 %collective-permute-start = (bf16[392,768]{1,0:T(8,128)(2,1)S(1)}, bf16[392,768]{1,0:T(8,128)(2,1)S(1)}, u32[]{:S(2)}, u32[]{:S(2)}) collective-permute-start(bf16[392,768]{1,0:T(8,128)(2,1)S(1)} %get-tuple-element.45.refs_0_.refs_2_.refs_1_), channel_id=1, source_target_pairs={{0,2},{1,3},{2,0},{3,1},{4,6},{5,7},{6,4},{7,5},{8,10},{9,11},{10,... | collective-permute-start | bytes 1806344 | tf_op jit(solution)/shard_map/ppermute | solution.py:275
  5.9 14.2 %collective-permute-start.8 = (bf16[392,768]{1,0:T(8,128)(2,1)S(1)}, bf16[392,768]{1,0:T(8,128)(2,1)S(1)}, u32[]{:S(2)}, u32[]{:S(2)}) collective-permute-start(bf16[392,768]{1,0:T(8,128)(2,1)S(1)} %get-tuple-element.45.refs_0_.refs_2_.refs_1_), channel_id=1, source_target_pairs={{0,1},{1,0},{2,3},{3,2},{4,5},{5,4},{6,7},{7,6},{8,9},{9,8},{10,11... | collective-permute-start | bytes 1806344 | tf_op jit(solution)/shard_map/ppermute | solution.py:275
  5.9 24.0 %collective-permute-start.6 = (bf16[392,768]{1,0:T(8,128)(2,1)S(1)}, bf16[392,768]{1,0:T(8,128)(2,1)S(1)}, u32[]{:S(2)}, u32[]{:S(2)}) collective-permute-start(bf16[392,768]{1,0:T(8,128)(2,1)S(1)} %get-tuple-element.45.refs_0_.refs_2_.refs_1_), channel_id=1, source_target_pairs={{0,8},{1,9},{2,10},{3,11},{4,12},{5,13},{6,14},{7,15},{8,16},{9,17... | collective-permute-start | bytes 1806344 | tf_op jit(solution)/shard_map/ppermute | solution.py:275
  18.0 15.3 %collective-permute-start.10 = (bf16[392,768]{1,0:T(8,128)(2,1)S(1)}, bf16[392,768]{1,0:T(8,128)(2,1)S(1)}, u32[]{:S(2)}, u32[]{:S(2)}) collective-permute-start(bf16[392,768]{1,0:T(8,128)(2,1)S(1)} %collective-permute-done.3.ref.refs_4_), channel_id=1, source_target_pairs={{0,1},{1,0},{2,3},{3,2},{4,5},{5,4},{6,7},{7,6},{8,9},{9,8},{10,11... | collective-permute-start | bytes 1806344 | tf_op jit(solution)/shard_map/ppermute | solution.py:275
  19.5 10.4 %collective-permute-start.1 = (bf16[264,768]{1,0:T(8,128)(2,1)S(1)}, bf16[264,768]{1,0:T(8,128)(2,1)S(1)}, u32[]{:S(2)}, u32[]{:S(2)}) collective-permute-start(bf16[264,768]{1,0:T(8,128)(2,1)S(1)} %piece.2), channel_id=1, source_target_pairs={{0,4},{1,5},{2,6},{3,7},{4,0},{5,1},{6,2},{7,3},{8,12},{9,13},{10,... | collective-permute-start | bytes 1216520 | tf_op jit(solution)/shard_map/ppermute | solution.py:275
  19.9 15.8 %collective-permute-start.9 = (bf16[392,768]{1,0:T(8,128)(2,1)S(1)}, bf16[392,768]{1,0:T(8,128)(2,1)S(1)}, u32[]{:S(2)}, u32[]{:S(2)}) collective-permute-start(bf16[392,768]{1,0:T(8,128)(2,1)S(1)} %collective-permute-done.ref.refs_3_), channel_id=1, source_target_pairs={{0,1},{1,0},{2,3},{3,2},{4,5},{5,4},{6,7},{7,6},{8,9},{9,8},{10,11... | collective-permute-start | bytes 1806344 | tf_op jit(solution)/shard_map/ppermute | solution.py:275
  20.1 11.9 %collective-permute-start.4 = (bf16[136,768]{1,0:T(8,128)(2,1)S(1)}, bf16[136,768]{1,0:T(8,128)(2,1)S(1)}, u32[]{:S(2)}, u32[]{:S(2)}) collective-permute-start(bf16[136,768]{1,0:T(8,128)(2,1)S(1)} %piece.3), channel_id=1, source_target_pairs={{0,2},{1,3},{2,0},{3,1},{4,6},{5,7},{6,4},{7,5},{8,10},{9,11},{10,... | collective-permute-start | bytes 626696 | tf_op jit(solution)/shard_map/ppermute | solution.py:275
  29.9 21.4 %collective-permute-start.2 = (bf16[264,768]{1,0:T(8,128)(2,1)S(1)}, bf16[264,768]{1,0:T(8,128)(2,1)S(1)}, u32[]{:S(2)}, u32[]{:S(2)}) collective-permute-start(bf16[264,768]{1,0:T(8,128)(2,1)S(1)} %collective-permute-done.1.refs_0_.refs_7_), channel_id=1, source_target_pairs={{0,1},{1,0},{2,3},{3,2},{4,5},{5,4},{6,7},{7,6},{8,9},{9,8},{10,11... | collective-permute-start | bytes 1216520 | tf_op jit(solution)/shard_map/ppermute | solution.py:275
  29.9 22.4 %collective-permute-start.12 = (bf16[264,768]{1,0:T(8,128)(2,1)S(1)}, bf16[264,768]{1,0:T(8,128)(2,1)S(1)}, u32[]{:S(2)}, u32[]{:S(2)}) collective-permute-start(bf16[264,768]{1,0:T(8,128)(2,1)S(1)} %get-tuple-element.74), channel_id=1, source_target_pairs={{8,24},{9,25},{10,26},{11,27},{12,28},{13,29},{14,30},{15,31},{16,... | collective-permute-start | bytes 1216520 | tf_op jit(solution)/shard_map/ppermute | solution.py:275
  32.0 16.9 %collective-permute-start.7 = (bf16[136,768]{1,0:T(8,128)(2,1)S(1)}, bf16[136,768]{1,0:T(8,128)(2,1)S(1)}, u32[]{:S(2)}, u32[]{:S(2)}) collective-permute-start(bf16[136,768]{1,0:T(8,128)(2,1)S(1)} %get-tuple-element.46), channel_id=1, source_target_pairs={{8,24},{9,25},{10,26},{11,27},{12,28},{13,29},{14,30},{15,31},{16,... | collective-permute-start | bytes 626696 | tf_op jit(solution)/shard_map/ppermute | solution.py:275
  33.3 18.0 %collective-permute-start.5 = (bf16[136,768]{1,0:T(8,128)(2,1)S(1)}, bf16[136,768]{1,0:T(8,128)(2,1)S(1)}, u32[]{:S(2)}, u32[]{:S(2)}) collective-permute-start(bf16[136,768]{1,0:T(8,128)(2,1)S(1)} %collective-permute-done.4.refs_1_.refs_8_), channel_id=1, source_target_pairs={{0,1},{1,0},{2,3},{3,2},{4,5},{5,4},{6,7},{7,6},{8,9},{9,8},{10,11... | collective-permute-start | bytes 626696 | tf_op jit(solution)/shard_map/ppermute | solution.py:275
  54.1 4.0 %collective-permute-start.14 = (f32[4,384]{1,0:T(4,128)S(1)}, f32[4,384]{1,0:T(4,128)S(1)}, u32[]{:S(2)}, u32[]{:S(2)}) collective-permute-start(f32[4,384]{1,0:T(4,128)S(1)} %get-tuple-element.80), channel_id=1, source_target_pairs={{0,1},{1,0},{2,3},{3,2},{4,5},{5,4},{6,7},{7,6},{8,9},{9,8},{10,11... | collective-permute-start | bytes 18440 | tf_op jit(solution)/shard_map/ppermute | solution.py:275
  54.1 7.4 %collective-permute-start.11 = (f32[1,384]{1,0:T(1,128)S(1)}, f32[1,384]{1,0:T(1,128)S(1)}, u32[]{:S(2)}, u32[]{:S(2)}) collective-permute-start(f32[1,384]{1,0:T(1,128)S(1)} %get-tuple-element.73), channel_id=1, source_target_pairs={{0,24},{1,25},{2,26},{3,27},{4,28},{5,29},{6,30},{7,31},{8,0},{9,1... | collective-permute-start | bytes 4616 | tf_op jit(solution)/shard_map/ppermute | solution.py:275
  58.0 3.6 %collective-permute-start.13 = (f32[1,384]{1,0:T(1,128)S(1)}, f32[1,384]{1,0:T(1,128)S(1)}, u32[]{:S(2)}, u32[]{:S(2)}) collective-permute-start(f32[1,384]{1,0:T(1,128)S(1)} %get-tuple-element.78), channel_id=1, source_target_pairs={{0,16},{1,17},{2,18},{3,19},{4,20},{5,21},{6,22},{7,23},{8,0},{9,1... | collective-permute-start | bytes 4616 | tf_op jit(solution)/shard_map/ppermute | solution.py:275
  58.0 3.6 %collective-permute-start.15 = (f32[1,384]{1,0:T(1,128)S(1)}, f32[1,384]{1,0:T(1,128)S(1)}, u32[]{:S(2)}, u32[]{:S(2)}) collective-permute-start(f32[1,384]{1,0:T(1,128)S(1)} %get-tuple-element.82), channel_id=1, source_target_pairs={{2,0},{3,1},{0,2},{1,3},{6,4},{7,5},{4,6},{5,7},{10,8},{11,9},{8,1... | collective-permute-start | bytes 4616 | tf_op jit(solution)/shard_map/ppermute | solution.py:275
  59.6 3.6 %collective-permute-start.16 = (f32[1,384]{1,0:T(1,128)S(1)}, f32[1,384]{1,0:T(1,128)S(1)}, u32[]{:S(2)}, u32[]{:S(2)}) collective-permute-start(f32[1,384]{1,0:T(1,128)S(1)} %get-tuple-element.83), channel_id=1, source_target_pairs={{4,0},{5,1},{6,2},{7,3},{0,4},{1,5},{2,6},{3,7},{12,8},{13,9},{14,... | collective-permute-start | bytes 4616 | tf_op jit(solution)/shard_map/ppermute | solution.py:275
  61.1 4.5 %collective-permute-start.17 = (f32[1,384]{1,0:T(1,128)S(1)}, f32[1,384]{1,0:T(1,128)S(1)}, u32[]{:S(2)}, u32[]{:S(2)}) collective-permute-start(f32[1,384]{1,0:T(1,128)S(1)} %get-tuple-element.84), channel_id=1, source_target_pairs={{6,0},{7,1},{4,2},{5,3},{2,4},{3,5},{0,6},{1,7},{14,8},{15,9},{12,... | collective-permute-start | bytes 4616 | tf_op jit(solution)/shard_map/ppermute | solution.py:275
